TPU v7x, 128 devices: a whole 4x4x4 slice. The times are simulated.
128 devices in a mesh: row: 8 (over z, y_lo), col: 16 (over x, y_hi, core).
Axes of the slice: x: 4, y: 4 (y_hi: 2, y_lo: 2; y = y_hi * 2 + y_lo), z: 4, core: 2. Of those that a mesh axis runs over, the one named last changes fastest.
Arguments:
- slab_pair: float32 [65536, 4096], P('row', 'col'), may hold values from -6 to 6, as said below
- butterfly_scale: float32 [65536], P('row'), may hold values from 0.5 to 2
Outputs:
- transformed: float32 [65536, 4096], P('row', 'col')
Inputs may be any that keep to these rules, and one draw needn't show every extreme that they name: The matrix is symmetric where the slab pair meets its own columns: with g(k) = k for k < 2048 and 32768 + k - 2048 otherwise, slab_pair[g(a), b] = slab_pair[g(b), a] for all a, b below 4096.
All inputs are finite; a program needn't handle non-finite values.
Results may differ from a plain program's by a relative error of at most 0.00002.
Values sent between devices are 32-bit elements; how exact they have to be, the bound alone decides.
No kernel may reach another device: no remote copies, remote signals or barrier semaphores. Data moves between devices by JAX's collectives and lax.ppermute only.
A program may use at most 64 MiB of HBM per device.

v0:
```python
import jax
import jax.numpy as jnp
from jax import lax
from jax.sharding import PartitionSpec as P

N = 65536
W = 2048


def from_partner(block, axis, distance):
    count = lax.axis_size(axis)
    route = []
    for low in range(count):
        high = low | 1 << distance
        if high != low and high < count:
            route += [(low, high), (high, low)]
    return lax.ppermute(block, axis, route)


def row_pass(block_data, scale_here, is_top):
    row_bit = lax.axis_size("row").bit_length() - 2
    partner = from_partner(block_data, "row", row_bit)
    mixed = jnp.where(is_top, block_data + partner, partner - block_data)
    return mixed * scale_here[:, None] / jnp.float32(2.0) ** 0.5


def col_pass(block_data, col_scale, is_left):
    col_bit = lax.axis_size("col").bit_length() - 2
    partner = from_partner(block_data, "col", col_bit)
    mixed = jnp.where(is_left, block_data + partner, partner - block_data)
    return mixed * col_scale[None, :] / jnp.float32(2.0) ** 0.5


def per_device(slab_pair, butterfly_scale):
    row_count = lax.axis_size("row")
    col_count = lax.axis_size("col")
    row_here = lax.axis_index("row")
    col_here = lax.axis_index("col")
    local_rows = slab_pair.shape[0]
    local_cols = slab_pair.shape[1]
    is_top = row_here < row_count // 2
    is_left = col_here < col_count // 2
    gathered = lax.all_gather(butterfly_scale[:W], "row", axis=0, tiled=True)
    middle = row_count // 2 * W
    full_scale = jnp.concatenate([gathered[:W], gathered[middle : middle + W]])
    col_scale = lax.dynamic_slice_in_dim(full_scale, col_here * local_cols, local_cols, 0)
    mixed = col_pass(row_pass(slab_pair, butterfly_scale, is_top), col_scale, is_left)
    row_index = row_here * local_rows + jnp.arange(local_rows, dtype=jnp.int32)[:, None]
    col_index = col_here * local_cols + jnp.arange(local_cols, dtype=jnp.int32)[None, :]
    global_col = jnp.where(col_index < W, col_index, N // 2 + col_index - W)
    return jnp.where(row_index >= global_col, mixed, jnp.float32(0.0))


def solution(mesh):
    in_specs = (P("row", "col"), P("row"))
    out_specs = P("row", "col")
    return jax.shard_map(
        per_device, mesh=mesh, in_specs=in_specs, out_specs=out_specs, check_vma=False
    )
```

profile of v0, /device:TPU:0, one launch (start us, length us, event | category | flops | bytes accessed | tf_op | source)
XLA Modules:
  0.0 387.8 jit_solution(3690508631358408823)
XLA Ops:
  0.0 4.0 %collective-permute-start = (f32[8192,256]{1,0:T(8,128)}, f32[8192,256]{1,0:T(8,128)}, u32[]{:S(2)}, u32[]{:S(2)}) collective-permute-start(f32[8192,256]{1,0:T(8,128)} %param.2), channel_id=1, source_target_pairs={{0,64},{64,0},{16,80},{80,16},{32,96},{96,32},{48,112},{112,48},{1... | collective-permute-start | bytes 25165832 | tf_op jit(solution)/shard_map/ppermute | solution.py:17
  4.0 0.0 slice-start
  4.0 180.8 %collective-permute-done = f32[8192,256]{1,0:T(8,128)} collective-permute-done((f32[8192,256]{1,0:T(8,128)}, f32[8192,256]{1,0:T(8,128)}, u32[]{:S(2)}, u32[]{:S(2)}) %collective-permute-start) | collective-permute-done | bytes 8388640 | tf_op jit(solution)/shard_map/ppermute | solution.py:17
  184.8 10.1 %multiply_multiply_fusion = f32[8192,256]{1,0:T(8,128)} fusion(f32[8192,256]{1,0:T(8,128)} %collective-permute-done, f32[8192,256]{1,0:T(8,128)} %param.2, f32[8192]{0:T(1024)} %param.3, pred[]{:T(512)S(6)} %lt.19), kind=kLoop, calls=%fused_computation.1 | loop fusion | flops 10485760 | bytes 25198592 | tf_op jit(solution)/shard_map/div | solution.py:24
  194.9 3.0 collective-permute-start.1
  197.9 0.0 slice-done
  197.9 29.0 %all_gather.3 = f32[16384]{0:T(1024)S(1)} all-gather(f32[2048]{0:T(1024)S(1)} %slice-done), channel_id=1, replica_groups=mesh['row'=8,'col'=16] {'row'}, dimensions={0}, use_global_device_ids=true | all-gather | bytes 73728 | tf_op jit(solution)/shard_map/all_gather | solution.py:43
  226.9 0.1 fusion
  227.0 151.3 %collective-permute-done.1 = f32[8192,256]{1,0:T(8,128)} collective-permute-done((f32[8192,256]{1,0:T(8,128)}, f32[8192,256]{1,0:T(8,128)}, u32[]{:S(2)}, u32[]{:S(2)}) %collective-permute-start.1) | collective-permute-done | bytes 8388640 | tf_op jit(solution)/shard_map/ppermute | solution.py:17
  378.3 9.5 %multiply_select_fusion = f32[8192,256]{1,0:T(8,128)} fusion(f32[8192,256]{1,0:T(8,128)} %collective-permute-done.1, f32[8192,256]{1,0:T(8,128)} %multiply_multiply_fusion, f32[256]{0:T(256)S(1)} %fusion, s32[256]{0:T(256)S(1)} %compare_select_fusion, s32[8192]{0:T(1024)S(1)} %iota_add_fusion, pred[]{:T(512)S(6)} %lt.18), kind=kLoop, calls=%fused_computation | loop fusion | flops 14680064 | bytes 25200640 | tf_op jit(solution)/shard_map/jit(_where)/select_n | solution.py:51
  (3 shorter events, 0.0 us)
Async XLA Ops:
  0.0 184.8 %collective-permute-start = (f32[8192,256]{1,0:T(8,128)}, f32[8192,256]{1,0:T(8,128)}, u32[]{:S(2)}, u32[]{:S(2)}) collective-permute-start(f32[8192,256]{1,0:T(8,128)} %param.2), channel_id=1, source_target_pairs={{0,64},{64,0},{16,80},{80,16},{32,96},{96,32},{48,112},{112,48},{1... | collective-permute-start | bytes 25165832 | tf_op jit(solution)/shard_map/ppermute | solution.py:17
  4.0 193.9 %slice-start = ((f32[8192]{0:T(1024)}), f32[2048]{0:T(1024)S(1)}, s32[]{:S(2)}) async-start(f32[8192]{0:T(1024)} %param.3), calls=%async_computation | async-start | bytes 16384 | tf_op jit(solution)/shard_map/slice | solution.py:43
  194.9 183.4 %collective-permute-start.1 = (f32[8192,256]{1,0:T(8,128)}, f32[8192,256]{1,0:T(8,128)}, u32[]{:S(2)}, u32[]{:S(2)}) collective-permute-start(f32[8192,256]{1,0:T(8,128)} %multiply_multiply_fusion), channel_id=1, source_target_pairs={{0,8},{8,0},{1,9},{9,1},{2,10},{10,2},{3,11},{11,3},{4,12},{12,4},... | collective-permute-start | bytes 25165832 | tf_op jit(solution)/shard_map/ppermute | solution.py:17
where the time goes:
time: 388 us
  waiting for transfers between devices  332 us (86%)
  blocking collectives  29 us (7%)
  other arithmetic  19.7 us (5%)
  starting transfers between devices  7.01 us (2%)
    ppermute x2, waiting for transfers between devices, from_partner(): return lax.ppermute(block, axis, route)  332 us
    all_gather x1, blocking collectives, per_device(): gathered = lax.all_gather(butterfly_scale[:W], 'row', axis=0, tiled=True)  29 us
    div x1, other arithmetic, row_pass(): return mixed * scale_here[:, None] / jnp.float32(2.0) ** 0.5  10.1 us
    select_n x1, other arithmetic, per_device(): return jnp.where(row_index >= global_col, mixed, jnp.float32(0.0))  9.48 us
  transfers between devices with their start and end apart: 2, of which 2 were waited for; matrix products, arithmetic and copies ran while one was open for 0% of the time, Pallas kernels for 0%

commit v1 on v0

v1 whole, which is shorter than its diff:
```python
import math

import jax
import jax.numpy as jnp
from jax import lax
from jax.experimental import pallas as pl
from jax.sharding import PartitionSpec as P


N = 65536
W = 2048
LANES = 128
SIZES = (512, 2560, 768, 256)


def from_partner(block, axis):
    count = lax.axis_size(axis)
    return lax.ppermute(block, axis, [(i, i ^ count // 2) for i in range(count)])


def in_first_half(axis):
    return lax.axis_index(axis) < lax.axis_size(axis) // 2


def rows_spec(tile, cols, start):
    return pl.BlockSpec((tile, cols), lambda i: (start // tile + i, 0))


def copy_rows(x, start, size):
    tile = math.gcd(start, size)
    cols = x.shape[1]

    def kernel(x_ref, out_ref):
        out_ref[...] = x_ref[...]

    return pl.pallas_call(
        kernel,
        grid=(size // tile,),
        in_specs=[rows_spec(tile, cols, start)],
        out_specs=rows_spec(tile, cols, 0),
        out_shape=jax.ShapeDtypeStruct((size, cols), x.dtype),
    )(x)


def mix_rows(x, partner, start, axis):
    size, cols = partner.shape
    tile = math.gcd(start, size)

    def kernel(x_ref, partner_ref, out_ref):
        sign = jnp.where(in_first_half(axis), jnp.float32(1.0), jnp.float32(-1.0))
        out_ref[...] = partner_ref[...] + sign * x_ref[...]

    return pl.pallas_call(
        kernel,
        grid=(size // tile,),
        in_specs=[rows_spec(tile, cols, start), rows_spec(tile, cols, 0)],
        out_specs=rows_spec(tile, cols, 0),
        out_shape=jax.ShapeDtypeStruct((size, cols), x.dtype),
    )(x, partner)


def finish_rows(out, mixed, across, row_scale, col_scale, start, axis, local_rows):
    size, cols = mixed.shape
    tile = math.gcd(start, size)

    def kernel(mixed_ref, across_ref, row_scale_ref, col_scale_ref, *rest):
        out_ref = rest[-1]
        sign = jnp.where(in_first_half(axis), jnp.float32(1.0), jnp.float32(-1.0))
        first_row = lax.axis_index("row") * local_rows + start + pl.program_id(0) * tile
        first_col = lax.axis_index("col") * cols
        first_col = jnp.where(first_col < W, first_col, N // 2 + first_col - W)
        col_scales = col_scale_ref[...]
        lead = lax.broadcasted_iota(jnp.int32, (LANES, cols), 0) - lax.broadcasted_iota(
            jnp.int32, (LANES, cols), 1
        )
        for g in range(tile // LANES):
            rows = pl.ds(g * LANES, LANES)
            at = start // LANES + pl.program_id(0) * (tile // LANES) + g
            scale = jnp.broadcast_to(row_scale_ref[pl.ds(at, 1), :], (LANES, LANES)).T
            both = across_ref[rows, :] + sign * mixed_ref[rows, :]
            both = both * (jnp.concatenate([scale] * (cols // LANES), axis=1) * col_scales)
            keep = lead >= first_col - first_row - g * LANES
            out_ref[rows, :] = jnp.where(keep, both, jnp.float32(0.0))

    in_specs = [
        rows_spec(tile, cols, 0),
        rows_spec(tile, cols, 0),
        pl.BlockSpec(row_scale.shape, lambda i: (0, 0)),
        pl.BlockSpec(col_scale.shape, lambda i: (0, 0)),
    ]
    operands = [mixed, across, row_scale, col_scale]
    aliases = {}
    if out is not None:
        in_specs.append(pl.BlockSpec(memory_space=pl.ANY))
        operands.append(out)
        aliases = {4: 0}
    return pl.pallas_call(
        kernel,
        grid=(size // tile,),
        in_specs=in_specs,
        out_specs=rows_spec(tile, cols, start),
        out_shape=jax.ShapeDtypeStruct((local_rows, cols), mixed.dtype),
        input_output_aliases=aliases,
    )(*operands)


def per_device(slab_pair, butterfly_scale):
    local_rows, local_cols = slab_pair.shape
    row_count = lax.axis_size("row")
    parts = []
    start = 0
    for size in SIZES:
        parts.append((start, size, "row", "col"))
        parts.append((local_rows // 2 + start, size, "col", "row"))
        start += size

    theirs = []
    for start, size, first, _ in parts:
        block = copy_rows(slab_pair, start, size)
        theirs.append(from_partner(block, first))

    at = lax.axis_index("col") * local_cols % W
    piece = lax.dynamic_slice_in_dim(butterfly_scale, at, local_cols, 0)
    pieces = lax.all_gather(piece, "row", axis=0)
    left = in_first_half("col")
    col_scale = jnp.where(left, pieces[0], pieces[row_count // 2])[None, :] * 0.5
    row_scale = butterfly_scale.reshape(-1, LANES)

    mixes, acrosses = [], []
    for j, (start, size, first, second) in enumerate(parts):
        mixes.append(mix_rows(slab_pair, theirs[j], start, first))
        acrosses.append(from_partner(mixes[j], second))

    out = None
    for j, (start, size, first, second) in enumerate(parts):
        out = finish_rows(
            out, mixes[j], acrosses[j], row_scale, col_scale, start, second, local_rows
        )
    return out


def solution(mesh):
    in_specs = (P("row", "col"), P("row"))
    out_specs = P("row", "col")
    return jax.shard_map(
        per_device, mesh=mesh, in_specs=in_specs, out_specs=out_specs, check_vma=False
    )
```

time: 388 us -> 264 us (0.68)
  waiting for transfers between devices: 332 us -> 136 us
  Pallas kernels: 0 us -> 70.8 us
  starting transfers between devices: 7.01 us -> 31.9 us
  other arithmetic: 19.7 us -> 0.58 us
  blocking collectives: 29 us -> 18.4 us
    ppermute x2 -> x16, waiting for transfers between devices: 332 us -> 136 us  [from_partner(): lax.ppermute(block, axis, [(i, i ^ count // 2) for i in range(count)])]
    pallas_call x0 -> x24, Pallas kernels: none -> 70.8 us  [the longest x8 25.2 us: finish_rows(): pl.pallas_call(kernel, grid=(size // tile,), in_specs=in_specs, out_specs...]
    ppermute x2 -> x16, starting transfers between devices: 7.01 us -> 31.9 us  [from_partner(): lax.ppermute(block, axis, [(i, i ^ count // 2) for i in range(count)])]
    all_gather x1, blocking collectives: 29 us -> 18.4 us  [per_device(): pieces = lax.all_gather(piece, 'row', axis=0)]
    div x1 -> x0, other arithmetic: 10.1 us -> none  [row_pass(): return mixed * scale_here[:, None] / jnp.float32(2.0) ** 0.5]
    select_n x2 -> x0, other arithmetic: 9.48 us -> none  [the longest x1 9.48 us: per_device(): return jnp.where(row_index >= global_col, mixed, jnp.float32(0.0))]
  transfers between devices with their start and end apart: 2 -> 16, of which waited for: 2 -> 4; matrix products, arithmetic and copies ran while one was open for 0% -> 1% of each run, Pallas kernels for 0% -> 25%
where the time goes in v1:
time: 264 us; the launch traced here: 262 us
  waiting for transfers between devices  136 us (52%)
  Pallas kernels  70.8 us (27%)
  starting transfers between devices  31.9 us (12%)
  blocking collectives  18.4 us (7%)
  local copies, waits for them, and re-layouts  3.78 us (1%)
    ppermute x16, waiting for transfers between devices, from_partner(): lax.ppermute(block, axis, [(i, i ^ count // 2) for i in range(count)])  136 us
    ppermute x16, starting transfers between devices, from_partner(): lax.ppermute(block, axis, [(i, i ^ count // 2) for i in range(count)])  31.9 us
    pallas_call x8, Pallas kernels, finish_rows(): pl.pallas_call(kernel, grid=(size // tile,), in_specs=in_specs, out_specs...  25.2 us
    pallas_call x8, Pallas kernels, mix_rows(): pl.pallas_call(kernel, grid=(size // tile,), in_specs=[rows_spec(tile, co...  24.1 us
    pallas_call x8, Pallas kernels, copy_rows(): pl.pallas_call(kernel, grid=(size // tile,), in_specs=[rows_spec(tile, co...  21.5 us
    all_gather x1, blocking collectives, per_device(): pieces = lax.all_gather(piece, 'row', axis=0)  18.4 us
  transfers between devices with their start and end apart: 16, of which 4 were waited for; matrix products, arithmetic and copies ran while one was open for 1% of the time, Pallas kernels for 25%

profile of v1, /device:TPU:0, one launch (start us, length us, event | category | flops | bytes accessed | tf_op | source)
XLA Modules:
  0.0 261.5 jit_solution(12957005066670805941)
XLA Ops:
  0.0 4.7 %shard_map.38 = f32[2560,256]{1,0:T(8,128)} custom-call(f32[8192,256]{1,0:T(8,128)} %x_ref.31), custom_call_target="tpu_custom_call" | custom-call | tf_op jit(solution)/shard_map/pallas_call | solution.py:36
  4.7 4.0 %collective-permute-start.10 = (f32[2560,256]{1,0:T(8,128)}, f32[2560,256]{1,0:T(8,128)}, u32[]{:S(2)}, u32[]{:S(2)}) collective-permute-start(f32[2560,256]{1,0:T(8,128)} %shard_map.38), channel_id=1, source_target_pairs={{0,64},{16,80},{32,96},{48,112},{64,0},{80,16},{96,32},{112,48},{1... | collective-permute-start | bytes 7864328 | tf_op jit(solution)/shard_map/ppermute | solution.py:18
  8.7 4.7 %shard_map.36 = f32[2560,256]{1,0:T(8,128)} custom-call(f32[8192,256]{1,0:T(8,128)} %x_ref.31), custom_call_target="tpu_custom_call" | custom-call | tf_op jit(solution)/shard_map/pallas_call | solution.py:36
  13.4 3.0 %collective-permute-start.8 = (f32[2560,256]{1,0:T(8,128)}, f32[2560,256]{1,0:T(8,128)S(1)}, u32[]{:S(2)}, u32[]{:S(2)}) collective-permute-start(f32[2560,256]{1,0:T(8,128)} %shard_map.36), channel_id=1, source_target_pairs={{0,8},{1,9},{2,10},{3,11},{4,12},{5,13},{6,14},{7,15},{8,0},{9,1},... | collective-permute-start | bytes 7864328 | tf_op jit(solution)/shard_map/ppermute | solution.py:18
  16.4 49.5 %collective-permute-done.10.partner_ref = f32[2560,256]{1,0:T(8,128)} collective-permute-done((f32[2560,256]{1,0:T(8,128)}, f32[2560,256]{1,0:T(8,128)}, u32[]{:S(2)}, u32[]{:S(2)}) %collective-permute-start.10) | collective-permute-done | bytes 2621472 | tf_op jit(solution)/shard_map/ppermute | solution.py:18
  65.9 5.5 %shard_map.39.mixed_ref = f32[2560,256]{1,0:T(8,128)} custom-call(f32[8192,256]{1,0:T(8,128)} %x_ref.31, f32[2560,256]{1,0:T(8,128)} %collective-permute-done.10.partner_ref), custom_call_target="tpu_custom_call" | custom-call | tf_op jit(solution)/shard_map/pallas_call | solution.py:53
  71.3 3.0 %collective-permute-start.11 = (f32[2560,256]{1,0:T(8,128)}, f32[2560,256]{1,0:T(8,128)}, u32[]{:S(2)}, u32[]{:S(2)}) collective-permute-start(f32[2560,256]{1,0:T(8,128)} %shard_map.39.mixed_ref), channel_id=1, source_target_pairs={{0,8},{1,9},{2,10},{3,11},{4,12},{5,13},{6,14},{7,15},{8,0},{9,1},... | collective-permute-start | bytes 7864328 | tf_op jit(solution)/shard_map/ppermute | solution.py:18
  75.9 5.5 %shard_map.37.mixed_ref = f32[2560,256]{1,0:T(8,128)} custom-call(f32[8192,256]{1,0:T(8,128)} %x_ref.31, f32[2560,256]{1,0:T(8,128)} %copy-done.1), custom_call_target="tpu_custom_call" | custom-call | tf_op jit(solution)/shard_map/pallas_call | solution.py:53
  81.3 3.2 %collective-permute-start.9 = (f32[2560,256]{1,0:T(8,128)}, f32[2560,256]{1,0:T(8,128)S(1)}, u32[]{:S(2)}, u32[]{:S(2)}) collective-permute-start(f32[2560,256]{1,0:T(8,128)} %shard_map.37.mixed_ref), channel_id=1, source_target_pairs={{0,64},{16,80},{32,96},{48,112},{64,0},{80,16},{96,32},{112,48},{1... | collective-permute-start | bytes 7864328 | tf_op jit(solution)/shard_map/ppermute | solution.py:18
  88.9 3.2 %collective-permute-start.6 = (f32[768,256]{1,0:T(8,128)}, f32[768,256]{1,0:T(8,128)S(1)}, u32[]{:S(2)}, u32[]{:S(2)}) collective-permute-start(f32[768,256]{1,0:T(8,128)} %shard_map.34), channel_id=1, source_target_pairs={{0,64},{16,80},{32,96},{48,112},{64,0},{80,16},{96,32},{112,48},{1... | collective-permute-start | bytes 2359304 | tf_op jit(solution)/shard_map/ppermute | solution.py:18
  92.2 2.9 %shard_map.32 = f32[768,256]{1,0:T(8,128)} custom-call(f32[8192,256]{1,0:T(8,128)} %x_ref.31), custom_call_target="tpu_custom_call" | custom-call | tf_op jit(solution)/shard_map/pallas_call | solution.py:36
  97.4 56.7 %collective-permute-done.14.partner_ref = f32[512,256]{1,0:T(8,128)} collective-permute-done((f32[512,256]{1,0:T(8,128)}, f32[512,256]{1,0:T(8,128)}, u32[]{:S(2)}, u32[]{:S(2)}) %collective-permute-start.14) | collective-permute-done | bytes 524320 | tf_op jit(solution)/shard_map/ppermute | solution.py:18
  158.2 8.0 %collective-permute-done.12.partner_ref = f32[512,256]{1,0:T(8,128)} collective-permute-done((f32[512,256]{1,0:T(8,128)}, f32[512,256]{1,0:T(8,128)}, u32[]{:S(2)}, u32[]{:S(2)}) %collective-permute-start.12) | collective-permute-done | bytes 524320 | tf_op jit(solution)/shard_map/ppermute | solution.py:18
  173.3 3.0 %collective-permute-start = (f32[256,256]{1,0:T(8,128)}, f32[256,256]{1,0:T(8,128)}, u32[]{:S(2)}, u32[]{:S(2)}) collective-permute-start(f32[256,256]{1,0:T(8,128)} %shard_map.28), channel_id=1, source_target_pairs={{0,8},{1,9},{2,10},{3,11},{4,12},{5,13},{6,14},{7,15},{8,0},{9,1},... | collective-permute-start | bytes 786440 | tf_op jit(solution)/shard_map/ppermute | solution.py:18
  178.4 2.4 shard_map.35.mixed_ref
  180.8 3.1 %shard_map.33.mixed_ref = f32[768,256]{1,0:T(8,128)} custom-call(f32[8192,256]{1,0:T(8,128)} %x_ref.31, f32[768,256]{1,0:T(8,128)} %collective-permute-done.4.partner_ref), custom_call_target="tpu_custom_call" | custom-call | tf_op jit(solution)/shard_map/pallas_call | solution.py:53
  184.5 3.9 %collective-permute-start.5 = (f32[768,256]{1,0:T(8,128)}, f32[768,256]{1,0:T(8,128)}, u32[]{:S(2)}, u32[]{:S(2)}) collective-permute-start(f32[768,256]{1,0:T(8,128)} %shard_map.33.mixed_ref), channel_id=1, source_target_pairs={{0,64},{16,80},{32,96},{48,112},{64,0},{80,16},{96,32},{112,48},{1... | collective-permute-start | bytes 2359304 | tf_op jit(solution)/shard_map/ppermute | solution.py:18
  192.0 21.8 %collective-permute-done.13.across_ref = f32[512,256]{1,0:T(8,128)} collective-permute-done((f32[512,256]{1,0:T(8,128)}, f32[512,256]{1,0:T(8,128)}, u32[]{:S(2)}, u32[]{:S(2)}) %collective-permute-start.13) | collective-permute-done | bytes 524320 | tf_op jit(solution)/shard_map/ppermute | solution.py:18
  215.8 18.4 %all-gather.1 = f32[8,1,256]{2,1,0:T(1,128)S(1)} all-gather(f32[1,1,256]{2,1,0:T(1,128)S(1)} %bitcast.12), channel_id=2, replica_groups=mesh['row'=8,'col'=16] {'row'}, dimensions={0}, use_global_device_ids=true | all-gather | bytes 9216 | tf_op jit(solution)/shard_map/all_gather | solution.py:124
  236.9 2.1 shard_map.45.rest_0_
  239.1 5.8 %shard_map.46.rest_0_ = f32[8192,256]{1,0:T(8,128)} custom-call(f32[2560,256]{1,0:T(8,128)} %shard_map.39.mixed_ref, f32[2560,256]{1,0:T(8,128)} %collective-permute-done.11.across_ref, f32[64,128]{1,0:T(8,128)} %bitcast.6, f32[1,256]{1,0:T(1,128)} %fusion.1.col_scale_ref, f32[8192,256]{1,0:T(8,128)} %shard_map.45.rest_0_), custom_call_target="tpu_custom_call", output_to_operand_aliasing={{}: (4, {})} | custom-call | tf_op jit(solution)/shard_map/pallas_call | solution.py:97
  246.4 5.8 %shard_map.47.rest_0_ = f32[8192,256]{1,0:T(8,128)} custom-call(f32[2560,256]{1,0:T(8,128)} %shard_map.37.mixed_ref, f32[2560,256]{1,0:T(8,128)} %copy-done.2, f32[64,128]{1,0:T(8,128)} %bitcast.7, f32[1,256]{1,0:T(1,128)} %fusion.1.col_scale_ref, f32[8192,256]{1,0:T(8,128)} %shard_map.46.rest_0_), custom_call_target="tpu_custom_call", output_to_operand_aliasing={{}: (4, {})} | custom-call | tf_op jit(solution)/shard_map/pallas_call | solution.py:97
  252.1 2.5 shard_map.48.rest_0_
  254.6 3.2 %shard_map.49.rest_0_ = f32[8192,256]{1,0:T(8,128)} custom-call(f32[768,256]{1,0:T(8,128)} %shard_map.33.mixed_ref, f32[768,256]{1,0:T(8,128)} %collective-permute-done.5.across_ref, f32[64,128]{1,0:T(8,128)} %bitcast.9, f32[1,256]{1,0:T(1,128)} %fusion.1.col_scale_ref, f32[8192,256]{1,0:T(8,128)} %shard_map.48.rest_0_), custom_call_target="tpu_custom_call", output_to_operand_aliasing={{}: (4, {})} | custom-call | tf_op jit(solution)/shard_map/pallas_call | solution.py:97
  (43 shorter events, 35.5 us)
Async XLA Ops:
  4.7 61.2 %collective-permute-start.10 = (f32[2560,256]{1,0:T(8,128)}, f32[2560,256]{1,0:T(8,128)}, u32[]{:S(2)}, u32[]{:S(2)}) collective-permute-start(f32[2560,256]{1,0:T(8,128)} %shard_map.38), channel_id=1, source_target_pairs={{0,64},{16,80},{32,96},{48,112},{64,0},{80,16},{96,32},{112,48},{1... | collective-permute-start | bytes 7864328 | tf_op jit(solution)/shard_map/ppermute | solution.py:18
  13.4 61.0 %collective-permute-start.8 = (f32[2560,256]{1,0:T(8,128)}, f32[2560,256]{1,0:T(8,128)S(1)}, u32[]{:S(2)}, u32[]{:S(2)}) collective-permute-start(f32[2560,256]{1,0:T(8,128)} %shard_map.36), channel_id=1, source_target_pairs={{0,8},{1,9},{2,10},{3,11},{4,12},{5,13},{6,14},{7,15},{8,0},{9,1},... | collective-permute-start | bytes 7864328 | tf_op jit(solution)/shard_map/ppermute | solution.py:18
  71.3 142.6 %collective-permute-start.11 = (f32[2560,256]{1,0:T(8,128)}, f32[2560,256]{1,0:T(8,128)}, u32[]{:S(2)}, u32[]{:S(2)}) collective-permute-start(f32[2560,256]{1,0:T(8,128)} %shard_map.39.mixed_ref), channel_id=1, source_target_pairs={{0,8},{1,9},{2,10},{3,11},{4,12},{5,13},{6,14},{7,15},{8,0},{9,1},... | collective-permute-start | bytes 7864328 | tf_op jit(solution)/shard_map/ppermute | solution.py:18
  74.4 1.5 copy-start.1
  81.3 163.5 %collective-permute-start.9 = (f32[2560,256]{1,0:T(8,128)}, f32[2560,256]{1,0:T(8,128)S(1)}, u32[]{:S(2)}, u32[]{:S(2)}) collective-permute-start(f32[2560,256]{1,0:T(8,128)} %shard_map.37.mixed_ref), channel_id=1, source_target_pairs={{0,64},{16,80},{32,96},{48,112},{64,0},{80,16},{96,32},{112,48},{1... | collective-permute-start | bytes 7864328 | tf_op jit(solution)/shard_map/ppermute | solution.py:18
  86.5 67.6 %collective-permute-start.14 = (f32[512,256]{1,0:T(8,128)}, f32[512,256]{1,0:T(8,128)}, u32[]{:S(2)}, u32[]{:S(2)}) collective-permute-start(f32[512,256]{1,0:T(8,128)} %shard_map.42), channel_id=1, source_target_pairs={{0,64},{16,80},{32,96},{48,112},{64,0},{80,16},{96,32},{112,48},{1... | collective-permute-start | bytes 1572872 | tf_op jit(solution)/shard_map/ppermute | solution.py:18
  88.9 82.7 %collective-permute-start.6 = (f32[768,256]{1,0:T(8,128)}, f32[768,256]{1,0:T(8,128)S(1)}, u32[]{:S(2)}, u32[]{:S(2)}) collective-permute-start(f32[768,256]{1,0:T(8,128)} %shard_map.34), channel_id=1, source_target_pairs={{0,64},{16,80},{32,96},{48,112},{64,0},{80,16},{96,32},{112,48},{1... | collective-permute-start | bytes 2359304 | tf_op jit(solution)/shard_map/ppermute | solution.py:18
  95.0 78.3 %collective-permute-start.4 = (f32[768,256]{1,0:T(8,128)}, f32[768,256]{1,0:T(8,128)}, u32[]{:S(2)}, u32[]{:S(2)}) collective-permute-start(f32[768,256]{1,0:T(8,128)} %shard_map.32), channel_id=1, source_target_pairs={{0,8},{1,9},{2,10},{3,11},{4,12},{5,13},{6,14},{7,15},{8,0},{9,1},... | collective-permute-start | bytes 2359304 | tf_op jit(solution)/shard_map/ppermute | solution.py:18
  154.1 12.1 %collective-permute-start.12 = (f32[512,256]{1,0:T(8,128)}, f32[512,256]{1,0:T(8,128)}, u32[]{:S(2)}, u32[]{:S(2)}) collective-permute-start(f32[512,256]{1,0:T(8,128)} %shard_map.40), channel_id=1, source_target_pairs={{0,8},{1,9},{2,10},{3,11},{4,12},{5,13},{6,14},{7,15},{8,0},{9,1},... | collective-permute-start | bytes 1572872 | tf_op jit(solution)/shard_map/ppermute | solution.py:18
  166.2 22.3 %collective-permute-start.15 = (f32[512,256]{1,0:T(8,128)}, f32[512,256]{1,0:T(8,128)}, u32[]{:S(2)}, u32[]{:S(2)}) collective-permute-start(f32[512,256]{1,0:T(8,128)} %shard_map.43.mixed_ref), channel_id=1, source_target_pairs={{0,8},{1,9},{2,10},{3,11},{4,12},{5,13},{6,14},{7,15},{8,0},{9,1},... | collective-permute-start | bytes 1572872 | tf_op jit(solution)/shard_map/ppermute | solution.py:18
  171.6 6.8 %copy-start.3 = (f32[768,256]{1,0:T(8,128)}, f32[768,256]{1,0:T(8,128)S(1)}, u32[]{:S(2)}) copy-start(f32[768,256]{1,0:T(8,128)S(1)} %collective-permute-done.6.partner_ref) | copy-start | bytes 2359300
  171.6 12.3 %collective-permute-start.2 = (f32[256,256]{1,0:T(8,128)}, f32[256,256]{1,0:T(8,128)}, u32[]{:S(2)}, u32[]{:S(2)}) collective-permute-start(f32[256,256]{1,0:T(8,128)} %shard_map.30), channel_id=1, source_target_pairs={{0,64},{16,80},{32,96},{48,112},{64,0},{80,16},{96,32},{112,48},{1... | collective-permute-start | bytes 786440 | tf_op jit(solution)/shard_map/ppermute | solution.py:18
  173.3 11.2 %collective-permute-start = (f32[256,256]{1,0:T(8,128)}, f32[256,256]{1,0:T(8,128)}, u32[]{:S(2)}, u32[]{:S(2)}) collective-permute-start(f32[256,256]{1,0:T(8,128)} %shard_map.28), channel_id=1, source_target_pairs={{0,8},{1,9},{2,10},{3,11},{4,12},{5,13},{6,14},{7,15},{8,0},{9,1},... | collective-permute-start | bytes 786440 | tf_op jit(solution)/shard_map/ppermute | solution.py:18
  180.8 3.1 %copy-start = (f32[768,256]{1,0:T(8,128)S(1)}, f32[768,256]{1,0:T(8,128)}, u32[]{:S(2)}) copy-start(f32[768,256]{1,0:T(8,128)} %shard_map.35.mixed_ref) | copy-start | bytes 2359300
  184.0 68.2 %collective-permute-start.7 = (f32[768,256]{1,0:T(8,128)S(1)}, f32[768,256]{1,0:T(8,128)}, u32[]{:S(2)}, u32[]{:S(2)}) collective-permute-start(f32[768,256]{1,0:T(8,128)S(1)} %copy-done), channel_id=1, source_target_pairs={{0,8},{1,9},{2,10},{3,11},{4,12},{5,13},{6,14},{7,15},{8,0},{9,1},... | collective-permute-start | bytes 2359304 | tf_op jit(solution)/shard_map/ppermute | solution.py:18
  184.5 70.0 %collective-permute-start.5 = (f32[768,256]{1,0:T(8,128)}, f32[768,256]{1,0:T(8,128)}, u32[]{:S(2)}, u32[]{:S(2)}) collective-permute-start(f32[768,256]{1,0:T(8,128)} %shard_map.33.mixed_ref), channel_id=1, source_target_pairs={{0,64},{16,80},{32,96},{48,112},{64,0},{80,16},{96,32},{112,48},{1... | collective-permute-start | bytes 2359304 | tf_op jit(solution)/shard_map/ppermute | solution.py:18
  188.5 25.4 %collective-permute-start.13 = (f32[512,256]{1,0:T(8,128)}, f32[512,256]{1,0:T(8,128)}, u32[]{:S(2)}, u32[]{:S(2)}) collective-permute-start(f32[512,256]{1,0:T(8,128)} %shard_map.41.mixed_ref), channel_id=1, source_target_pairs={{0,64},{16,80},{32,96},{48,112},{64,0},{80,16},{96,32},{112,48},{1... | collective-permute-start | bytes 1572872 | tf_op jit(solution)/shard_map/ppermute | solution.py:18
  213.9 43.9 %collective-permute-start.3 = (f32[256,256]{1,0:T(8,128)}, f32[256,256]{1,0:T(8,128)}, u32[]{:S(2)}, u32[]{:S(2)}) collective-permute-start(f32[256,256]{1,0:T(8,128)} %shard_map.31.mixed_ref), channel_id=1, source_target_pairs={{0,8},{1,9},{2,10},{3,11},{4,12},{5,13},{6,14},{7,15},{8,0},{9,1},... | collective-permute-start | bytes 786440 | tf_op jit(solution)/shard_map/ppermute | solution.py:18
  213.9 45.8 %collective-permute-start.1 = (f32[256,256]{1,0:T(8,128)}, f32[256,256]{1,0:T(8,128)}, u32[]{:S(2)}, u32[]{:S(2)}) collective-permute-start(f32[256,256]{1,0:T(8,128)} %shard_map.29.mixed_ref), channel_id=1, source_target_pairs={{0,64},{16,80},{32,96},{48,112},{64,0},{80,16},{96,32},{112,48},{1... | collective-permute-start | bytes 786440 | tf_op jit(solution)/shard_map/ppermute | solution.py:18
  244.9 1.5 copy-start.2

commit v2 on v0

v2 whole, which is shorter than its diff:
```python
import jax
import jax.numpy as jnp
from jax import lax
from jax.experimental import pallas as pl
from jax.experimental.pallas import tpu as pltpu
from jax.sharding import PartitionSpec as P


N = 65536
W = 2048
SIZES = (512, 2688, 768, 128)


def from_partner(block, axis):
    count = lax.axis_size(axis)
    return lax.ppermute(block, axis, [(i, i ^ count // 2) for i in range(count)])


def in_first_half(axis):
    return lax.axis_index(axis) < lax.axis_size(axis) // 2


def kept_apart(*arrays):
    return lax.optimization_barrier(arrays)


def copy_rows(x, start, size):
    (x,) = kept_apart(x)
    return lax.slice_in_dim(x, start, start + size)


def mix_rows(x, partner, start, axis):
    x, partner = kept_apart(x, partner)
    block = lax.slice_in_dim(x, start, start + partner.shape[0])
    return jnp.where(in_first_half(axis), partner + block, partner - block)


def first_global_col(cols):
    first = lax.axis_index("col") * cols
    return jnp.where(first < W, first, N // 2 + first - W)


def unwritten(shape, dtype):
    return pl.pallas_call(
        lambda out_ref: None,
        out_specs=pl.BlockSpec(memory_space=pltpu.HBM),
        out_shape=jax.ShapeDtypeStruct(shape, dtype),
    )()


def finish_rows(out, mixed, across, row_scale, col_scale, start, axis):
    size, cols = mixed.shape
    both = jnp.where(in_first_half(axis), across + mixed, across - mixed)
    both = both * (row_scale[start : start + size, None] * col_scale)
    gap = first_global_col(cols) - lax.axis_index("row") * row_scale.shape[0] - start
    row = lax.broadcasted_iota(jnp.int32, (size, cols), 0)
    col = lax.broadcasted_iota(jnp.int32, (size, cols), 1)
    kept = jnp.where(row - col >= gap, both, jnp.float32(0.0))
    return lax.dynamic_update_slice(out, kept, (start, 0))


def per_device(slab_pair, butterfly_scale):
    local_rows, local_cols = slab_pair.shape
    row_count = lax.axis_size("row")
    parts = []
    start = 0
    for size in SIZES:
        parts.append((start, size, "row", "col"))
        parts.append((local_rows // 2 + start, size, "col", "row"))
        start += size

    theirs = []
    for start, size, first, _ in parts:
        block = copy_rows(slab_pair, start, size)
        theirs.append(from_partner(block, first))

    at = lax.axis_index("col") * local_cols % W
    piece = lax.dynamic_slice_in_dim(butterfly_scale, at, local_cols, 0)
    pieces = lax.all_gather(piece, "row", axis=0)
    left = in_first_half("col")
    col_scale = jnp.where(left, pieces[0], pieces[row_count // 2]) * 0.5

    mixes, acrosses = [], []
    for j, (start, size, first, second) in enumerate(parts):
        mixes.append(mix_rows(slab_pair, theirs[j], start, first))
        acrosses.append(from_partner(mixes[j], second))

    out = unwritten(slab_pair.shape, slab_pair.dtype)
    for j, (start, _, _, axis) in enumerate(parts):
        out = finish_rows(out, mixes[j], acrosses[j], butterfly_scale, col_scale, start, axis)
    return out


def solution(mesh):
    in_specs = (P("row", "col"), P("row"))
    out_specs = P("row", "col")
    return jax.shard_map(
        per_device, mesh=mesh, in_specs=in_specs, out_specs=out_specs, check_vma=False
    )
```

time: 388 us -> 217 us (0.56)
  waiting for transfers between devices: 332 us -> 133 us
  starting transfers between devices: 7.01 us -> 32.6 us
  local copies, waits for them, and re-layouts: 0.01 us -> 17 us
  blocking collectives: 29 us -> 16.9 us
    ppermute x2 -> x16, waiting for transfers between devices: 332 us -> 133 us  [from_partner(): lax.ppermute(block, axis, [(i, i ^ count // 2) for i in range(count)])]
    ppermute x2 -> x16, starting transfers between devices: 7.01 us -> 32.6 us  [from_partner(): lax.ppermute(block, axis, [(i, i ^ count // 2) for i in range(count)])]
    slice x3 -> x8, local copies, waits for them, and re-layouts: 0.01 us -> 12.8 us  [the longest x4 9.98 us: copy_rows(): return lax.slice_in_dim(x, start, start + size)]
    all_gather x1, blocking collectives: 29 us -> 16.9 us  [per_device(): pieces = lax.all_gather(piece, 'row', axis=0)]
    div x1 -> x0, other arithmetic: 10.1 us -> none  [row_pass(): return mixed * scale_here[:, None] / jnp.float32(2.0) ** 0.5]
    dynamic_update_slice x0 -> x8, other arithmetic: none -> 4.34 us  [finish_rows(): return lax.dynamic_update_slice(out, kept, (start, 0))]
    select_n x2 -> x8, other arithmetic: 9.48 us -> 12.8 us  [mix_rows(): return jnp.where(in_first_half(axis), partner + block, partner - block)]
  transfers between devices with their start and end apart: 2 -> 16, of which waited for: 2 -> 6; matrix products, arithmetic and copies ran while one was open for 0% -> 12% of each run, Pallas kernels for 0% -> 0%
where the time goes in v2:
time: 217 us
  waiting for transfers between devices  133 us (61%)
  starting transfers between devices  32.6 us (15%)
  other arithmetic  17.2 us (8%)
  local copies, waits for them, and re-layouts  17 us (8%)
  blocking collectives  16.9 us (8%)
    ppermute x16, waiting for transfers between devices, from_partner(): lax.ppermute(block, axis, [(i, i ^ count // 2) for i in range(count)])  133 us
    ppermute x16, starting transfers between devices, from_partner(): lax.ppermute(block, axis, [(i, i ^ count // 2) for i in range(count)])  32.6 us
    all_gather x1, blocking collectives, per_device(): pieces = lax.all_gather(piece, 'row', axis=0)  16.9 us
    select_n x8, other arithmetic, mix_rows(): return jnp.where(in_first_half(axis), partner + block, partner - block)  12.8 us
    slice x4, local copies, waits for them, and re-layouts, copy_rows(): return lax.slice_in_dim(x, start, start + size)  9.98 us
    dynamic_update_slice x8, other arithmetic, finish_rows(): return lax.dynamic_update_slice(out, kept, (start, 0))  4.34 us
  transfers between devices with their start and end apart: 16, of which 6 were waited for; matrix products, arithmetic and copies ran while one was open for 12% of the time, Pallas kernels for 0%

profile of v2, /device:TPU:0, one launch (start us, length us, event | category | flops | bytes accessed | tf_op | source)
XLA Modules:
  0.0 216.6 jit_solution(2334840023576769899)
XLA Ops:
  0.0 4.5 %fusion.11 = (f32[2688,256]{1,0:T(8,128)S(1)}, f32[2688,256]{1,0:T(8,128)}) fusion(f32[8192,256]{1,0:T(8,128)} %param.2), kind=kLoop, calls=%fused_computation.32 | loop fusion | bytes 11010048 | tf_op jit(solution)/shard_map/slice | solution.py:29
  4.5 4.0 %collective-permute-start.4 = (f32[2688,256]{1,0:T(8,128)}, f32[2688,256]{1,0:T(8,128)}, u32[]{:S(2)}, u32[]{:S(2)}) collective-permute-start(f32[2688,256]{1,0:T(8,128)} %get-tuple-element.42), channel_id=1, source_target_pairs={{0,64},{16,80},{32,96},{48,112},{64,0},{80,16},{96,32},{112,48},{1... | collective-permute-start | bytes 8257544 | tf_op jit(solution)/shard_map/ppermute | solution.py:16
  8.5 2.3 %fusion.12 = (f32[512,256]{1,0:T(8,128)}, f32[512,256]{1,0:T(8,128)}) fusion(f32[8192,256]{1,0:T(8,128)} %param.2), kind=kLoop, calls=%fused_computation.33 | loop fusion | bytes 2097152 | tf_op jit(solution)/shard_map/slice | solution.py:29
  10.8 3.0 %collective-permute-start.6 = (f32[2688,256]{1,0:T(8,128)S(1)}, f32[2688,256]{1,0:T(8,128)}, u32[]{:S(2)}, u32[]{:S(2)}) collective-permute-start(f32[2688,256]{1,0:T(8,128)S(1)} %get-tuple-element.41), channel_id=1, source_target_pairs={{0,8},{1,9},{2,10},{3,11},{4,12},{5,13},{6,14},{7,15},{8,0},{9,1},... | collective-permute-start | bytes 8257544 | tf_op jit(solution)/shard_map/ppermute | solution.py:16
  13.9 1.7 fusion.9
  15.5 3.5 %collective-permute-start.12 = (f32[128,256]{1,0:T(8,128)}, f32[128,256]{1,0:T(8,128)S(1)}, u32[]{:S(2)}, u32[]{:S(2)}) collective-permute-start(f32[128,256]{1,0:T(8,128)} %get-tuple-element.38), channel_id=1, source_target_pairs={{0,64},{16,80},{32,96},{48,112},{64,0},{80,16},{96,32},{112,48},{1... | collective-permute-start | bytes 393224 | tf_op jit(solution)/shard_map/ppermute | solution.py:16
  20.4 16.9 %all-gather.1 = f32[8,1,256]{2,1,0:T(1,128)S(1)} all-gather(f32[1,1,256]{2,1,0:T(1,128)S(1)} %bitcast.12), channel_id=2, replica_groups=mesh['row'=8,'col'=16] {'row'}, dimensions={0}, use_global_device_ids=true | all-gather | bytes 9216 | tf_op jit(solution)/shard_map/all_gather | solution.py:79
  40.2 1.5 fusion.10
  41.6 40.9 %collective-permute-done.12 = f32[128,256]{1,0:T(8,128)S(1)} collective-permute-done((f32[128,256]{1,0:T(8,128)}, f32[128,256]{1,0:T(8,128)S(1)}, u32[]{:S(2)}, u32[]{:S(2)}) %collective-permute-start.12) | collective-permute-done | bytes 131104 | tf_op jit(solution)/shard_map/ppermute | solution.py:16
  82.5 3.0 %collective-permute-start.2 = (f32[512,256]{1,0:T(8,128)S(1)}, f32[512,256]{1,0:T(8,128)S(1)}, u32[]{:S(2)}, u32[]{:S(2)}) collective-permute-start(f32[512,256]{1,0:T(8,128)S(1)} %copy-done.1), channel_id=1, source_target_pairs={{0,8},{1,9},{2,10},{3,11},{4,12},{5,13},{6,14},{7,15},{8,0},{9,1},... | collective-permute-start | bytes 1572872 | tf_op jit(solution)/shard_map/ppermute | solution.py:16
  85.6 3.2 %collective-permute-start.8 = (f32[768,256]{1,0:T(8,128)S(1)}, f32[768,256]{1,0:T(8,128)S(1)}, u32[]{:S(2)}, u32[]{:S(2)}) collective-permute-start(f32[768,256]{1,0:T(8,128)S(1)} %get-tuple-element.40), channel_id=1, source_target_pairs={{0,64},{16,80},{32,96},{48,112},{64,0},{80,16},{96,32},{112,48},{1... | collective-permute-start | bytes 2359304 | tf_op jit(solution)/shard_map/ppermute | solution.py:16
  90.3 3.0 %subtract_select_fusion.1 = f32[2688,256]{1,0:T(8,128)S(1)} fusion(f32[2688,256]{1,0:T(8,128)} %collective-permute-done.4, f32[8192,256]{1,0:T(8,128)} %param.2, pred[]{:T(512)S(6)} %lt.16), kind=kLoop, calls=%fused_computation.3 | loop fusion | flops 2064384 | bytes 8257537 | tf_op jit(solution)/shard_map/jit(_where)/select_n | solution.py:35
  93.3 3.1 %collective-permute-start.5 = (f32[2688,256]{1,0:T(8,128)S(1)}, f32[2688,256]{1,0:T(8,128)S(1)}, u32[]{:S(2)}, u32[]{:S(2)}) collective-permute-start(f32[2688,256]{1,0:T(8,128)S(1)} %subtract_select_fusion.1), channel_id=1, source_target_pairs={{0,8},{1,9},{2,10},{3,11},{4,12},{5,13},{6,14},{7,15},{8,0},{9,1},... | collective-permute-start | bytes 8257544 | tf_op jit(solution)/shard_map/ppermute | solution.py:16
  96.4 3.1 %subtract_select_fusion = f32[2688,256]{1,0:T(8,128)S(1)} fusion(f32[2688,256]{1,0:T(8,128)} %collective-permute-done.6, f32[8192,256]{1,0:T(8,128)} %param.2, pred[]{:T(512)S(6)} %lt.15), kind=kLoop, calls=%fused_computation.1 | loop fusion | flops 2064384 | bytes 8257537 | tf_op jit(solution)/shard_map/jit(_where)/select_n | solution.py:35
  104.1 3.4 %collective-permute-done.8 = f32[768,256]{1,0:T(8,128)S(1)} collective-permute-done((f32[768,256]{1,0:T(8,128)S(1)}, f32[768,256]{1,0:T(8,128)S(1)}, u32[]{:S(2)}, u32[]{:S(2)}) %collective-permute-start.8) | collective-permute-done | bytes 786464 | tf_op jit(solution)/shard_map/ppermute | solution.py:16
  108.0 7.7 %collective-permute-done.10 = f32[768,256]{1,0:T(8,128)S(1)} collective-permute-done((f32[768,256]{1,0:T(8,128)S(1)}, f32[768,256]{1,0:T(8,128)S(1)}, u32[]{:S(2)}, u32[]{:S(2)}) %collective-permute-start.10) | collective-permute-done | bytes 786464 | tf_op jit(solution)/shard_map/ppermute | solution.py:16
  115.7 3.2 %collective-permute-start.3 = (f32[512,256]{1,0:T(8,128)S(1)}, f32[512,256]{1,0:T(8,128)S(1)}, u32[]{:S(2)}, u32[]{:S(2)}) collective-permute-start(f32[512,256]{1,0:T(8,128)S(1)} %subtract_select_fusion.4), channel_id=1, source_target_pairs={{0,64},{16,80},{32,96},{48,112},{64,0},{80,16},{96,32},{112,48},{1... | collective-permute-start | bytes 1572872 | tf_op jit(solution)/shard_map/ppermute | solution.py:16
  121.4 65.6 %collective-permute-done.1 = f32[512,256]{1,0:T(8,128)S(1)} collective-permute-done((f32[512,256]{1,0:T(8,128)S(1)}, f32[512,256]{1,0:T(8,128)S(1)}, u32[]{:S(2)}, u32[]{:S(2)}) %collective-permute-start.1) | collective-permute-done | bytes 524320 | tf_op jit(solution)/shard_map/ppermute | solution.py:16
  187.0 3.0 %collective-permute-start.15 = (f32[128,256]{1,0:T(8,128)S(1)}, f32[128,256]{1,0:T(8,128)S(1)}, u32[]{:S(2)}, u32[]{:S(2)}) collective-permute-start(f32[128,256]{1,0:T(8,128)S(1)} %subtract_select_fusion.6), channel_id=1, source_target_pairs={{0,64},{16,80},{32,96},{48,112},{64,0},{80,16},{96,32},{112,48},{1... | collective-permute-start | bytes 393224 | tf_op jit(solution)/shard_map/ppermute | solution.py:16
  190.2 3.1 %collective-permute-start.9 = (f32[768,256]{1,0:T(8,128)S(1)}, f32[768,256]{1,0:T(8,128)S(1)}, u32[]{:S(2)}, u32[]{:S(2)}) collective-permute-start(f32[768,256]{1,0:T(8,128)S(1)} %subtract_select_fusion.3), channel_id=1, source_target_pairs={{0,8},{1,9},{2,10},{3,11},{4,12},{5,13},{6,14},{7,15},{8,0},{9,1},... | collective-permute-start | bytes 2359304 | tf_op jit(solution)/shard_map/ppermute | solution.py:16
  195.4 1.3 select_dynamic-update-slice_fusion
  196.7 12.3 %collective-permute-done.9 = f32[768,256]{1,0:T(8,128)S(1)} collective-permute-done((f32[768,256]{1,0:T(8,128)S(1)}, f32[768,256]{1,0:T(8,128)S(1)}, u32[]{:S(2)}, u32[]{:S(2)}) %collective-permute-start.9) | collective-permute-done | bytes 786464 | tf_op jit(solution)/shard_map/ppermute | solution.py:16
  209.3 2.8 %collective-permute-done.11 = f32[768,256]{1,0:T(8,128)S(1)} collective-permute-done((f32[768,256]{1,0:T(8,128)S(1)}, f32[768,256]{1,0:T(8,128)S(1)}, u32[]{:S(2)}, u32[]{:S(2)}) %collective-permute-start.11) | collective-permute-done | bytes 786464 | tf_op jit(solution)/shard_map/ppermute | solution.py:16
  212.5 3.4 %copy-done = f32[8192,256]{1,0:T(8,128)} copy-done((f32[8192,256]{1,0:T(8,128)}, f32[8192,256]{1,0:T(8,128)S(1)}, u32[]{:S(2)}) %copy-start) | copy-done | bytes 8388632
  (45 shorter events, 16.9 us)
Async XLA Ops:
  4.5 85.2 %collective-permute-start.4 = (f32[2688,256]{1,0:T(8,128)}, f32[2688,256]{1,0:T(8,128)}, u32[]{:S(2)}, u32[]{:S(2)}) collective-permute-start(f32[2688,256]{1,0:T(8,128)} %get-tuple-element.42), channel_id=1, source_target_pairs={{0,64},{16,80},{32,96},{48,112},{64,0},{80,16},{96,32},{112,48},{1... | collective-permute-start | bytes 8257544 | tf_op jit(solution)/shard_map/ppermute | solution.py:16
  10.8 88.7 %collective-permute-start = (f32[512,256]{1,0:T(8,128)}, f32[512,256]{1,0:T(8,128)S(1)}, u32[]{:S(2)}, u32[]{:S(2)}) collective-permute-start(f32[512,256]{1,0:T(8,128)} %get-tuple-element.44), channel_id=1, source_target_pairs={{0,64},{16,80},{32,96},{48,112},{64,0},{80,16},{96,32},{112,48},{1... | collective-permute-start | bytes 1572872 | tf_op jit(solution)/shard_map/ppermute | solution.py:16
  10.8 82.5 %collective-permute-start.6 = (f32[2688,256]{1,0:T(8,128)S(1)}, f32[2688,256]{1,0:T(8,128)}, u32[]{:S(2)}, u32[]{:S(2)}) collective-permute-start(f32[2688,256]{1,0:T(8,128)S(1)} %get-tuple-element.41), channel_id=1, source_target_pairs={{0,8},{1,9},{2,10},{3,11},{4,12},{5,13},{6,14},{7,15},{8,0},{9,1},... | collective-permute-start | bytes 8257544 | tf_op jit(solution)/shard_map/ppermute | solution.py:16
  15.5 67.0 %collective-permute-start.12 = (f32[128,256]{1,0:T(8,128)}, f32[128,256]{1,0:T(8,128)S(1)}, u32[]{:S(2)}, u32[]{:S(2)}) collective-permute-start(f32[128,256]{1,0:T(8,128)} %get-tuple-element.38), channel_id=1, source_target_pairs={{0,64},{16,80},{32,96},{48,112},{64,0},{80,16},{96,32},{112,48},{1... | collective-permute-start | bytes 393224 | tf_op jit(solution)/shard_map/ppermute | solution.py:16
  19.1 66.5 %collective-permute-start.14 = (f32[128,256]{1,0:T(8,128)}, f32[128,256]{1,0:T(8,128)S(1)}, u32[]{:S(2)}, u32[]{:S(2)}) collective-permute-start(f32[128,256]{1,0:T(8,128)} %get-tuple-element.37), channel_id=1, source_target_pairs={{0,8},{1,9},{2,10},{3,11},{4,12},{5,13},{6,14},{7,15},{8,0},{9,1},... | collective-permute-start | bytes 393224 | tf_op jit(solution)/shard_map/ppermute | solution.py:16
  19.6 63.0 %copy-start.1 = (f32[512,256]{1,0:T(8,128)S(1)}, f32[512,256]{1,0:T(8,128)}, u32[]{:S(2)}) copy-start(f32[512,256]{1,0:T(8,128)} %get-tuple-element.43) | copy-start | bytes 1572868
  82.5 18.5 %collective-permute-start.2 = (f32[512,256]{1,0:T(8,128)S(1)}, f32[512,256]{1,0:T(8,128)S(1)}, u32[]{:S(2)}, u32[]{:S(2)}) collective-permute-start(f32[512,256]{1,0:T(8,128)S(1)} %copy-done.1), channel_id=1, source_target_pairs={{0,8},{1,9},{2,10},{3,11},{4,12},{5,13},{6,14},{7,15},{8,0},{9,1},... | collective-permute-start | bytes 1572872 | tf_op jit(solution)/shard_map/ppermute | solution.py:16
  85.6 21.9 %collective-permute-start.8 = (f32[768,256]{1,0:T(8,128)S(1)}, f32[768,256]{1,0:T(8,128)S(1)}, u32[]{:S(2)}, u32[]{:S(2)}) collective-permute-start(f32[768,256]{1,0:T(8,128)S(1)} %get-tuple-element.40), channel_id=1, source_target_pairs={{0,64},{16,80},{32,96},{48,112},{64,0},{80,16},{96,32},{112,48},{1... | collective-permute-start | bytes 2359304 | tf_op jit(solution)/shard_map/ppermute | solution.py:16
  89.7 26.0 %collective-permute-start.10 = (f32[768,256]{1,0:T(8,128)S(1)}, f32[768,256]{1,0:T(8,128)S(1)}, u32[]{:S(2)}, u32[]{:S(2)}) collective-permute-start(f32[768,256]{1,0:T(8,128)S(1)} %get-tuple-element.39), channel_id=1, source_target_pairs={{0,8},{1,9},{2,10},{3,11},{4,12},{5,13},{6,14},{7,15},{8,0},{9,1},... | collective-permute-start | bytes 2359304 | tf_op jit(solution)/shard_map/ppermute | solution.py:16
  93.3 100.2 %collective-permute-start.5 = (f32[2688,256]{1,0:T(8,128)S(1)}, f32[2688,256]{1,0:T(8,128)S(1)}, u32[]{:S(2)}, u32[]{:S(2)}) collective-permute-start(f32[2688,256]{1,0:T(8,128)S(1)} %subtract_select_fusion.1), channel_id=1, source_target_pairs={{0,8},{1,9},{2,10},{3,11},{4,12},{5,13},{6,14},{7,15},{8,0},{9,1},... | collective-permute-start | bytes 8257544 | tf_op jit(solution)/shard_map/ppermute | solution.py:16
  96.4 93.6 %slice-start = ((s8[8388608]{0:T(1024)(128)(4,1)}), s8[4194304]{0:T(1024)(128)(4,1)S(1)}, s32[]{:S(2)}) async-start(s8[8388608]{0:T(1024)(128)(4,1)} %bitcast.2), calls=%async_computation | async-start | bytes 8388608
  99.5 90.4 %slice-start.1 = ((s8[8388608]{0:T(1024)(128)(4,1)}), s8[4194304]{0:T(1024)(128)(4,1)S(1)}, s32[]{:S(2)}) async-start(s8[8388608]{0:T(1024)(128)(4,1)} %bitcast.2), calls=%async_computation.1 | async-start | bytes 8388608
  99.6 95.8 %collective-permute-start.7 = (f32[2688,256]{1,0:T(8,128)S(1)}, f32[2688,256]{1,0:T(8,128)S(1)}, u32[]{:S(2)}, u32[]{:S(2)}) collective-permute-start(f32[2688,256]{1,0:T(8,128)S(1)} %subtract_select_fusion), channel_id=1, source_target_pairs={{0,64},{16,80},{32,96},{48,112},{64,0},{80,16},{96,32},{112,48},{1... | collective-permute-start | bytes 8257544 | tf_op jit(solution)/shard_map/ppermute | solution.py:16
  101.0 111.3 %collective-permute-start.13 = (f32[128,256]{1,0:T(8,128)S(1)}, f32[128,256]{1,0:T(8,128)S(1)}, u32[]{:S(2)}, u32[]{:S(2)}) collective-permute-start(f32[128,256]{1,0:T(8,128)S(1)} %subtract_select_fusion.7), channel_id=1, source_target_pairs={{0,8},{1,9},{2,10},{3,11},{4,12},{5,13},{6,14},{7,15},{8,0},{9,1},... | collective-permute-start | bytes 393224 | tf_op jit(solution)/shard_map/ppermute | solution.py:16
  107.5 79.5 %collective-permute-start.1 = (f32[512,256]{1,0:T(8,128)S(1)}, f32[512,256]{1,0:T(8,128)S(1)}, u32[]{:S(2)}, u32[]{:S(2)}) collective-permute-start(f32[512,256]{1,0:T(8,128)S(1)} %subtract_select_fusion.5), channel_id=1, source_target_pairs={{0,8},{1,9},{2,10},{3,11},{4,12},{5,13},{6,14},{7,15},{8,0},{9,1},... | collective-permute-start | bytes 1572872 | tf_op jit(solution)/shard_map/ppermute | solution.py:16
  115.7 74.5 %collective-permute-start.3 = (f32[512,256]{1,0:T(8,128)S(1)}, f32[512,256]{1,0:T(8,128)S(1)}, u32[]{:S(2)}, u32[]{:S(2)}) collective-permute-start(f32[512,256]{1,0:T(8,128)S(1)} %subtract_select_fusion.4), channel_id=1, source_target_pairs={{0,64},{16,80},{32,96},{48,112},{64,0},{80,16},{96,32},{112,48},{1... | collective-permute-start | bytes 1572872 | tf_op jit(solution)/shard_map/ppermute | solution.py:16
  187.0 25.5 %collective-permute-start.15 = (f32[128,256]{1,0:T(8,128)S(1)}, f32[128,256]{1,0:T(8,128)S(1)}, u32[]{:S(2)}, u32[]{:S(2)}) collective-permute-start(f32[128,256]{1,0:T(8,128)S(1)} %subtract_select_fusion.6), channel_id=1, source_target_pairs={{0,64},{16,80},{32,96},{48,112},{64,0},{80,16},{96,32},{112,48},{1... | collective-permute-start | bytes 393224 | tf_op jit(solution)/shard_map/ppermute | solution.py:16
  190.2 18.9 %collective-permute-start.9 = (f32[768,256]{1,0:T(8,128)S(1)}, f32[768,256]{1,0:T(8,128)S(1)}, u32[]{:S(2)}, u32[]{:S(2)}) collective-permute-start(f32[768,256]{1,0:T(8,128)S(1)} %subtract_select_fusion.3), channel_id=1, source_target_pairs={{0,8},{1,9},{2,10},{3,11},{4,12},{5,13},{6,14},{7,15},{8,0},{9,1},... | collective-permute-start | bytes 2359304 | tf_op jit(solution)/shard_map/ppermute | solution.py:16
  193.5 18.6 %collective-permute-start.11 = (f32[768,256]{1,0:T(8,128)S(1)}, f32[768,256]{1,0:T(8,128)S(1)}, u32[]{:S(2)}, u32[]{:S(2)}) collective-permute-start(f32[768,256]{1,0:T(8,128)S(1)} %subtract_select_fusion.2), channel_id=1, source_target_pairs={{0,64},{16,80},{32,96},{48,112},{64,0},{80,16},{96,32},{112,48},{1... | collective-permute-start | bytes 2359304 | tf_op jit(solution)/shard_map/ppermute | solution.py:16
  212.4 3.4 %copy-start = (f32[8192,256]{1,0:T(8,128)}, f32[8192,256]{1,0:T(8,128)S(1)}, u32[]{:S(2)}) copy-start(f32[8192,256]{1,0:T(8,128)S(1)} %select_dynamic-update-slice_fusion.7) | copy-start | bytes 25165828

commit v3 on v2

--- a/solution.py
+++ b/solution.py
@@ -8,7 +8,7 @@
 
 N = 65536
 W = 2048
-SIZES = (512, 2688, 768, 128)
+SIZES = (512, 2688, 704, 192)
 
 
 def from_partner(block, axis):
@@ -27,6 +27,37 @@
 def copy_rows(x, start, size):
     (x,) = kept_apart(x)
     return lax.slice_in_dim(x, start, start + size)
+
+
+def copy_first(x, starts, size):
+    pieces = 4
+    step = size // pieces
+
+    def kernel(x_ref, *refs):
+        out_refs, sems = refs[:-1], refs[-1]
+        copies = []
+        for p in range(pieces):
+            for k, (start, out_ref) in enumerate(zip(starts, out_refs)):
+                copies.append(
+                    pltpu.make_async_copy(
+                        x_ref.at[pl.ds(start + p * step, step), :],
+                        out_ref.at[pl.ds(p * step, step), :],
+                        sems.at[k, p],
+                    )
+                )
+        for copy in copies:
+            copy.start()
+        for copy in copies:
+            copy.wait()
+
+    hbm = pl.BlockSpec(memory_space=pltpu.HBM)
+    return pl.pallas_call(
+        kernel,
+        in_specs=[hbm],
+        out_specs=[hbm] * len(starts),
+        out_shape=[jax.ShapeDtypeStruct((size, x.shape[1]), x.dtype)] * len(starts),
+        scratch_shapes=[pltpu.SemaphoreType.DMA((len(starts), pieces))],
+    )(x)
 
 
 def mix_rows(x, partner, start, axis):
@@ -70,8 +101,9 @@
         start += size
 
     theirs = []
-    for start, size, first, _ in parts:
-        block = copy_rows(slab_pair, start, size)
+    firsts = copy_first(slab_pair, [part[0] for part in parts[:2]], SIZES[0])
+    for j, (start, size, first, _) in enumerate(parts):
+        block = firsts[j] if j < 2 else copy_rows(slab_pair, start, size)
         theirs.append(from_partner(block, first))
 
     at = lax.axis_index("col") * local_cols % W
@@ -86,9 +118,14 @@
         acrosses.append(from_partner(mixes[j], second))
 
     out = unwritten(slab_pair.shape, slab_pair.dtype)
-    for j, (start, _, _, axis) in enumerate(parts):
+    for j in finish_order(len(parts)):
+        start, _, _, axis = parts[j]
         out = finish_rows(out, mixes[j], acrosses[j], butterfly_scale, col_scale, start, axis)
     return out
+
+
+def finish_order(n):
+    return [j ^ 1 for j in range(n)]
 
 
 def solution(mesh):

time: 217 us -> 239 us (1.10)
  Pallas kernels: 0.01 us -> 32.9 us
  waiting for transfers between devices: 133 us -> 119 us
  local copies, waits for them, and re-layouts: 17 us -> 12 us
  starting transfers between devices: 32.6 us -> 37.2 us
  blocking collectives: 16.9 us -> 20 us
    pallas_call x0 -> x1, Pallas kernels: none -> 32.9 us  [copy_first(): pl.pallas_call(kernel, in_specs=[hbm], out_specs=[hbm] * len(starts), out...]
    ppermute x16, waiting for transfers between devices: 133 us -> 119 us  [from_partner(): lax.ppermute(block, axis, [(i, i ^ count // 2) for i in range(count)])]
    ppermute x16, starting transfers between devices: 32.6 us -> 37.2 us  [from_partner(): lax.ppermute(block, axis, [(i, i ^ count // 2) for i in range(count)])]
    all_gather x1, blocking collectives: 16.9 us -> 20 us  [per_device(): pieces = lax.all_gather(piece, 'row', axis=0)]
    slice x4, local copies, waits for them, and re-layouts: 2.86 us -> 0.08 us  [finish_rows(): both = both * (row_scale[start:start + size, None] * col_scale)]
    slice x4 -> x3, local copies, waits for them, and re-layouts: 9.98 us -> 7.72 us  [copy_rows(): return lax.slice_in_dim(x, start, start + size)]
  transfers between devices with their start and end apart: 16 -> 16, of which waited for: 6 -> 6; matrix products, arithmetic and copies ran while one was open for 12% -> 8% of each run, Pallas kernels for 0% -> 14%
where the time goes in v3:
time: 239 us; the launch traced here: 238 us
  waiting for transfers between devices  119 us (50%)
  starting transfers between devices  37.2 us (16%)
  Pallas kernels  32.9 us (14%)
  blocking collectives  20 us (8%)
  other arithmetic  17.3 us (7%)
  local copies, waits for them, and re-layouts  12 us (5%)
    ppermute x16, waiting for transfers between devices, from_partner(): lax.ppermute(block, axis, [(i, i ^ count // 2) for i in range(count)])  119 us
    ppermute x16, starting transfers between devices, from_partner(): lax.ppermute(block, axis, [(i, i ^ count // 2) for i in range(count)])  37.2 us
    pallas_call x1, Pallas kernels, copy_first(): pl.pallas_call(kernel, in_specs=[hbm], out_specs=[hbm] * len(starts), out...  32.9 us
    all_gather x1, blocking collectives, per_device(): pieces = lax.all_gather(piece, 'row', axis=0)  20 us
    select_n x8, other arithmetic, mix_rows(): return jnp.where(in_first_half(axis), partner + block, partner - block)  12.9 us
    slice x3, local copies, waits for them, and re-layouts, copy_rows(): return lax.slice_in_dim(x, start, start + size)  7.72 us
  transfers between devices with their start and end apart: 16, of which 6 were waited for; matrix products, arithmetic and copies ran while one was open for 8% of the time, Pallas kernels for 14%

profile of v3, /device:TPU:0, one launch (start us, length us, event | category | flops | bytes accessed | tf_op | source)
XLA Modules:
  0.0 238.4 jit_solution(17690636887149522511)
XLA Ops:
  0.0 4.5 %fusion.11 = (f32[2688,256]{1,0:T(8,128)S(1)}, f32[2688,256]{1,0:T(8,128)}) fusion(f32[8192,256]{1,0:T(8,128)} %x_ref.1), kind=kLoop, calls=%fused_computation.32 | loop fusion | bytes 11010048 | tf_op jit(solution)/shard_map/slice | solution.py:29
  4.5 3.1 %collective-permute-start.4 = (f32[2688,256]{1,0:T(8,128)}, f32[2688,256]{1,0:T(8,128)}, u32[]{:S(2)}, u32[]{:S(2)}) collective-permute-start(f32[2688,256]{1,0:T(8,128)} %get-tuple-element.46), channel_id=1, source_target_pairs={{0,8},{1,9},{2,10},{3,11},{4,12},{5,13},{6,14},{7,15},{8,0},{9,1},... | collective-permute-start | bytes 8257544 | tf_op jit(solution)/shard_map/ppermute | solution.py:16
  7.6 32.9 %shard_map.29 = (f32[512,256]{1,0:T(8,128)}, f32[512,256]{1,0:T(8,128)}) custom-call(f32[8192,256]{1,0:T(8,128)} %x_ref.1), custom_call_target="tpu_custom_call" | custom-call | tf_op jit(solution)/shard_map/pallas_call | solution.py:54
  41.0 4.0 %collective-permute-start.6 = (f32[2688,256]{1,0:T(8,128)S(1)}, f32[2688,256]{1,0:T(8,128)}, u32[]{:S(2)}, u32[]{:S(2)}) collective-permute-start(f32[2688,256]{1,0:T(8,128)S(1)} %get-tuple-element.45), channel_id=1, source_target_pairs={{0,64},{16,80},{32,96},{48,112},{64,0},{80,16},{96,32},{112,48},{1... | collective-permute-start | bytes 8257544 | tf_op jit(solution)/shard_map/ppermute | solution.py:16
  45.0 1.8 fusion.9
  46.8 3.0 %collective-permute-start.12 = (f32[192,256]{1,0:T(8,128)}, f32[192,256]{1,0:T(8,128)}, u32[]{:S(2)}, u32[]{:S(2)}) collective-permute-start(f32[192,256]{1,0:T(8,128)} %get-tuple-element.42), channel_id=1, source_target_pairs={{0,8},{1,9},{2,10},{3,11},{4,12},{5,13},{6,14},{7,15},{8,0},{9,1},... | collective-permute-start | bytes 589832 | tf_op jit(solution)/shard_map/ppermute | solution.py:16
  50.7 20.0 %all-gather.1 = f32[8,1,256]{2,1,0:T(1,128)S(1)} all-gather(f32[1,1,256]{2,1,0:T(1,128)S(1)} %bitcast.12), channel_id=2, replica_groups=mesh['row'=8,'col'=16] {'row'}, dimensions={0}, use_global_device_ids=true | all-gather | bytes 9216 | tf_op jit(solution)/shard_map/all_gather | solution.py:111
  72.2 10.8 %collective-permute-done.12 = f32[192,256]{1,0:T(8,128)} collective-permute-done((f32[192,256]{1,0:T(8,128)}, f32[192,256]{1,0:T(8,128)}, u32[]{:S(2)}, u32[]{:S(2)}) %collective-permute-start.12) | collective-permute-done | bytes 196640 | tf_op jit(solution)/shard_map/ppermute | solution.py:16
  83.1 4.1 %collective-permute-start.2 = (f32[512,256]{1,0:T(8,128)S(1)}, f32[512,256]{1,0:T(8,128)S(1)}, u32[]{:S(2)}, u32[]{:S(2)}) collective-permute-start(f32[512,256]{1,0:T(8,128)S(1)} %copy-done.2), channel_id=1, source_target_pairs={{0,64},{16,80},{32,96},{48,112},{64,0},{80,16},{96,32},{112,48},{1... | collective-permute-start | bytes 1572872 | tf_op jit(solution)/shard_map/ppermute | solution.py:16
  87.2 22.7 %collective-permute-done.14 = f32[192,256]{1,0:T(8,128)S(1)} collective-permute-done((f32[192,256]{1,0:T(8,128)}, f32[192,256]{1,0:T(8,128)S(1)}, u32[]{:S(2)}, u32[]{:S(2)}) %collective-permute-start.14) | collective-permute-done | bytes 196640 | tf_op jit(solution)/shard_map/ppermute | solution.py:16
  109.9 3.0 %collective-permute-start.8 = (f32[704,256]{1,0:T(8,128)S(1)}, f32[704,256]{1,0:T(8,128)S(1)}, u32[]{:S(2)}, u32[]{:S(2)}) collective-permute-start(f32[704,256]{1,0:T(8,128)S(1)} %get-tuple-element.44), channel_id=1, source_target_pairs={{0,8},{1,9},{2,10},{3,11},{4,12},{5,13},{6,14},{7,15},{8,0},{9,1},... | collective-permute-start | bytes 2162696 | tf_op jit(solution)/shard_map/ppermute | solution.py:16
  114.0 3.6 %collective-permute-start.10 = (f32[704,256]{1,0:T(8,128)S(1)}, f32[704,256]{1,0:T(8,128)S(1)}, u32[]{:S(2)}, u32[]{:S(2)}) collective-permute-start(f32[704,256]{1,0:T(8,128)S(1)} %get-tuple-element.43), channel_id=1, source_target_pairs={{0,64},{16,80},{32,96},{48,112},{64,0},{80,16},{96,32},{112,48},{1... | collective-permute-start | bytes 2162696 | tf_op jit(solution)/shard_map/ppermute | solution.py:16
  117.6 3.1 %subtract_select_fusion.1 = f32[2688,256]{1,0:T(8,128)S(1)} fusion(f32[2688,256]{1,0:T(8,128)} %collective-permute-done.4, f32[8192,256]{1,0:T(8,128)} %x_ref.1, pred[]{:T(512)S(6)} %lt.16), kind=kLoop, calls=%fused_computation.3 | loop fusion | flops 2064384 | bytes 8257537 | tf_op jit(solution)/shard_map/jit(_where)/select_n | solution.py:66
  120.8 3.1 %subtract_select_fusion = f32[2688,256]{1,0:T(8,128)S(1)} fusion(f32[2688,256]{1,0:T(8,128)} %collective-permute-done.6, f32[8192,256]{1,0:T(8,128)} %x_ref.1, pred[]{:T(512)S(6)} %lt.15), kind=kLoop, calls=%fused_computation.1 | loop fusion | flops 2064384 | bytes 8257537 | tf_op jit(solution)/shard_map/jit(_where)/select_n | solution.py:66
  125.5 3.4 %collective-permute-start.13 = (f32[192,256]{1,0:T(8,128)S(1)}, f32[192,256]{1,0:T(8,128)S(1)}, u32[]{:S(2)}, u32[]{:S(2)}) collective-permute-start(f32[192,256]{1,0:T(8,128)S(1)} %subtract_select_fusion.7), channel_id=1, source_target_pairs={{0,64},{16,80},{32,96},{48,112},{64,0},{80,16},{96,32},{112,48},{1... | collective-permute-start | bytes 589832 | tf_op jit(solution)/shard_map/ppermute | solution.py:16
  131.2 1.8 collective-permute-start.1
  133.0 3.6 %collective-permute-done.10 = f32[704,256]{1,0:T(8,128)S(1)} collective-permute-done((f32[704,256]{1,0:T(8,128)S(1)}, f32[704,256]{1,0:T(8,128)S(1)}, u32[]{:S(2)}, u32[]{:S(2)}) %collective-permute-start.10) | collective-permute-done | bytes 720928 | tf_op jit(solution)/shard_map/ppermute | solution.py:16
  136.6 3.0 %collective-permute-start.3 = (f32[512,256]{1,0:T(8,128)S(1)}, f32[512,256]{1,0:T(8,128)S(1)}, u32[]{:S(2)}, u32[]{:S(2)}) collective-permute-start(f32[512,256]{1,0:T(8,128)S(1)} %subtract_select_fusion.4), channel_id=1, source_target_pairs={{0,8},{1,9},{2,10},{3,11},{4,12},{5,13},{6,14},{7,15},{8,0},{9,1},... | collective-permute-start | bytes 1572872 | tf_op jit(solution)/shard_map/ppermute | solution.py:16
  142.0 67.6 %collective-permute-done.1 = f32[512,256]{1,0:T(8,128)S(1)} collective-permute-done((f32[512,256]{1,0:T(8,128)S(1)}, f32[512,256]{1,0:T(8,128)S(1)}, u32[]{:S(2)}, u32[]{:S(2)}) %collective-permute-start.1) | collective-permute-done | bytes 524320 | tf_op jit(solution)/shard_map/ppermute | solution.py:16
  209.6 3.0 %collective-permute-start.15 = (f32[192,256]{1,0:T(8,128)S(1)}, f32[192,256]{1,0:T(8,128)S(1)}, u32[]{:S(2)}, u32[]{:S(2)}) collective-permute-start(f32[192,256]{1,0:T(8,128)S(1)} %subtract_select_fusion.6), channel_id=1, source_target_pairs={{0,8},{1,9},{2,10},{3,11},{4,12},{5,13},{6,14},{7,15},{8,0},{9,1},... | collective-permute-start | bytes 589832 | tf_op jit(solution)/shard_map/ppermute | solution.py:16
  212.8 3.3 %collective-permute-start.9 = (f32[704,256]{1,0:T(8,128)S(1)}, f32[704,256]{1,0:T(8,128)S(1)}, u32[]{:S(2)}, u32[]{:S(2)}) collective-permute-start(f32[704,256]{1,0:T(8,128)S(1)} %subtract_select_fusion.3), channel_id=1, source_target_pairs={{0,64},{16,80},{32,96},{48,112},{64,0},{80,16},{96,32},{112,48},{1... | collective-permute-start | bytes 2162696 | tf_op jit(solution)/shard_map/ppermute | solution.py:16
  219.6 11.3 %collective-permute-done.9 = f32[704,256]{1,0:T(8,128)S(1)} collective-permute-done((f32[704,256]{1,0:T(8,128)S(1)}, f32[704,256]{1,0:T(8,128)S(1)}, u32[]{:S(2)}, u32[]{:S(2)}) %collective-permute-start.9) | collective-permute-done | bytes 720928 | tf_op jit(solution)/shard_map/ppermute | solution.py:16
  231.1 2.7 %collective-permute-done.11 = f32[704,256]{1,0:T(8,128)S(1)} collective-permute-done((f32[704,256]{1,0:T(8,128)S(1)}, f32[704,256]{1,0:T(8,128)S(1)}, u32[]{:S(2)}, u32[]{:S(2)}) %collective-permute-start.11) | collective-permute-done | bytes 720928 | tf_op jit(solution)/shard_map/ppermute | solution.py:16
  234.2 3.4 %copy-done = f32[8192,256]{1,0:T(8,128)} copy-done((f32[8192,256]{1,0:T(8,128)}, f32[8192,256]{1,0:T(8,128)S(1)}, u32[]{:S(2)}) %copy-start) | copy-done | bytes 8388632
  (47 shorter events, 15.2 us)
Async XLA Ops:
  4.5 109.5 %collective-permute-start.4 = (f32[2688,256]{1,0:T(8,128)}, f32[2688,256]{1,0:T(8,128)}, u32[]{:S(2)}, u32[]{:S(2)}) collective-permute-start(f32[2688,256]{1,0:T(8,128)} %get-tuple-element.46), channel_id=1, source_target_pairs={{0,8},{1,9},{2,10},{3,11},{4,12},{5,13},{6,14},{7,15},{8,0},{9,1},... | collective-permute-start | bytes 8257544 | tf_op jit(solution)/shard_map/ppermute | solution.py:16
  40.6 83.4 %collective-permute-start = (f32[512,256]{1,0:T(8,128)}, f32[512,256]{1,0:T(8,128)S(1)}, u32[]{:S(2)}, u32[]{:S(2)}) collective-permute-start(f32[512,256]{1,0:T(8,128)} %get-tuple-element.23), channel_id=1, source_target_pairs={{0,8},{1,9},{2,10},{3,11},{4,12},{5,13},{6,14},{7,15},{8,0},{9,1},... | collective-permute-start | bytes 1572872 | tf_op jit(solution)/shard_map/ppermute | solution.py:16
  41.0 79.7 %collective-permute-start.6 = (f32[2688,256]{1,0:T(8,128)S(1)}, f32[2688,256]{1,0:T(8,128)}, u32[]{:S(2)}, u32[]{:S(2)}) collective-permute-start(f32[2688,256]{1,0:T(8,128)S(1)} %get-tuple-element.45), channel_id=1, source_target_pairs={{0,64},{16,80},{32,96},{48,112},{64,0},{80,16},{96,32},{112,48},{1... | collective-permute-start | bytes 8257544 | tf_op jit(solution)/shard_map/ppermute | solution.py:16
  46.8 36.2 %collective-permute-start.12 = (f32[192,256]{1,0:T(8,128)}, f32[192,256]{1,0:T(8,128)}, u32[]{:S(2)}, u32[]{:S(2)}) collective-permute-start(f32[192,256]{1,0:T(8,128)} %get-tuple-element.42), channel_id=1, source_target_pairs={{0,8},{1,9},{2,10},{3,11},{4,12},{5,13},{6,14},{7,15},{8,0},{9,1},... | collective-permute-start | bytes 589832 | tf_op jit(solution)/shard_map/ppermute | solution.py:16
  49.9 60.0 %collective-permute-start.14 = (f32[192,256]{1,0:T(8,128)}, f32[192,256]{1,0:T(8,128)S(1)}, u32[]{:S(2)}, u32[]{:S(2)}) collective-permute-start(f32[192,256]{1,0:T(8,128)} %get-tuple-element.41), channel_id=1, source_target_pairs={{0,64},{16,80},{32,96},{48,112},{64,0},{80,16},{96,32},{112,48},{1... | collective-permute-start | bytes 589832 | tf_op jit(solution)/shard_map/ppermute | solution.py:16
  49.9 0.8 copy-start.1
  50.6 32.4 %copy-start.2 = (f32[512,256]{1,0:T(8,128)S(1)}, f32[512,256]{1,0:T(8,128)}, u32[]{:S(2)}) copy-start(f32[512,256]{1,0:T(8,128)} %get-tuple-element.26) | copy-start | bytes 1572868
  83.1 42.5 %collective-permute-start.2 = (f32[512,256]{1,0:T(8,128)S(1)}, f32[512,256]{1,0:T(8,128)S(1)}, u32[]{:S(2)}, u32[]{:S(2)}) collective-permute-start(f32[512,256]{1,0:T(8,128)S(1)} %copy-done.2), channel_id=1, source_target_pairs={{0,64},{16,80},{32,96},{48,112},{64,0},{80,16},{96,32},{112,48},{1... | collective-permute-start | bytes 1572872 | tf_op jit(solution)/shard_map/ppermute | solution.py:16
  109.9 21.3 %collective-permute-start.8 = (f32[704,256]{1,0:T(8,128)S(1)}, f32[704,256]{1,0:T(8,128)S(1)}, u32[]{:S(2)}, u32[]{:S(2)}) collective-permute-start(f32[704,256]{1,0:T(8,128)S(1)} %get-tuple-element.44), channel_id=1, source_target_pairs={{0,8},{1,9},{2,10},{3,11},{4,12},{5,13},{6,14},{7,15},{8,0},{9,1},... | collective-permute-start | bytes 2162696 | tf_op jit(solution)/shard_map/ppermute | solution.py:16
  114.0 22.6 %collective-permute-start.10 = (f32[704,256]{1,0:T(8,128)S(1)}, f32[704,256]{1,0:T(8,128)S(1)}, u32[]{:S(2)}, u32[]{:S(2)}) collective-permute-start(f32[704,256]{1,0:T(8,128)S(1)} %get-tuple-element.43), channel_id=1, source_target_pairs={{0,64},{16,80},{32,96},{48,112},{64,0},{80,16},{96,32},{112,48},{1... | collective-permute-start | bytes 2162696 | tf_op jit(solution)/shard_map/ppermute | solution.py:16
  117.6 95.0 %slice-start = ((s8[8388608]{0:T(1024)(128)(4,1)}), s8[4194304]{0:T(1024)(128)(4,1)S(1)}, s32[]{:S(2)}) async-start(s8[8388608]{0:T(1024)(128)(4,1)} %bitcast.2), calls=%async_computation | async-start | bytes 8388608
  120.7 91.9 %slice-start.1 = ((s8[8388608]{0:T(1024)(128)(4,1)}), s8[4194304]{0:T(1024)(128)(4,1)S(1)}, s32[]{:S(2)}) async-start(s8[8388608]{0:T(1024)(128)(4,1)} %bitcast.2), calls=%async_computation.1 | async-start | bytes 8388608
  120.7 95.6 %collective-permute-start.5 = (f32[2688,256]{1,0:T(8,128)S(1)}, f32[2688,256]{1,0:T(8,128)S(1)}, u32[]{:S(2)}, u32[]{:S(2)}) collective-permute-start(f32[2688,256]{1,0:T(8,128)S(1)} %subtract_select_fusion.1), channel_id=1, source_target_pairs={{0,64},{16,80},{32,96},{48,112},{64,0},{80,16},{96,32},{112,48},{1... | collective-permute-start | bytes 8257544 | tf_op jit(solution)/shard_map/ppermute | solution.py:16
  124.0 94.2 %collective-permute-start.7 = (f32[2688,256]{1,0:T(8,128)S(1)}, f32[2688,256]{1,0:T(8,128)S(1)}, u32[]{:S(2)}, u32[]{:S(2)}) collective-permute-start(f32[2688,256]{1,0:T(8,128)S(1)} %subtract_select_fusion), channel_id=1, source_target_pairs={{0,8},{1,9},{2,10},{3,11},{4,12},{5,13},{6,14},{7,15},{8,0},{9,1},... | collective-permute-start | bytes 8257544 | tf_op jit(solution)/shard_map/ppermute | solution.py:16
  125.5 108.5 %collective-permute-start.13 = (f32[192,256]{1,0:T(8,128)S(1)}, f32[192,256]{1,0:T(8,128)S(1)}, u32[]{:S(2)}, u32[]{:S(2)}) collective-permute-start(f32[192,256]{1,0:T(8,128)S(1)} %subtract_select_fusion.7), channel_id=1, source_target_pairs={{0,64},{16,80},{32,96},{48,112},{64,0},{80,16},{96,32},{112,48},{1... | collective-permute-start | bytes 589832 | tf_op jit(solution)/shard_map/ppermute | solution.py:16
  131.2 78.4 %collective-permute-start.1 = (f32[512,256]{1,0:T(8,128)S(1)}, f32[512,256]{1,0:T(8,128)S(1)}, u32[]{:S(2)}, u32[]{:S(2)}) collective-permute-start(f32[512,256]{1,0:T(8,128)S(1)} %subtract_select_fusion.5), channel_id=1, source_target_pairs={{0,64},{16,80},{32,96},{48,112},{64,0},{80,16},{96,32},{112,48},{1... | collective-permute-start | bytes 1572872 | tf_op jit(solution)/shard_map/ppermute | solution.py:16
  136.6 76.2 %collective-permute-start.3 = (f32[512,256]{1,0:T(8,128)S(1)}, f32[512,256]{1,0:T(8,128)S(1)}, u32[]{:S(2)}, u32[]{:S(2)}) collective-permute-start(f32[512,256]{1,0:T(8,128)S(1)} %subtract_select_fusion.4), channel_id=1, source_target_pairs={{0,8},{1,9},{2,10},{3,11},{4,12},{5,13},{6,14},{7,15},{8,0},{9,1},... | collective-permute-start | bytes 1572872 | tf_op jit(solution)/shard_map/ppermute | solution.py:16
  209.6 24.6 %collective-permute-start.15 = (f32[192,256]{1,0:T(8,128)S(1)}, f32[192,256]{1,0:T(8,128)S(1)}, u32[]{:S(2)}, u32[]{:S(2)}) collective-permute-start(f32[192,256]{1,0:T(8,128)S(1)} %subtract_select_fusion.6), channel_id=1, source_target_pairs={{0,8},{1,9},{2,10},{3,11},{4,12},{5,13},{6,14},{7,15},{8,0},{9,1},... | collective-permute-start | bytes 589832 | tf_op jit(solution)/shard_map/ppermute | solution.py:16
  212.8 18.0 %collective-permute-start.9 = (f32[704,256]{1,0:T(8,128)S(1)}, f32[704,256]{1,0:T(8,128)S(1)}, u32[]{:S(2)}, u32[]{:S(2)}) collective-permute-start(f32[704,256]{1,0:T(8,128)S(1)} %subtract_select_fusion.3), channel_id=1, source_target_pairs={{0,64},{16,80},{32,96},{48,112},{64,0},{80,16},{96,32},{112,48},{1... | collective-permute-start | bytes 2162696 | tf_op jit(solution)/shard_map/ppermute | solution.py:16
  216.3 17.5 %collective-permute-start.11 = (f32[704,256]{1,0:T(8,128)S(1)}, f32[704,256]{1,0:T(8,128)S(1)}, u32[]{:S(2)}, u32[]{:S(2)}) collective-permute-start(f32[704,256]{1,0:T(8,128)S(1)} %subtract_select_fusion.2), channel_id=1, source_target_pairs={{0,8},{1,9},{2,10},{3,11},{4,12},{5,13},{6,14},{7,15},{8,0},{9,1},... | collective-permute-start | bytes 2162696 | tf_op jit(solution)/shard_map/ppermute | solution.py:16
  234.2 3.4 %copy-start = (f32[8192,256]{1,0:T(8,128)}, f32[8192,256]{1,0:T(8,128)S(1)}, u32[]{:S(2)}) copy-start(f32[8192,256]{1,0:T(8,128)S(1)} %select_dynamic-update-slice_fusion.7) | copy-start | bytes 25165828

commit v4 on v3

--- a/solution.py
+++ b/solution.py
@@ -50,12 +50,11 @@
         for copy in copies:
             copy.wait()
 
-    hbm = pl.BlockSpec(memory_space=pltpu.HBM)
     return pl.pallas_call(
         kernel,
-        in_specs=[hbm],
-        out_specs=[hbm] * len(starts),
-        out_shape=[jax.ShapeDtypeStruct((size, x.shape[1]), x.dtype)] * len(starts),
+        in_specs=[pl.BlockSpec(memory_space=pltpu.HBM)],
+        out_specs=[pl.BlockSpec(memory_space=pltpu.VMEM)] * len(starts),
+        out_shape=[pltpu.VMEM((size, x.shape[1]), x.dtype)] * len(starts),
         scratch_shapes=[pltpu.SemaphoreType.DMA((len(starts), pieces))],
     )(x)
 
@@ -77,6 +76,46 @@
         out_specs=pl.BlockSpec(memory_space=pltpu.HBM),
         out_shape=jax.ShapeDtypeStruct(shape, dtype),
     )()
+
+
+def factors(row_scale, col_scale, start, size):
+    row_scale, col_scale = kept_apart(row_scale, col_scale)
+    cols = col_scale.shape[0]
+    gap = first_global_col(cols) - lax.axis_index("row") * row_scale.shape[0] - start
+    row = lax.broadcasted_iota(jnp.int32, (size, cols), 0)
+    col = lax.broadcasted_iota(jnp.int32, (size, cols), 1)
+    scales = row_scale[start : start + size, None] * col_scale
+    return jnp.where(row - col >= gap, scales, jnp.float32(0.0))
+
+
+def finish_last(out, mixed, across, factor, start):
+    size, cols = mixed.shape
+    half = size // 2
+
+    def kernel(mixed_ref, across_ref, factor_ref, _, out_ref, done_ref, sems):
+        copies = []
+        for p in range(2):
+            rows = pl.ds(p * half, half)
+            done_ref[rows, :] = (across_ref[rows, :] + mixed_ref[rows, :]) * factor_ref[rows, :]
+            copy = pltpu.make_async_copy(
+                done_ref.at[rows, :], out_ref.at[pl.ds(start + p * half, half), :], sems.at[p]
+            )
+            copy.start()
+            copies.append(copy)
+        for copy in copies:
+            copy.wait()
+
+    vmem = pl.BlockSpec(memory_space=pltpu.VMEM)
+    hbm = pl.BlockSpec(memory_space=pltpu.HBM)
+    held = [pltpu.with_memory_space_constraint(x, pltpu.VMEM) for x in (mixed, across, factor)]
+    return pl.pallas_call(
+        kernel,
+        in_specs=[vmem, vmem, vmem, hbm],
+        out_specs=hbm,
+        out_shape=jax.ShapeDtypeStruct(out.shape, out.dtype),
+        scratch_shapes=[pltpu.VMEM((size, cols), mixed.dtype), pltpu.SemaphoreType.DMA((2,))],
+        input_output_aliases={3: 0},
+    )(*held, out)
 
 
 def finish_rows(out, mixed, across, row_scale, col_scale, start, axis):
@@ -119,7 +158,14 @@
 
     out = unwritten(slab_pair.shape, slab_pair.dtype)
     for j in finish_order(len(parts)):
-        start, _, _, axis = parts[j]
+        start, size, _, axis = parts[j]
+        if j == len(parts) - 2:
+            (mixed,) = kept_apart(mixes[j])
+            mixed = jnp.where(in_first_half(axis), mixed, -mixed)
+            factor = factors(butterfly_scale, col_scale, start, size)
+            mixed, factor = kept_apart(mixed, factor)
+            out = finish_last(out, mixed, acrosses[j], factor, start)
+            continue
         out = finish_rows(out, mixes[j], acrosses[j], butterfly_scale, col_scale, start, axis)
     return out
 

time: 239 us -> 211 us (0.88)
  Pallas kernels: 32.9 us -> 2.05 us
  other arithmetic: 17.3 us -> 22.2 us
  local copies, waits for them, and re-layouts: 12 us -> 8.82 us
  waiting for transfers between devices: 119 us -> 122 us
    pallas_call x1 -> x2, Pallas kernels: 32.9 us -> 2.05 us  [the longest x1 1.35 us: copy_first(): pl.pallas_call(kernel, in_specs=[pl.BlockSpec(memory_space=pltpu.HBM)], o...]
    dynamic_update_slice x8 -> x7, other arithmetic: 4.37 us -> 9.66 us  [finish_rows(): return lax.dynamic_update_slice(out, kept, (start, 0))]
    unnamed x10 -> x2, local copies, waits for them, and re-layouts: 4.15 us -> 0.76 us
    ppermute x16, waiting for transfers between devices: 119 us -> 122 us  [from_partner(): lax.ppermute(block, axis, [(i, i ^ count // 2) for i in range(count)])]
  transfers between devices with their start and end apart: 16 -> 16, of which waited for: 6 -> 4; matrix products, arithmetic and copies ran while one was open for 8% -> 12% of each run, Pallas kernels for 14% -> 1%
where the time goes in v4:
time: 211 us
  waiting for transfers between devices  122 us (58%)
  starting transfers between devices  35.8 us (17%)
  other arithmetic  22.2 us (11%)
  blocking collectives  19.9 us (9%)
  local copies, waits for them, and re-layouts  8.82 us (4%)
    ppermute x16, waiting for transfers between devices, from_partner(): lax.ppermute(block, axis, [(i, i ^ count // 2) for i in range(count)])  122 us
    ppermute x16, starting transfers between devices, from_partner(): lax.ppermute(block, axis, [(i, i ^ count // 2) for i in range(count)])  35.8 us
    all_gather x1, blocking collectives, per_device(): pieces = lax.all_gather(piece, 'row', axis=0)  19.9 us
    select_n x8, other arithmetic, mix_rows(): return jnp.where(in_first_half(axis), partner + block, partner - block)  12.5 us
    dynamic_update_slice x7, other arithmetic, finish_rows(): return lax.dynamic_update_slice(out, kept, (start, 0))  9.66 us
    slice x3, local copies, waits for them, and re-layouts, copy_rows(): return lax.slice_in_dim(x, start, start + size)  7.83 us
  transfers between devices with their start and end apart: 16, of which 4 were waited for; matrix products, arithmetic and copies ran while one was open for 12% of the time, Pallas kernels for 1%

profile of v4, /device:TPU:0, one launch (start us, length us, event | category | flops | bytes accessed | tf_op | source)
XLA Modules:
  0.0 211.0 jit_solution(6429120219895666883)
XLA Ops:
  0.0 5.4 %fusion.11 = (f32[2688,256]{1,0:T(8,128)}, f32[2688,256]{1,0:T(8,128)}) fusion(f32[8192,256]{1,0:T(8,128)} %x_ref.1), kind=kLoop, calls=%fused_computation.33 | loop fusion | bytes 11010048 | tf_op jit(solution)/shard_map/slice | solution.py:29
  5.4 3.1 %collective-permute-start.6 = (f32[2688,256]{1,0:T(8,128)}, f32[2688,256]{1,0:T(8,128)}, u32[]{:S(2)}, u32[]{:S(2)}) collective-permute-start(f32[2688,256]{1,0:T(8,128)} %get-tuple-element.54), channel_id=1, source_target_pairs={{0,8},{1,9},{2,10},{3,11},{4,12},{5,13},{6,14},{7,15},{8,0},{9,1},... | collective-permute-start | bytes 8257544 | tf_op jit(solution)/shard_map/ppermute | solution.py:16
  8.5 1.3 shard_map.29
  10.3 4.0 %collective-permute-start.8 = (f32[2688,256]{1,0:T(8,128)}, f32[2688,256]{1,0:T(8,128)}, u32[]{:S(2)}, u32[]{:S(2)}) collective-permute-start(f32[2688,256]{1,0:T(8,128)} %get-tuple-element.53), channel_id=1, source_target_pairs={{0,64},{16,80},{32,96},{48,112},{64,0},{80,16},{96,32},{112,48},{1... | collective-permute-start | bytes 8257544 | tf_op jit(solution)/shard_map/ppermute | solution.py:16
  15.4 3.1 %collective-permute-start.14 = (f32[192,256]{1,0:T(8,128)S(1)}, f32[192,256]{1,0:T(8,128)S(1)}, u32[]{:S(2)}, u32[]{:S(2)}) collective-permute-start(f32[192,256]{1,0:T(8,128)S(1)} %get-tuple-element.49), channel_id=1, source_target_pairs={{0,8},{1,9},{2,10},{3,11},{4,12},{5,13},{6,14},{7,15},{8,0},{9,1},... | collective-permute-start | bytes 589832 | tf_op jit(solution)/shard_map/ppermute | solution.py:16
  19.4 19.9 %all-gather.1 = f32[8,1,256]{2,1,0:T(1,128)S(1)} all-gather(f32[1,1,256]{2,1,0:T(1,128)S(1)} %bitcast.10), channel_id=2, replica_groups=mesh['row'=8,'col'=16] {'row'}, dimensions={0}, use_global_device_ids=true | all-gather | bytes 9216 | tf_op jit(solution)/shard_map/all_gather | solution.py:150
  39.4 1.4 fusion.10
  40.9 42.9 %collective-permute-done.14 = f32[192,256]{1,0:T(8,128)S(1)} collective-permute-done((f32[192,256]{1,0:T(8,128)S(1)}, f32[192,256]{1,0:T(8,128)S(1)}, u32[]{:S(2)}, u32[]{:S(2)}) %collective-permute-start.14) | collective-permute-done | bytes 196640 | tf_op jit(solution)/shard_map/ppermute | solution.py:16
  83.8 4.1 %collective-permute-start.4 = (f32[512,256]{1,0:T(8,128)S(1)}, f32[512,256]{1,0:T(8,128)S(1)}, u32[]{:S(2)}, u32[]{:S(2)}) collective-permute-start(f32[512,256]{1,0:T(8,128)S(1)} %get-tuple-element.36), channel_id=1, source_target_pairs={{0,64},{16,80},{32,96},{48,112},{64,0},{80,16},{96,32},{112,48},{1... | collective-permute-start | bytes 1572872 | tf_op jit(solution)/shard_map/ppermute | solution.py:16
  87.9 3.0 %collective-permute-start.10 = (f32[704,256]{1,0:T(8,128)S(1)}, f32[704,256]{1,0:T(8,128)S(1)}, u32[]{:S(2)}, u32[]{:S(2)}) collective-permute-start(f32[704,256]{1,0:T(8,128)S(1)} %get-tuple-element.52), channel_id=1, source_target_pairs={{0,8},{1,9},{2,10},{3,11},{4,12},{5,13},{6,14},{7,15},{8,0},{9,1},... | collective-permute-start | bytes 2162696 | tf_op jit(solution)/shard_map/ppermute | solution.py:16
  92.0 3.0 %subtract_select_fusion.1 = f32[2688,256]{1,0:T(8,128)S(1)} fusion(f32[2688,256]{1,0:T(8,128)} %collective-permute-done.6, f32[8192,256]{1,0:T(8,128)} %x_ref.1, pred[]{:T(512)S(6)} %lt.14), kind=kLoop, calls=%fused_computation.3 | loop fusion | flops 2064384 | bytes 8257537 | tf_op jit(solution)/shard_map/jit(_where)/select_n | solution.py:65
  95.0 3.6 %collective-permute-start.7 = (f32[2688,256]{1,0:T(8,128)S(1)}, f32[2688,256]{1,0:T(8,128)S(1)}, u32[]{:S(2)}, u32[]{:S(2)}) collective-permute-start(f32[2688,256]{1,0:T(8,128)S(1)} %subtract_select_fusion.1), channel_id=1, source_target_pairs={{0,64},{16,80},{32,96},{48,112},{64,0},{80,16},{96,32},{112,48},{1... | collective-permute-start | bytes 8257544 | tf_op jit(solution)/shard_map/ppermute | solution.py:16
  98.6 3.0 %subtract_select_fusion = f32[2688,256]{1,0:T(8,128)S(1)} fusion(f32[2688,256]{1,0:T(8,128)} %collective-permute-done.8, f32[8192,256]{1,0:T(8,128)} %x_ref.1, pred[]{:T(512)S(6)} %lt.15), kind=kLoop, calls=%fused_computation.1 | loop fusion | flops 2064384 | bytes 8257537 | tf_op jit(solution)/shard_map/jit(_where)/select_n | solution.py:65
  103.2 3.1 %collective-permute-start.1 = (f32[192,256]{1,0:T(8,128)S(1)}, f32[192,256]{1,0:T(8,128)S(1)}, u32[]{:S(2)}, u32[]{:S(2)}) collective-permute-start(f32[192,256]{1,0:T(8,128)S(1)} %subtract_select_fusion.7), channel_id=1, source_target_pairs={{0,8},{1,9},{2,10},{3,11},{4,12},{5,13},{6,14},{7,15},{8,0},{9,1},... | collective-permute-start | bytes 589832 | tf_op jit(solution)/shard_map/ppermute | solution.py:16
  109.6 6.6 %collective-permute-done.12 = f32[704,256]{1,0:T(8,128)S(1)} collective-permute-done((f32[704,256]{1,0:T(8,128)S(1)}, f32[704,256]{1,0:T(8,128)S(1)}, u32[]{:S(2)}, u32[]{:S(2)}) %collective-permute-start.12) | collective-permute-done | bytes 720928 | tf_op jit(solution)/shard_map/ppermute | solution.py:16
  116.1 3.0 %collective-permute-start.5 = (f32[512,256]{1,0:T(8,128)S(1)}, f32[512,256]{1,0:T(8,128)S(1)}, u32[]{:S(2)}, u32[]{:S(2)}) collective-permute-start(f32[512,256]{1,0:T(8,128)S(1)} %subtract_select_fusion.4), channel_id=1, source_target_pairs={{0,8},{1,9},{2,10},{3,11},{4,12},{5,13},{6,14},{7,15},{8,0},{9,1},... | collective-permute-start | bytes 1572872 | tf_op jit(solution)/shard_map/ppermute | solution.py:16
  119.2 1.2 subtract_select_fusion.3
  120.4 1.2 subtract_select_fusion.2
  121.6 63.1 %collective-permute-done.3 = f32[512,256]{1,0:T(8,128)S(1)} collective-permute-done((f32[512,256]{1,0:T(8,128)S(1)}, f32[512,256]{1,0:T(8,128)S(1)}, u32[]{:S(2)}, u32[]{:S(2)}) %collective-permute-start.3) | collective-permute-done | bytes 524320 | tf_op jit(solution)/shard_map/ppermute | solution.py:16
  184.7 3.2 %collective-permute-start.15 = (f32[192,256]{1,0:T(8,128)S(1)}, f32[192,256]{1,0:T(8,128)S(1)}, u32[]{:S(2)}, u32[]{:S(2)}) collective-permute-start(f32[192,256]{1,0:T(8,128)S(1)} %subtract_select_fusion.6), channel_id=1, source_target_pairs={{0,64},{16,80},{32,96},{48,112},{64,0},{80,16},{96,32},{112,48},{1... | collective-permute-start | bytes 589832 | tf_op jit(solution)/shard_map/ppermute | solution.py:16
  190.1 3.0 %collective-permute-start.13 = (f32[704,256]{1,0:T(8,128)S(1)}, f32[704,256]{1,0:T(8,128)S(1)}, u32[]{:S(2)}, u32[]{:S(2)}) collective-permute-start(f32[704,256]{1,0:T(8,128)S(1)} %subtract_select_fusion.2), channel_id=1, source_target_pairs={{0,8},{1,9},{2,10},{3,11},{4,12},{5,13},{6,14},{7,15},{8,0},{9,1},... | collective-permute-start | bytes 2162696 | tf_op jit(solution)/shard_map/ppermute | solution.py:16
  193.2 2.3 %select_dynamic-update-slice_fusion.1 = f32[8192,256]{1,0:T(8,128)} fusion(f32[8192,256]{1,0:T(8,128)} %select_dynamic-update-slice_fusion.4, f32[2688,256]{1,0:T(8,128)S(1)} %collective-permute-done.7, f32[2688,256]{1,0:T(8,128)S(1)} %subtract_select_fusion.1, f32[256]{0:T(256)S(1)} %bitcast.5, f32[2688]{0:T(1024)S(1)} %get-tuple-element.58, s32[]{:T(128)S(6)} %sub.122, ...), kind=kLoop, calls=%fused_computation.2 | loop fusion | flops 5505024 | bytes 8269317 | tf_op jit(solution)/shard_map/dynamic_update_slice | solution.py:129
  195.5 2.4 %select_dynamic-update-slice_fusion = f32[8192,256]{1,0:T(8,128)} fusion(f32[8192,256]{1,0:T(8,128)} %select_dynamic-update-slice_fusion.1, f32[2688,256]{1,0:T(8,128)S(1)} %collective-permute-done.9, f32[2688,256]{1,0:T(8,128)S(1)} %subtract_select_fusion, f32[2688]{0:T(1024)S(1)} %get-tuple-element.57, s32[]{:T(128)S(6)} %sub.125, f32[256]{0:T(256)S(1)} %bitcast.6, ...), kind=kLoop, calls=%fused_computation | loop fusion | flops 5505024 | bytes 8269317 | tf_op jit(solution)/shard_map/dynamic_update_slice | solution.py:129
  197.9 9.4 %collective-permute-done.11 = f32[704,256]{1,0:T(8,128)S(1)} collective-permute-done((f32[704,256]{1,0:T(8,128)S(1)}, f32[704,256]{1,0:T(8,128)S(1)}, u32[]{:S(2)}, u32[]{:S(2)}) %collective-permute-start.11) | collective-permute-done | bytes 720928 | tf_op jit(solution)/shard_map/ppermute | solution.py:16
  (41 shorter events, 14.5 us)
Async XLA Ops:
  5.4 86.6 %collective-permute-start.6 = (f32[2688,256]{1,0:T(8,128)}, f32[2688,256]{1,0:T(8,128)}, u32[]{:S(2)}, u32[]{:S(2)}) collective-permute-start(f32[2688,256]{1,0:T(8,128)} %get-tuple-element.54), channel_id=1, source_target_pairs={{0,8},{1,9},{2,10},{3,11},{4,12},{5,13},{6,14},{7,15},{8,0},{9,1},... | collective-permute-start | bytes 8257544 | tf_op jit(solution)/shard_map/ppermute | solution.py:16
  9.9 91.7 %collective-permute-start.2 = (f32[512,256]{1,0:T(8,128)S(1)}, f32[512,256]{1,0:T(8,128)S(1)}, u32[]{:S(2)}, u32[]{:S(2)}) collective-permute-start(f32[512,256]{1,0:T(8,128)S(1)} %get-tuple-element.33), channel_id=1, source_target_pairs={{0,8},{1,9},{2,10},{3,11},{4,12},{5,13},{6,14},{7,15},{8,0},{9,1},... | collective-permute-start | bytes 1572872 | tf_op jit(solution)/shard_map/ppermute | solution.py:16
  10.3 84.7 %collective-permute-start.8 = (f32[2688,256]{1,0:T(8,128)}, f32[2688,256]{1,0:T(8,128)}, u32[]{:S(2)}, u32[]{:S(2)}) collective-permute-start(f32[2688,256]{1,0:T(8,128)} %get-tuple-element.53), channel_id=1, source_target_pairs={{0,64},{16,80},{32,96},{48,112},{64,0},{80,16},{96,32},{112,48},{1... | collective-permute-start | bytes 8257544 | tf_op jit(solution)/shard_map/ppermute | solution.py:16
  15.4 68.5 %collective-permute-start.14 = (f32[192,256]{1,0:T(8,128)S(1)}, f32[192,256]{1,0:T(8,128)S(1)}, u32[]{:S(2)}, u32[]{:S(2)}) collective-permute-start(f32[192,256]{1,0:T(8,128)S(1)} %get-tuple-element.49), channel_id=1, source_target_pairs={{0,8},{1,9},{2,10},{3,11},{4,12},{5,13},{6,14},{7,15},{8,0},{9,1},... | collective-permute-start | bytes 589832 | tf_op jit(solution)/shard_map/ppermute | solution.py:16
  18.5 69.5 %collective-permute-start = (f32[192,256]{1,0:T(8,128)S(1)}, f32[192,256]{1,0:T(8,128)S(1)}, u32[]{:S(2)}, u32[]{:S(2)}) collective-permute-start(f32[192,256]{1,0:T(8,128)S(1)} %get-tuple-element.50), channel_id=1, source_target_pairs={{0,64},{16,80},{32,96},{48,112},{64,0},{80,16},{96,32},{112,48},{1... | collective-permute-start | bytes 589832 | tf_op jit(solution)/shard_map/ppermute | solution.py:16
  18.5 0.8 copy-start
  83.8 19.3 %collective-permute-start.4 = (f32[512,256]{1,0:T(8,128)S(1)}, f32[512,256]{1,0:T(8,128)S(1)}, u32[]{:S(2)}, u32[]{:S(2)}) collective-permute-start(f32[512,256]{1,0:T(8,128)S(1)} %get-tuple-element.36), channel_id=1, source_target_pairs={{0,64},{16,80},{32,96},{48,112},{64,0},{80,16},{96,32},{112,48},{1... | collective-permute-start | bytes 1572872 | tf_op jit(solution)/shard_map/ppermute | solution.py:16
  87.9 20.6 %collective-permute-start.10 = (f32[704,256]{1,0:T(8,128)S(1)}, f32[704,256]{1,0:T(8,128)S(1)}, u32[]{:S(2)}, u32[]{:S(2)}) collective-permute-start(f32[704,256]{1,0:T(8,128)S(1)} %get-tuple-element.52), channel_id=1, source_target_pairs={{0,8},{1,9},{2,10},{3,11},{4,12},{5,13},{6,14},{7,15},{8,0},{9,1},... | collective-permute-start | bytes 2162696 | tf_op jit(solution)/shard_map/ppermute | solution.py:16
  91.9 24.2 %collective-permute-start.12 = (f32[704,256]{1,0:T(8,128)S(1)}, f32[704,256]{1,0:T(8,128)S(1)}, u32[]{:S(2)}, u32[]{:S(2)}) collective-permute-start(f32[704,256]{1,0:T(8,128)S(1)} %get-tuple-element.51), channel_id=1, source_target_pairs={{0,64},{16,80},{32,96},{48,112},{64,0},{80,16},{96,32},{112,48},{1... | collective-permute-start | bytes 2162696 | tf_op jit(solution)/shard_map/ppermute | solution.py:16
  95.0 95.1 %collective-permute-start.7 = (f32[2688,256]{1,0:T(8,128)S(1)}, f32[2688,256]{1,0:T(8,128)S(1)}, u32[]{:S(2)}, u32[]{:S(2)}) collective-permute-start(f32[2688,256]{1,0:T(8,128)S(1)} %subtract_select_fusion.1), channel_id=1, source_target_pairs={{0,64},{16,80},{32,96},{48,112},{64,0},{80,16},{96,32},{112,48},{1... | collective-permute-start | bytes 8257544 | tf_op jit(solution)/shard_map/ppermute | solution.py:16
  101.6 93.9 %collective-permute-start.9 = (f32[2688,256]{1,0:T(8,128)S(1)}, f32[2688,256]{1,0:T(8,128)S(1)}, u32[]{:S(2)}, u32[]{:S(2)}) collective-permute-start(f32[2688,256]{1,0:T(8,128)S(1)} %subtract_select_fusion), channel_id=1, source_target_pairs={{0,8},{1,9},{2,10},{3,11},{4,12},{5,13},{6,14},{7,15},{8,0},{9,1},... | collective-permute-start | bytes 8257544 | tf_op jit(solution)/shard_map/ppermute | solution.py:16
  103.2 107.1 %collective-permute-start.1 = (f32[192,256]{1,0:T(8,128)S(1)}, f32[192,256]{1,0:T(8,128)S(1)}, u32[]{:S(2)}, u32[]{:S(2)}) collective-permute-start(f32[192,256]{1,0:T(8,128)S(1)} %subtract_select_fusion.7), channel_id=1, source_target_pairs={{0,8},{1,9},{2,10},{3,11},{4,12},{5,13},{6,14},{7,15},{8,0},{9,1},... | collective-permute-start | bytes 589832 | tf_op jit(solution)/shard_map/ppermute | solution.py:16
  108.5 76.2 %collective-permute-start.3 = (f32[512,256]{1,0:T(8,128)S(1)}, f32[512,256]{1,0:T(8,128)S(1)}, u32[]{:S(2)}, u32[]{:S(2)}) collective-permute-start(f32[512,256]{1,0:T(8,128)S(1)} %subtract_select_fusion.5), channel_id=1, source_target_pairs={{0,64},{16,80},{32,96},{48,112},{64,0},{80,16},{96,32},{112,48},{1... | collective-permute-start | bytes 1572872 | tf_op jit(solution)/shard_map/ppermute | solution.py:16
  116.1 72.7 %collective-permute-start.5 = (f32[512,256]{1,0:T(8,128)S(1)}, f32[512,256]{1,0:T(8,128)S(1)}, u32[]{:S(2)}, u32[]{:S(2)}) collective-permute-start(f32[512,256]{1,0:T(8,128)S(1)} %subtract_select_fusion.4), channel_id=1, source_target_pairs={{0,8},{1,9},{2,10},{3,11},{4,12},{5,13},{6,14},{7,15},{8,0},{9,1},... | collective-permute-start | bytes 1572872 | tf_op jit(solution)/shard_map/ppermute | solution.py:16
  184.7 24.8 %collective-permute-start.15 = (f32[192,256]{1,0:T(8,128)S(1)}, f32[192,256]{1,0:T(8,128)S(1)}, u32[]{:S(2)}, u32[]{:S(2)}) collective-permute-start(f32[192,256]{1,0:T(8,128)S(1)} %subtract_select_fusion.6), channel_id=1, source_target_pairs={{0,64},{16,80},{32,96},{48,112},{64,0},{80,16},{96,32},{112,48},{1... | collective-permute-start | bytes 589832 | tf_op jit(solution)/shard_map/ppermute | solution.py:16
  188.9 18.4 %collective-permute-start.11 = (f32[704,256]{1,0:T(8,128)S(1)}, f32[704,256]{1,0:T(8,128)S(1)}, u32[]{:S(2)}, u32[]{:S(2)}) collective-permute-start(f32[704,256]{1,0:T(8,128)S(1)} %subtract_select_fusion.3), channel_id=1, source_target_pairs={{0,64},{16,80},{32,96},{48,112},{64,0},{80,16},{96,32},{112,48},{1... | collective-permute-start | bytes 2162696 | tf_op jit(solution)/shard_map/ppermute | solution.py:16
  190.1 18.2 %collective-permute-start.13 = (f32[704,256]{1,0:T(8,128)S(1)}, f32[704,256]{1,0:T(8,128)S(1)}, u32[]{:S(2)}, u32[]{:S(2)}) collective-permute-start(f32[704,256]{1,0:T(8,128)S(1)} %subtract_select_fusion.2), channel_id=1, source_target_pairs={{0,8},{1,9},{2,10},{3,11},{4,12},{5,13},{6,14},{7,15},{8,0},{9,1},... | collective-permute-start | bytes 2162696 | tf_op jit(solution)/shard_map/ppermute | solution.py:16

commit v5 on v4

--- a/solution.py
+++ b/solution.py
@@ -8,12 +8,26 @@
 
 N = 65536
 W = 2048
-SIZES = (512, 2688, 704, 192)
+SIZES = (512, 2752, 672, 160)
+LAST = 2
 
 
 def from_partner(block, axis):
     count = lax.axis_size(axis)
     return lax.ppermute(block, axis, [(i, i ^ count // 2) for i in range(count)])
+
+
+def from_needed_partner(block, axis):
+    if axis == "row":
+        return from_partner(block, axis)
+    rows, cols = lax.axis_size("row"), lax.axis_size("col")
+    pairs = [
+        (r * cols + c, r * cols + (c ^ cols // 2))
+        for r in range(rows)
+        for c in range(cols)
+        if r >= rows // 2 or c >= cols // 2
+    ]
+    return lax.ppermute(block, ("row", "col"), pairs)
 
 
 def in_first_half(axis):
@@ -154,12 +168,12 @@
     mixes, acrosses = [], []
     for j, (start, size, first, second) in enumerate(parts):
         mixes.append(mix_rows(slab_pair, theirs[j], start, first))
-        acrosses.append(from_partner(mixes[j], second))
+        acrosses.append(from_needed_partner(mixes[j], second))
 
     out = unwritten(slab_pair.shape, slab_pair.dtype)
     for j in finish_order(len(parts)):
         start, size, _, axis = parts[j]
-        if j == len(parts) - 2:
+        if j >= len(parts) - LAST:
             (mixed,) = kept_apart(mixes[j])
             mixed = jnp.where(in_first_half(axis), mixed, -mixed)
             factor = factors(butterfly_scale, col_scale, start, size)

time: 211 us -> 218 us (1.033)
  waiting for transfers between devices: 122 us -> 130 us
    ppermute x16 -> x12, starting transfers between devices: 35.8 us -> 30.7 us  [from_partner(): lax.ppermute(block, axis, [(i, i ^ count // 2) for i in range(count)])]
    ppermute x0 -> x4, starting transfers between devices: none -> 5.13 us  [from_needed_partner(): return lax.ppermute(block, ('row', 'col'), pairs)]
    ppermute x0 -> x4, waiting for transfers between devices: none -> 4.37 us  [from_needed_partner(): return lax.ppermute(block, ('row', 'col'), pairs)]
    ppermute x16 -> x12, waiting for transfers between devices: 122 us -> 125 us  [from_partner(): lax.ppermute(block, axis, [(i, i ^ count // 2) for i in range(count)])]
    dynamic_update_slice x7 -> x6, other arithmetic: 9.66 us -> 8.94 us  [finish_rows(): return lax.dynamic_update_slice(out, kept, (start, 0))]
  transfers between devices with their start and end apart: 16 -> 16, of which waited for: 4 -> 6; matrix products, arithmetic and copies ran while one was open for 12% -> 11% of each run, Pallas kernels for 1% -> 1%
where the time goes in v5:
time: 218 us
  waiting for transfers between devices  130 us (60%)
  starting transfers between devices  35.8 us (16%)
  other arithmetic  21.6 us (10%)
  blocking collectives  19.8 us (9%)
  local copies, waits for them, and re-layouts  8.12 us (4%)
  Pallas kernels  2.74 us (1%)
    ppermute x12, waiting for transfers between devices, from_partner(): lax.ppermute(block, axis, [(i, i ^ count // 2) for i in range(count)])  125 us
    ppermute x12, starting transfers between devices, from_partner(): lax.ppermute(block, axis, [(i, i ^ count // 2) for i in range(count)])  30.7 us
    all_gather x1, blocking collectives, per_device(): pieces = lax.all_gather(piece, 'row', axis=0)  19.8 us
    select_n x8, other arithmetic, mix_rows(): return jnp.where(in_first_half(axis), partner + block, partner - block)  12.5 us
    dynamic_update_slice x6, other arithmetic, finish_rows(): return lax.dynamic_update_slice(out, kept, (start, 0))  8.94 us
    slice x3, local copies, waits for them, and re-layouts, copy_rows(): return lax.slice_in_dim(x, start, start + size)  7.89 us
    ppermute x4, starting transfers between devices, from_needed_partner(): return lax.ppermute(block, ('row', 'col'), pairs)  5.13 us
    ppermute x4, waiting for transfers between devices, from_needed_partner(): return lax.ppermute(block, ('row', 'col'), pairs)  4.37 us
  transfers between devices with their start and end apart: 16, of which 6 were waited for; matrix products, arithmetic and copies ran while one was open for 11% of the time, Pallas kernels for 1%

profile of v5, /device:TPU:0, one launch (start us, length us, event | category | flops | bytes accessed | tf_op | source)
XLA Modules:
  0.0 217.9 jit_solution(17691934397693820537)
XLA Ops:
  0.0 5.5 %fusion.10 = (f32[2752,256]{1,0:T(8,128)}, f32[2752,256]{1,0:T(8,128)}) fusion(f32[8192,256]{1,0:T(8,128)} %x_ref.1), kind=kLoop, calls=%fused_computation.33 | loop fusion | bytes 11272192 | tf_op jit(solution)/shard_map/slice | solution.py:43
  5.5 3.1 %collective-permute-start.8 = (f32[2752,256]{1,0:T(8,128)}, f32[2752,256]{1,0:T(8,128)}, u32[]{:S(2)}, u32[]{:S(2)}) collective-permute-start(f32[2752,256]{1,0:T(8,128)} %get-tuple-element.56), channel_id=1, source_target_pairs={{0,8},{1,9},{2,10},{3,11},{4,12},{5,13},{6,14},{7,15},{8,0},{9,1},... | collective-permute-start | bytes 8454152 | tf_op jit(solution)/shard_map/ppermute | solution.py:17
  8.6 1.3 shard_map.29
  10.4 4.0 %collective-permute-start.6 = (f32[512,256]{1,0:T(8,128)S(1)}, f32[512,256]{1,0:T(8,128)S(1)}, u32[]{:S(2)}, u32[]{:S(2)}) collective-permute-start(f32[512,256]{1,0:T(8,128)S(1)} %get-tuple-element.42), channel_id=1, source_target_pairs={{0,64},{16,80},{32,96},{48,112},{64,0},{80,16},{96,32},{112,48},{1... | collective-permute-start | bytes 1572872 | tf_op jit(solution)/shard_map/ppermute | solution.py:17
  15.5 3.1 %collective-permute-start.2 = (f32[160,256]{1,0:T(8,128)S(1)}, f32[160,256]{1,0:T(8,128)S(1)}, u32[]{:S(2)}, u32[]{:S(2)}) collective-permute-start(f32[160,256]{1,0:T(8,128)S(1)} %get-tuple-element.57), channel_id=1, source_target_pairs={{0,8},{1,9},{2,10},{3,11},{4,12},{5,13},{6,14},{7,15},{8,0},{9,1},... | collective-permute-start | bytes 491528 | tf_op jit(solution)/shard_map/ppermute | solution.py:17
  18.7 19.8 %all-gather.1 = f32[8,1,256]{2,1,0:T(1,128)S(1)} all-gather(f32[1,1,256]{2,1,0:T(1,128)S(1)} %bitcast.9), channel_id=2, replica_groups=mesh['row'=8,'col'=16] {'row'}, dimensions={0}, use_global_device_ids=true | all-gather | bytes 9216 | tf_op jit(solution)/shard_map/all_gather | solution.py:164
  38.8 1.4 fusion.9
  40.2 44.4 %collective-permute-done.2 = f32[160,256]{1,0:T(8,128)S(1)} collective-permute-done((f32[160,256]{1,0:T(8,128)S(1)}, f32[160,256]{1,0:T(8,128)S(1)}, u32[]{:S(2)}, u32[]{:S(2)}) %collective-permute-start.2) | collective-permute-done | bytes 163872 | tf_op jit(solution)/shard_map/ppermute | solution.py:17
  84.6 4.1 %collective-permute-start = (f32[160,256]{1,0:T(8,128)S(1)}, f32[160,256]{1,0:T(8,128)S(1)}, u32[]{:S(2)}, u32[]{:S(2)}) collective-permute-start(f32[160,256]{1,0:T(8,128)S(1)} %get-tuple-element.58), channel_id=1, source_target_pairs={{0,64},{16,80},{32,96},{48,112},{64,0},{80,16},{96,32},{112,48},{1... | collective-permute-start | bytes 491528 | tf_op jit(solution)/shard_map/ppermute | solution.py:17
  89.7 2.4 %collective-permute-done = f32[160,256]{1,0:T(8,128)S(1)} collective-permute-done((f32[160,256]{1,0:T(8,128)S(1)}, f32[160,256]{1,0:T(8,128)S(1)}, u32[]{:S(2)}, u32[]{:S(2)}) %collective-permute-start) | collective-permute-done | bytes 163872 | tf_op jit(solution)/shard_map/ppermute | solution.py:17
  92.1 3.1 %collective-permute-start.12 = (f32[672,256]{1,0:T(8,128)S(1)}, f32[672,256]{1,0:T(8,128)S(1)}, u32[]{:S(2)}, u32[]{:S(2)}) collective-permute-start(f32[672,256]{1,0:T(8,128)S(1)} %get-tuple-element.54), channel_id=1, source_target_pairs={{0,8},{1,9},{2,10},{3,11},{4,12},{5,13},{6,14},{7,15},{8,0},{9,1},... | collective-permute-start | bytes 2064392 | tf_op jit(solution)/shard_map/ppermute | solution.py:17
  96.2 3.0 %subtract_select_fusion.1 = f32[2752,256]{1,0:T(8,128)S(1)} fusion(f32[2752,256]{1,0:T(8,128)} %collective-permute-done.8, f32[8192,256]{1,0:T(8,128)} %x_ref.1, pred[]{:T(512)S(6)} %lt.14), kind=kLoop, calls=%fused_computation.3 | loop fusion | flops 2113536 | bytes 8454145 | tf_op jit(solution)/shard_map/jit(_where)/select_n | solution.py:79
  99.2 3.5 %collective-permute-start.9 = (f32[2752,256]{1,0:T(8,128)S(1)}, f32[2752,256]{1,0:T(8,128)S(1)}, u32[]{:S(2)}, u32[]{:S(2)}) collective-permute-start(f32[2752,256]{1,0:T(8,128)S(1)} %subtract_select_fusion.1), channel_id=1, source_target_pairs={{0,64},{16,80},{32,96},{48,112},{64,0},{80,16},{96,32},{112,48},{1... | collective-permute-start | bytes 8454152 | tf_op jit(solution)/shard_map/ppermute | solution.py:17
  102.7 3.0 %subtract_select_fusion = f32[2752,256]{1,0:T(8,128)S(1)} fusion(f32[2752,256]{1,0:T(8,128)} %collective-permute-done.10, f32[8192,256]{1,0:T(8,128)} %x_ref.1, pred[]{:T(512)S(6)} %lt.15), kind=kLoop, calls=%fused_computation.1 | loop fusion | flops 2113536 | bytes 8454145 | tf_op jit(solution)/shard_map/jit(_where)/select_n | solution.py:79
  105.7 1.3 collective-permute-start.11
  108.3 2.4 %collective-permute-start.3 = (f32[160,256]{1,0:T(8,128)S(1)}, f32[160,256]{1,0:T(8,128)S(1)}, u32[]{:S(2)}, u32[]{:S(2)}) collective-permute-start(f32[160,256]{1,0:T(8,128)S(1)} %subtract_select_fusion.6), channel_id=1, source_target_pairs={{0,64},{16,80},{32,96},{48,112},{64,0},{80,16},{96,32},{112,48},{1... | collective-permute-start | bytes 491528 | tf_op jit(solution)/shard_map/ppermute | solution.py:17
  113.0 1.7 collective-permute-start.5
  114.7 64.8 %collective-permute-done.14 = f32[672,256]{1,0:T(8,128)S(1)} collective-permute-done((f32[672,256]{1,0:T(8,128)S(1)}, f32[672,256]{1,0:T(8,128)S(1)}, u32[]{:S(2)}, u32[]{:S(2)}) %collective-permute-start.14) | collective-permute-done | bytes 688160 | tf_op jit(solution)/shard_map/ppermute | solution.py:17
  183.2 8.3 %collective-permute-done.5 = f32[512,256]{1,0:T(8,128)S(1)} collective-permute-done((f32[512,256]{1,0:T(8,128)S(1)}, f32[512,256]{1,0:T(8,128)S(1)}, u32[]{:S(2)}, u32[]{:S(2)}) %collective-permute-start.5) | collective-permute-done | bytes 524320 | tf_op jit(solution)/shard_map/ppermute | solution.py:17
  193.8 3.8 %collective-permute-start.13 = (f32[672,256]{1,0:T(8,128)S(1)}, f32[672,256]{1,0:T(8,128)S(1)}, u32[]{:S(2)}, u32[]{:S(2)}) collective-permute-start(f32[672,256]{1,0:T(8,128)S(1)} %subtract_select_fusion.3), channel_id=1, source_target_pairs={{0,64},{16,80},{32,96},{48,112},{64,0},{80,16},{96,32},{112,48},{1... | collective-permute-start | bytes 2064392 | tf_op jit(solution)/shard_map/ppermute | solution.py:17
  199.8 2.4 %select_dynamic-update-slice_fusion.1 = f32[8192,256]{1,0:T(8,128)} fusion(f32[8192,256]{1,0:T(8,128)} %select_dynamic-update-slice_fusion.4, f32[2752,256]{1,0:T(8,128)S(1)} %collective-permute-done.9, f32[2752,256]{1,0:T(8,128)S(1)} %subtract_select_fusion.1, f32[256]{0:T(256)S(1)} %bitcast.5, f32[2752]{0:T(1024)S(1)} %get-tuple-element.62, s32[]{:T(128)S(6)} %sub.121, ...), kind=kLoop, calls=%fused_computation.2 | loop fusion | flops 5636096 | bytes 8466181 | tf_op jit(solution)/shard_map/dynamic_update_slice | solution.py:143
  202.3 2.4 %select_dynamic-update-slice_fusion = f32[8192,256]{1,0:T(8,128)} fusion(f32[8192,256]{1,0:T(8,128)} %select_dynamic-update-slice_fusion.1, f32[2752,256]{1,0:T(8,128)S(1)} %collective-permute-done.11, f32[2752,256]{1,0:T(8,128)S(1)} %subtract_select_fusion, f32[2752]{0:T(1024)S(1)} %get-tuple-element.61, s32[]{:T(128)S(6)} %sub.124, f32[256]{0:T(256)S(1)} %bitcast.6, ...), kind=kLoop, calls=%fused_computation | loop fusion | flops 5636096 | bytes 8466181 | tf_op jit(solution)/shard_map/dynamic_update_slice | solution.py:143
  204.7 5.3 %collective-permute-done.13 = f32[672,256]{1,0:T(8,128)S(1)} collective-permute-done((f32[672,256]{1,0:T(8,128)S(1)}, f32[672,256]{1,0:T(8,128)S(1)}, u32[]{:S(2)}, u32[]{:S(2)}) %collective-permute-start.13) | collective-permute-done | bytes 688160 | tf_op jit(solution)/shard_map/ppermute | solution.py:17
  211.0 4.4 %collective-permute-done.15 = f32[672,256]{1,0:T(8,128)S(1)} collective-permute-done((f32[672,256]{1,0:T(8,128)S(1)}, f32[672,256]{1,0:T(8,128)S(1)}, u32[]{:S(2)}, u32[]{:S(2)}) %collective-permute-start.15) | collective-permute-done | bytes 688160 | tf_op jit(solution)/shard_map/ppermute | solution.py:30
  (41 shorter events, 19.0 us)
Async XLA Ops:
  5.5 13.1 %copy-start = (f32[8192]{0:T(1024)S(1)}, f32[8192]{0:T(1024)}, u32[]{:S(2)}) copy-start(f32[8192]{0:T(1024)} %param.3) | copy-start | bytes 98308
  5.5 90.7 %collective-permute-start.8 = (f32[2752,256]{1,0:T(8,128)}, f32[2752,256]{1,0:T(8,128)}, u32[]{:S(2)}, u32[]{:S(2)}) collective-permute-start(f32[2752,256]{1,0:T(8,128)} %get-tuple-element.56), channel_id=1, source_target_pairs={{0,8},{1,9},{2,10},{3,11},{4,12},{5,13},{6,14},{7,15},{8,0},{9,1},... | collective-permute-start | bytes 8454152 | tf_op jit(solution)/shard_map/ppermute | solution.py:17
  10.0 97.0 %collective-permute-start.4 = (f32[512,256]{1,0:T(8,128)S(1)}, f32[512,256]{1,0:T(8,128)S(1)}, u32[]{:S(2)}, u32[]{:S(2)}) collective-permute-start(f32[512,256]{1,0:T(8,128)S(1)} %get-tuple-element.39), channel_id=1, source_target_pairs={{0,8},{1,9},{2,10},{3,11},{4,12},{5,13},{6,14},{7,15},{8,0},{9,1},... | collective-permute-start | bytes 1572872 | tf_op jit(solution)/shard_map/ppermute | solution.py:17
  10.4 97.8 %collective-permute-start.6 = (f32[512,256]{1,0:T(8,128)S(1)}, f32[512,256]{1,0:T(8,128)S(1)}, u32[]{:S(2)}, u32[]{:S(2)}) collective-permute-start(f32[512,256]{1,0:T(8,128)S(1)} %get-tuple-element.42), channel_id=1, source_target_pairs={{0,64},{16,80},{32,96},{48,112},{64,0},{80,16},{96,32},{112,48},{1... | collective-permute-start | bytes 1572872 | tf_op jit(solution)/shard_map/ppermute | solution.py:17
  14.4 88.2 %collective-permute-start.10 = (f32[2752,256]{1,0:T(8,128)}, f32[2752,256]{1,0:T(8,128)}, u32[]{:S(2)}, u32[]{:S(2)}) collective-permute-start(f32[2752,256]{1,0:T(8,128)} %get-tuple-element.55), channel_id=1, source_target_pairs={{0,64},{16,80},{32,96},{48,112},{64,0},{80,16},{96,32},{112,48},{1... | collective-permute-start | bytes 8454152 | tf_op jit(solution)/shard_map/ppermute | solution.py:17
  15.5 69.2 %collective-permute-start.2 = (f32[160,256]{1,0:T(8,128)S(1)}, f32[160,256]{1,0:T(8,128)S(1)}, u32[]{:S(2)}, u32[]{:S(2)}) collective-permute-start(f32[160,256]{1,0:T(8,128)S(1)} %get-tuple-element.57), channel_id=1, source_target_pairs={{0,8},{1,9},{2,10},{3,11},{4,12},{5,13},{6,14},{7,15},{8,0},{9,1},... | collective-permute-start | bytes 491528 | tf_op jit(solution)/shard_map/ppermute | solution.py:17
  84.6 7.4 %collective-permute-start = (f32[160,256]{1,0:T(8,128)S(1)}, f32[160,256]{1,0:T(8,128)S(1)}, u32[]{:S(2)}, u32[]{:S(2)}) collective-permute-start(f32[160,256]{1,0:T(8,128)S(1)} %get-tuple-element.58), channel_id=1, source_target_pairs={{0,64},{16,80},{32,96},{48,112},{64,0},{80,16},{96,32},{112,48},{1... | collective-permute-start | bytes 491528 | tf_op jit(solution)/shard_map/ppermute | solution.py:17
  92.1 20.9 %collective-permute-start.12 = (f32[672,256]{1,0:T(8,128)S(1)}, f32[672,256]{1,0:T(8,128)S(1)}, u32[]{:S(2)}, u32[]{:S(2)}) collective-permute-start(f32[672,256]{1,0:T(8,128)S(1)} %get-tuple-element.54), channel_id=1, source_target_pairs={{0,8},{1,9},{2,10},{3,11},{4,12},{5,13},{6,14},{7,15},{8,0},{9,1},... | collective-permute-start | bytes 2064392 | tf_op jit(solution)/shard_map/ppermute | solution.py:17
  99.2 99.4 %collective-permute-start.9 = (f32[2752,256]{1,0:T(8,128)S(1)}, f32[2752,256]{1,0:T(8,128)S(1)}, u32[]{:S(2)}, u32[]{:S(2)}) collective-permute-start(f32[2752,256]{1,0:T(8,128)S(1)} %subtract_select_fusion.1), channel_id=1, source_target_pairs={{0,64},{16,80},{32,96},{48,112},{64,0},{80,16},{96,32},{112,48},{1... | collective-permute-start | bytes 8454152 | tf_op jit(solution)/shard_map/ppermute | solution.py:17
  105.7 96.6 %collective-permute-start.11 = (f32[2752,256]{1,0:T(8,128)S(1)}, f32[2752,256]{1,0:T(8,128)S(1)}, u32[]{:S(2)}, u32[]{:S(2)}) collective-permute-start(f32[2752,256]{1,0:T(8,128)S(1)} %subtract_select_fusion), channel_id=1, source_target_pairs={{8,0},{9,1},{10,2},{11,3},{12,4},{13,5},{14,6},{15,7},{24,16},{25,... | collective-permute-start | bytes 8454152 | tf_op jit(solution)/shard_map/ppermute | solution.py:30
  107.0 72.5 %collective-permute-start.14 = (f32[672,256]{1,0:T(8,128)S(1)}, f32[672,256]{1,0:T(8,128)S(1)}, u32[]{:S(2)}, u32[]{:S(2)}) collective-permute-start(f32[672,256]{1,0:T(8,128)S(1)} %get-tuple-element.53), channel_id=1, source_target_pairs={{0,64},{16,80},{32,96},{48,112},{64,0},{80,16},{96,32},{112,48},{1... | collective-permute-start | bytes 2064392 | tf_op jit(solution)/shard_map/ppermute | solution.py:17
  108.3 108.2 %collective-permute-start.3 = (f32[160,256]{1,0:T(8,128)S(1)}, f32[160,256]{1,0:T(8,128)S(1)}, u32[]{:S(2)}, u32[]{:S(2)}) collective-permute-start(f32[160,256]{1,0:T(8,128)S(1)} %subtract_select_fusion.6), channel_id=1, source_target_pairs={{0,64},{16,80},{32,96},{48,112},{64,0},{80,16},{96,32},{112,48},{1... | collective-permute-start | bytes 491528 | tf_op jit(solution)/shard_map/ppermute | solution.py:17
  113.0 78.5 %collective-permute-start.5 = (f32[512,256]{1,0:T(8,128)S(1)}, f32[512,256]{1,0:T(8,128)S(1)}, u32[]{:S(2)}, u32[]{:S(2)}) collective-permute-start(f32[512,256]{1,0:T(8,128)S(1)} %subtract_select_fusion.5), channel_id=1, source_target_pairs={{0,64},{16,80},{32,96},{48,112},{64,0},{80,16},{96,32},{112,48},{1... | collective-permute-start | bytes 1572872 | tf_op jit(solution)/shard_map/ppermute | solution.py:17
  179.5 14.3 %collective-permute-start.7 = (f32[512,256]{1,0:T(8,128)S(1)}, f32[512,256]{1,0:T(8,128)S(1)}, u32[]{:S(2)}, u32[]{:S(2)}) collective-permute-start(f32[512,256]{1,0:T(8,128)S(1)} %subtract_select_fusion.4), channel_id=1, source_target_pairs={{8,0},{9,1},{10,2},{11,3},{12,4},{13,5},{14,6},{15,7},{24,16},{25,... | collective-permute-start | bytes 1572872 | tf_op jit(solution)/shard_map/ppermute | solution.py:30
  191.5 25.7 %collective-permute-start.1 = (f32[160,256]{1,0:T(8,128)S(1)}, f32[160,256]{1,0:T(8,128)S(1)}, u32[]{:S(2)}, u32[]{:S(2)}) collective-permute-start(f32[160,256]{1,0:T(8,128)S(1)} %subtract_select_fusion.7), channel_id=1, source_target_pairs={{8,0},{9,1},{10,2},{11,3},{12,4},{13,5},{14,6},{15,7},{24,16},{25,... | collective-permute-start | bytes 491528 | tf_op jit(solution)/shard_map/ppermute | solution.py:30
  193.8 16.2 %collective-permute-start.13 = (f32[672,256]{1,0:T(8,128)S(1)}, f32[672,256]{1,0:T(8,128)S(1)}, u32[]{:S(2)}, u32[]{:S(2)}) collective-permute-start(f32[672,256]{1,0:T(8,128)S(1)} %subtract_select_fusion.3), channel_id=1, source_target_pairs={{0,64},{16,80},{32,96},{48,112},{64,0},{80,16},{96,32},{112,48},{1... | collective-permute-start | bytes 2064392 | tf_op jit(solution)/shard_map/ppermute | solution.py:17
  198.5 16.9 %collective-permute-start.15 = (f32[672,256]{1,0:T(8,128)S(1)}, f32[672,256]{1,0:T(8,128)S(1)}, u32[]{:S(2)}, u32[]{:S(2)}) collective-permute-start(f32[672,256]{1,0:T(8,128)S(1)} %subtract_select_fusion.2), channel_id=1, source_target_pairs={{8,0},{9,1},{10,2},{11,3},{12,4},{13,5},{14,6},{15,7},{24,16},{25,... | collective-permute-start | bytes 2064392 | tf_op jit(solution)/shard_map/ppermute | solution.py:30

commit v6 on v5

--- a/solution.py
+++ b/solution.py
@@ -8,8 +8,7 @@
 
 N = 65536
 W = 2048
-SIZES = (512, 2752, 672, 160)
-LAST = 2
+SIZES = (512, 2720, 640, 224)
 
 
 def from_partner(block, axis):
@@ -102,33 +101,39 @@
     return jnp.where(row - col >= gap, scales, jnp.float32(0.0))
 
 
-def finish_last(out, mixed, across, factor, start):
-    size, cols = mixed.shape
+def finish_last(out, chunks):
+    size, cols = chunks[0][0].shape
     half = size // 2
 
-    def kernel(mixed_ref, across_ref, factor_ref, _, out_ref, done_ref, sems):
+    def kernel(*refs):
+        out_ref, done_ref, sems = refs[-3:]
         copies = []
-        for p in range(2):
-            rows = pl.ds(p * half, half)
-            done_ref[rows, :] = (across_ref[rows, :] + mixed_ref[rows, :]) * factor_ref[rows, :]
-            copy = pltpu.make_async_copy(
-                done_ref.at[rows, :], out_ref.at[pl.ds(start + p * half, half), :], sems.at[p]
-            )
-            copy.start()
-            copies.append(copy)
+        for k, (_, _, _, start) in enumerate(chunks):
+            mixed_ref, across_ref, factor_ref = refs[3 * k : 3 * k + 3]
+            for p in range(2):
+                rows = pl.ds(p * half, half)
+                done_ref[k, rows, :] = (across_ref[rows, :] + mixed_ref[rows, :]) * factor_ref[rows, :]
+                copy = pltpu.make_async_copy(
+                    done_ref.at[k, rows, :], out_ref.at[pl.ds(start + p * half, half), :], sems.at[k, p]
+                )
+                copy.start()
+                copies.append(copy)
         for copy in copies:
             copy.wait()
 
     vmem = pl.BlockSpec(memory_space=pltpu.VMEM)
     hbm = pl.BlockSpec(memory_space=pltpu.HBM)
-    held = [pltpu.with_memory_space_constraint(x, pltpu.VMEM) for x in (mixed, across, factor)]
+    held = [pltpu.with_memory_space_constraint(x, pltpu.VMEM) for chunk in chunks for x in chunk[:3]]
     return pl.pallas_call(
         kernel,
-        in_specs=[vmem, vmem, vmem, hbm],
+        in_specs=[vmem] * len(held) + [hbm],
         out_specs=hbm,
         out_shape=jax.ShapeDtypeStruct(out.shape, out.dtype),
-        scratch_shapes=[pltpu.VMEM((size, cols), mixed.dtype), pltpu.SemaphoreType.DMA((2,))],
-        input_output_aliases={3: 0},
+        scratch_shapes=[
+            pltpu.VMEM((len(chunks), size, cols), jnp.float32),
+            pltpu.SemaphoreType.DMA((len(chunks), 2)),
+        ],
+        input_output_aliases={len(held): 0},
     )(*held, out)
 
 
@@ -171,17 +176,18 @@
         acrosses.append(from_needed_partner(mixes[j], second))
 
     out = unwritten(slab_pair.shape, slab_pair.dtype)
+    last = []
     for j in finish_order(len(parts)):
         start, size, _, axis = parts[j]
-        if j >= len(parts) - LAST:
+        if j >= len(parts) - 2:
             (mixed,) = kept_apart(mixes[j])
             mixed = jnp.where(in_first_half(axis), mixed, -mixed)
             factor = factors(butterfly_scale, col_scale, start, size)
             mixed, factor = kept_apart(mixed, factor)
-            out = finish_last(out, mixed, acrosses[j], factor, start)
+            last.append((mixed, acrosses[j], factor, start))
             continue
         out = finish_rows(out, mixes[j], acrosses[j], butterfly_scale, col_scale, start, axis)
-    return out
+    return finish_last(out, last)
 
 
 def finish_order(n):

time: 218 us -> 225 us (1.032)
  waiting for transfers between devices: 130 us -> 142 us
  other arithmetic: 21.6 us -> 16.7 us
  local copies, waits for them, and re-layouts: 8.12 us -> 12.1 us
  blocking collectives: 19.8 us -> 16.9 us
    ppermute x12, waiting for transfers between devices: 125 us -> 135 us  [from_partner(): lax.ppermute(block, axis, [(i, i ^ count // 2) for i in range(count)])]
    dynamic_update_slice x6, other arithmetic: 8.94 us -> 3.52 us  [finish_rows(): return lax.dynamic_update_slice(out, kept, (start, 0))]
    unnamed x2 -> x10, local copies, waits for them, and re-layouts: 0.01 us -> 3.4 us
    all_gather x1, blocking collectives: 19.8 us -> 16.9 us  [per_device(): pieces = lax.all_gather(piece, 'row', axis=0)]
    ppermute x4, waiting for transfers between devices: 4.37 us -> 6.8 us  [from_needed_partner(): return lax.ppermute(block, ('row', 'col'), pairs)]
  transfers between devices with their start and end apart: 16 -> 16, of which waited for: 6 -> 6; matrix products, arithmetic and copies ran while one was open for 11% -> 9% of each run, Pallas kernels for 1% -> 1%
where the time goes in v6:
time: 225 us
  waiting for transfers between devices  142 us (63%)
  starting transfers between devices  34.8 us (15%)
  blocking collectives  16.9 us (8%)
  other arithmetic  16.7 us (7%)
  local copies, waits for them, and re-layouts  12.1 us (5%)
    ppermute x12, waiting for transfers between devices, from_partner(): lax.ppermute(block, axis, [(i, i ^ count // 2) for i in range(count)])  135 us
    ppermute x12, starting transfers between devices, from_partner(): lax.ppermute(block, axis, [(i, i ^ count // 2) for i in range(count)])  29.7 us
    all_gather x1, blocking collectives, per_device(): pieces = lax.all_gather(piece, 'row', axis=0)  16.9 us
    select_n x8, other arithmetic, mix_rows(): return jnp.where(in_first_half(axis), partner + block, partner - block)  13 us
    slice x3, local copies, waits for them, and re-layouts, copy_rows(): return lax.slice_in_dim(x, start, start + size)  7.89 us
    ppermute x4, waiting for transfers between devices, from_needed_partner(): return lax.ppermute(block, ('row', 'col'), pairs)  6.8 us
    ppermute x4, starting transfers between devices, from_needed_partner(): return lax.ppermute(block, ('row', 'col'), pairs)  5.15 us
  transfers between devices with their start and end apart: 16, of which 6 were waited for; matrix products, arithmetic and copies ran while one was open for 9% of the time, Pallas kernels for 1%

profile of v6, /device:TPU:0, one launch (start us, length us, event | category | flops | bytes accessed | tf_op | source)
XLA Modules:
  0.0 224.8 jit_solution(9686341263381215317)
XLA Ops:
  0.0 5.4 %fusion.10 = (f32[2720,256]{1,0:T(8,128)}, f32[2720,256]{1,0:T(8,128)}) fusion(f32[8192,256]{1,0:T(8,128)} %x_ref.1), kind=kLoop, calls=%fused_computation.33 | loop fusion | bytes 11141120 | tf_op jit(solution)/shard_map/slice | solution.py:42
  5.4 3.1 %collective-permute-start.8 = (f32[2720,256]{1,0:T(8,128)}, f32[2720,256]{1,0:T(8,128)}, u32[]{:S(2)}, u32[]{:S(2)}) collective-permute-start(f32[2720,256]{1,0:T(8,128)} %get-tuple-element.56), channel_id=1, source_target_pairs={{0,8},{1,9},{2,10},{3,11},{4,12},{5,13},{6,14},{7,15},{8,0},{9,1},... | collective-permute-start | bytes 8355848 | tf_op jit(solution)/shard_map/ppermute | solution.py:16
  8.6 1.3 shard_map.29
  10.4 4.0 %collective-permute-start.6 = (f32[512,256]{1,0:T(8,128)S(1)}, f32[512,256]{1,0:T(8,128)}, u32[]{:S(2)}, u32[]{:S(2)}) collective-permute-start(f32[512,256]{1,0:T(8,128)S(1)} %get-tuple-element.42), channel_id=1, source_target_pairs={{0,64},{16,80},{32,96},{48,112},{64,0},{80,16},{96,32},{112,48},{1... | collective-permute-start | bytes 1572872 | tf_op jit(solution)/shard_map/ppermute | solution.py:16
  15.5 3.6 %collective-permute-start.2 = (f32[224,256]{1,0:T(8,128)S(1)}, f32[224,256]{1,0:T(8,128)S(1)}, u32[]{:S(2)}, u32[]{:S(2)}) collective-permute-start(f32[224,256]{1,0:T(8,128)S(1)} %get-tuple-element.57), channel_id=1, source_target_pairs={{0,64},{16,80},{32,96},{48,112},{64,0},{80,16},{96,32},{112,48},{1... | collective-permute-start | bytes 688136 | tf_op jit(solution)/shard_map/ppermute | solution.py:16
  19.2 16.9 %all-gather.1 = f32[8,1,256]{2,1,0:T(1,128)S(1)} all-gather(f32[1,1,256]{2,1,0:T(1,128)S(1)} %bitcast.11), channel_id=2, replica_groups=mesh['row'=8,'col'=16] {'row'}, dimensions={0}, use_global_device_ids=true | all-gather | bytes 9216 | tf_op jit(solution)/shard_map/all_gather | solution.py:169
  36.4 1.4 fusion.9
  38.3 52.1 %collective-permute-done.2 = f32[224,256]{1,0:T(8,128)S(1)} collective-permute-done((f32[224,256]{1,0:T(8,128)S(1)}, f32[224,256]{1,0:T(8,128)S(1)}, u32[]{:S(2)}, u32[]{:S(2)}) %collective-permute-start.2) | collective-permute-done | bytes 229408 | tf_op jit(solution)/shard_map/ppermute | solution.py:16
  90.5 3.0 %collective-permute-start = (f32[224,256]{1,0:T(8,128)S(1)}, f32[224,256]{1,0:T(8,128)S(1)}, u32[]{:S(2)}, u32[]{:S(2)}) collective-permute-start(f32[224,256]{1,0:T(8,128)S(1)} %get-tuple-element.58), channel_id=1, source_target_pairs={{0,8},{1,9},{2,10},{3,11},{4,12},{5,13},{6,14},{7,15},{8,0},{9,1},... | collective-permute-start | bytes 688136 | tf_op jit(solution)/shard_map/ppermute | solution.py:16
  94.5 3.7 %collective-permute-done = f32[224,256]{1,0:T(8,128)S(1)} collective-permute-done((f32[224,256]{1,0:T(8,128)S(1)}, f32[224,256]{1,0:T(8,128)S(1)}, u32[]{:S(2)}, u32[]{:S(2)}) %collective-permute-start) | collective-permute-done | bytes 229408 | tf_op jit(solution)/shard_map/ppermute | solution.py:16
  98.2 3.0 %collective-permute-start.12 = (f32[640,256]{1,0:T(8,128)S(1)}, f32[640,256]{1,0:T(8,128)S(1)}, u32[]{:S(2)}, u32[]{:S(2)}) collective-permute-start(f32[640,256]{1,0:T(8,128)S(1)} %get-tuple-element.54), channel_id=1, source_target_pairs={{0,8},{1,9},{2,10},{3,11},{4,12},{5,13},{6,14},{7,15},{8,0},{9,1},... | collective-permute-start | bytes 1966088 | tf_op jit(solution)/shard_map/ppermute | solution.py:16
  102.2 3.2 %subtract_select_fusion.1 = f32[2720,256]{1,0:T(8,128)S(1)} fusion(f32[2720,256]{1,0:T(8,128)} %collective-permute-done.8, f32[8192,256]{1,0:T(8,128)} %x_ref.1, pred[]{:T(512)S(6)} %lt.15), kind=kLoop, calls=%fused_computation.3 | loop fusion | flops 2088960 | bytes 8355841 | tf_op jit(solution)/shard_map/jit(_where)/select_n | solution.py:78
  105.4 3.1 %collective-permute-start.9 = (f32[2720,256]{1,0:T(8,128)S(1)}, f32[2720,256]{1,0:T(8,128)S(1)}, u32[]{:S(2)}, u32[]{:S(2)}) collective-permute-start(f32[2720,256]{1,0:T(8,128)S(1)} %subtract_select_fusion.1), channel_id=1, source_target_pairs={{0,64},{16,80},{32,96},{48,112},{64,0},{80,16},{96,32},{112,48},{1... | collective-permute-start | bytes 8355848 | tf_op jit(solution)/shard_map/ppermute | solution.py:16
  108.5 3.0 %subtract_select_fusion = f32[2720,256]{1,0:T(8,128)S(1)} fusion(f32[2720,256]{1,0:T(8,128)} %collective-permute-done.10, f32[8192,256]{1,0:T(8,128)} %x_ref.1, pred[]{:T(512)S(6)} %lt.14), kind=kLoop, calls=%fused_computation.1 | loop fusion | flops 2088960 | bytes 8355841 | tf_op jit(solution)/shard_map/jit(_where)/select_n | solution.py:78
  112.8 1.9 collective-permute-start.14
  114.8 1.8 collective-permute-start.1
  119.1 1.9 collective-permute-start.5
  121.0 63.2 %collective-permute-done.14 = f32[640,256]{1,0:T(8,128)S(1)} collective-permute-done((f32[640,256]{1,0:T(8,128)S(1)}, f32[640,256]{1,0:T(8,128)S(1)}, u32[]{:S(2)}, u32[]{:S(2)}) %collective-permute-start.14) | collective-permute-done | bytes 655392 | tf_op jit(solution)/shard_map/ppermute | solution.py:16
  187.9 9.1 %collective-permute-done.5 = f32[512,256]{1,0:T(8,128)S(1)} collective-permute-done((f32[512,256]{1,0:T(8,128)S(1)}, f32[512,256]{1,0:T(8,128)S(1)}, u32[]{:S(2)}, u32[]{:S(2)}) %collective-permute-start.5) | collective-permute-done | bytes 524320 | tf_op jit(solution)/shard_map/ppermute | solution.py:16
  198.5 3.7 %collective-permute-start.13 = (f32[640,256]{1,0:T(8,128)S(1)}, f32[640,256]{1,0:T(8,128)S(1)}, u32[]{:S(2)}, u32[]{:S(2)}) collective-permute-start(f32[640,256]{1,0:T(8,128)S(1)} %subtract_select_fusion.3), channel_id=1, source_target_pairs={{0,64},{16,80},{32,96},{48,112},{64,0},{80,16},{96,32},{112,48},{1... | collective-permute-start | bytes 1966088 | tf_op jit(solution)/shard_map/ppermute | solution.py:16
  205.0 1.4 select_dynamic-update-slice_fusion
  206.4 7.0 %collective-permute-done.13 = f32[640,256]{1,0:T(8,128)S(1)} collective-permute-done((f32[640,256]{1,0:T(8,128)S(1)}, f32[640,256]{1,0:T(8,128)S(1)}, u32[]{:S(2)}, u32[]{:S(2)}) %collective-permute-start.13) | collective-permute-done | bytes 655392 | tf_op jit(solution)/shard_map/ppermute | solution.py:16
  213.6 6.8 %collective-permute-done.15 = f32[640,256]{1,0:T(8,128)S(1)} collective-permute-done((f32[640,256]{1,0:T(8,128)S(1)}, f32[640,256]{1,0:T(8,128)S(1)}, u32[]{:S(2)}, u32[]{:S(2)}) %collective-permute-start.15) | collective-permute-done | bytes 655392 | tf_op jit(solution)/shard_map/ppermute | solution.py:29
  220.7 3.4 %copy-done = f32[8192,256]{1,0:T(8,128)} copy-done((f32[8192,256]{1,0:T(8,128)}, f32[8192,256]{1,0:T(8,128)S(1)}, u32[]{:S(2)}) %copy-start) | copy-done | bytes 8388632
  (49 shorter events, 17.5 us)
Async XLA Ops:
  5.4 13.7 %copy-start.1 = (f32[8192]{0:T(1024)S(1)}, f32[8192]{0:T(1024)}, u32[]{:S(2)}) copy-start(f32[8192]{0:T(1024)} %param.3) | copy-start | bytes 98308
  5.4 96.7 %collective-permute-start.8 = (f32[2720,256]{1,0:T(8,128)}, f32[2720,256]{1,0:T(8,128)}, u32[]{:S(2)}, u32[]{:S(2)}) collective-permute-start(f32[2720,256]{1,0:T(8,128)} %get-tuple-element.56), channel_id=1, source_target_pairs={{0,8},{1,9},{2,10},{3,11},{4,12},{5,13},{6,14},{7,15},{8,0},{9,1},... | collective-permute-start | bytes 8355848 | tf_op jit(solution)/shard_map/ppermute | solution.py:16
  9.9 102.9 %collective-permute-start.4 = (f32[512,256]{1,0:T(8,128)S(1)}, f32[512,256]{1,0:T(8,128)}, u32[]{:S(2)}, u32[]{:S(2)}) collective-permute-start(f32[512,256]{1,0:T(8,128)S(1)} %get-tuple-element.39), channel_id=1, source_target_pairs={{0,8},{1,9},{2,10},{3,11},{4,12},{5,13},{6,14},{7,15},{8,0},{9,1},... | collective-permute-start | bytes 1572872 | tf_op jit(solution)/shard_map/ppermute | solution.py:16
  10.4 104.4 %collective-permute-start.6 = (f32[512,256]{1,0:T(8,128)S(1)}, f32[512,256]{1,0:T(8,128)}, u32[]{:S(2)}, u32[]{:S(2)}) collective-permute-start(f32[512,256]{1,0:T(8,128)S(1)} %get-tuple-element.42), channel_id=1, source_target_pairs={{0,64},{16,80},{32,96},{48,112},{64,0},{80,16},{96,32},{112,48},{1... | collective-permute-start | bytes 1572872 | tf_op jit(solution)/shard_map/ppermute | solution.py:16
  14.4 94.1 %collective-permute-start.10 = (f32[2720,256]{1,0:T(8,128)}, f32[2720,256]{1,0:T(8,128)}, u32[]{:S(2)}, u32[]{:S(2)}) collective-permute-start(f32[2720,256]{1,0:T(8,128)} %get-tuple-element.55), channel_id=1, source_target_pairs={{0,64},{16,80},{32,96},{48,112},{64,0},{80,16},{96,32},{112,48},{1... | collective-permute-start | bytes 8355848 | tf_op jit(solution)/shard_map/ppermute | solution.py:16
  15.5 75.0 %collective-permute-start.2 = (f32[224,256]{1,0:T(8,128)S(1)}, f32[224,256]{1,0:T(8,128)S(1)}, u32[]{:S(2)}, u32[]{:S(2)}) collective-permute-start(f32[224,256]{1,0:T(8,128)S(1)} %get-tuple-element.57), channel_id=1, source_target_pairs={{0,64},{16,80},{32,96},{48,112},{64,0},{80,16},{96,32},{112,48},{1... | collective-permute-start | bytes 688136 | tf_op jit(solution)/shard_map/ppermute | solution.py:16
  90.5 7.7 %collective-permute-start = (f32[224,256]{1,0:T(8,128)S(1)}, f32[224,256]{1,0:T(8,128)S(1)}, u32[]{:S(2)}, u32[]{:S(2)}) collective-permute-start(f32[224,256]{1,0:T(8,128)S(1)} %get-tuple-element.58), channel_id=1, source_target_pairs={{0,8},{1,9},{2,10},{3,11},{4,12},{5,13},{6,14},{7,15},{8,0},{9,1},... | collective-permute-start | bytes 688136 | tf_op jit(solution)/shard_map/ppermute | solution.py:16
  98.2 21.0 %collective-permute-start.12 = (f32[640,256]{1,0:T(8,128)S(1)}, f32[640,256]{1,0:T(8,128)S(1)}, u32[]{:S(2)}, u32[]{:S(2)}) collective-permute-start(f32[640,256]{1,0:T(8,128)S(1)} %get-tuple-element.54), channel_id=1, source_target_pairs={{0,8},{1,9},{2,10},{3,11},{4,12},{5,13},{6,14},{7,15},{8,0},{9,1},... | collective-permute-start | bytes 1966088 | tf_op jit(solution)/shard_map/ppermute | solution.py:16
  102.2 96.1 %slice-start = ((s8[8388608]{0:T(1024)(128)(4,1)}), s8[4194304]{0:T(1024)(128)(4,1)S(1)}, s32[]{:S(2)}) async-start(s8[8388608]{0:T(1024)(128)(4,1)} %bitcast.2), calls=%async_computation | async-start | bytes 8388608
  105.3 92.9 %slice-start.1 = ((s8[8388608]{0:T(1024)(128)(4,1)}), s8[4194304]{0:T(1024)(128)(4,1)S(1)}, s32[]{:S(2)}) async-start(s8[8388608]{0:T(1024)(128)(4,1)} %bitcast.2), calls=%async_computation.1 | async-start | bytes 8388608
  105.4 97.0 %collective-permute-start.9 = (f32[2720,256]{1,0:T(8,128)S(1)}, f32[2720,256]{1,0:T(8,128)S(1)}, u32[]{:S(2)}, u32[]{:S(2)}) collective-permute-start(f32[2720,256]{1,0:T(8,128)S(1)} %subtract_select_fusion.1), channel_id=1, source_target_pairs={{0,64},{16,80},{32,96},{48,112},{64,0},{80,16},{96,32},{112,48},{1... | collective-permute-start | bytes 8355848 | tf_op jit(solution)/shard_map/ppermute | solution.py:16
  111.5 93.5 %collective-permute-start.11 = (f32[2720,256]{1,0:T(8,128)S(1)}, f32[2720,256]{1,0:T(8,128)S(1)}, u32[]{:S(2)}, u32[]{:S(2)}) collective-permute-start(f32[2720,256]{1,0:T(8,128)S(1)} %subtract_select_fusion), channel_id=1, source_target_pairs={{8,0},{9,1},{10,2},{11,3},{12,4},{13,5},{14,6},{15,7},{24,16},{25,... | collective-permute-start | bytes 8355848 | tf_op jit(solution)/shard_map/ppermute | solution.py:29
  112.8 71.4 %collective-permute-start.14 = (f32[640,256]{1,0:T(8,128)S(1)}, f32[640,256]{1,0:T(8,128)S(1)}, u32[]{:S(2)}, u32[]{:S(2)}) collective-permute-start(f32[640,256]{1,0:T(8,128)S(1)} %get-tuple-element.53), channel_id=1, source_target_pairs={{0,64},{16,80},{32,96},{48,112},{64,0},{80,16},{96,32},{112,48},{1... | collective-permute-start | bytes 1966088 | tf_op jit(solution)/shard_map/ppermute | solution.py:16
  114.8 105.9 %collective-permute-start.1 = (f32[224,256]{1,0:T(8,128)S(1)}, f32[224,256]{1,0:T(8,128)S(1)}, u32[]{:S(2)}, u32[]{:S(2)}) collective-permute-start(f32[224,256]{1,0:T(8,128)S(1)} %subtract_select_fusion.7), channel_id=1, source_target_pairs={{0,64},{16,80},{32,96},{48,112},{64,0},{80,16},{96,32},{112,48},{1... | collective-permute-start | bytes 688136 | tf_op jit(solution)/shard_map/ppermute | solution.py:16
  117.8 80.4 %copy-start.2 = (f32[512]{0:T(512)S(1)}, f32[512]{0:T(512)}, u32[]{:S(2)}) copy-start(f32[512]{0:T(512)} %get-tuple-element.64) | copy-start | bytes 6148
  119.1 77.8 %collective-permute-start.5 = (f32[512,256]{1,0:T(8,128)S(1)}, f32[512,256]{1,0:T(8,128)S(1)}, u32[]{:S(2)}, u32[]{:S(2)}) collective-permute-start(f32[512,256]{1,0:T(8,128)S(1)} %subtract_select_fusion.5), channel_id=1, source_target_pairs={{0,64},{16,80},{32,96},{48,112},{64,0},{80,16},{96,32},{112,48},{1... | collective-permute-start | bytes 1572872 | tf_op jit(solution)/shard_map/ppermute | solution.py:16
  184.2 14.2 %collective-permute-start.7 = (f32[512,256]{1,0:T(8,128)S(1)}, f32[512,256]{1,0:T(8,128)S(1)}, u32[]{:S(2)}, u32[]{:S(2)}) collective-permute-start(f32[512,256]{1,0:T(8,128)S(1)} %subtract_select_fusion.4), channel_id=1, source_target_pairs={{8,0},{9,1},{10,2},{11,3},{12,4},{13,5},{14,6},{15,7},{24,16},{25,... | collective-permute-start | bytes 1572872 | tf_op jit(solution)/shard_map/ppermute | solution.py:29
  197.0 27.1 %collective-permute-start.3 = (f32[224,256]{1,0:T(8,128)S(1)}, f32[224,256]{1,0:T(8,128)S(1)}, u32[]{:S(2)}, u32[]{:S(2)}) collective-permute-start(f32[224,256]{1,0:T(8,128)S(1)} %subtract_select_fusion.6), channel_id=1, source_target_pairs={{8,0},{9,1},{10,2},{11,3},{12,4},{13,5},{14,6},{15,7},{24,16},{25,... | collective-permute-start | bytes 688136 | tf_op jit(solution)/shard_map/ppermute | solution.py:29
  198.5 14.9 %collective-permute-start.13 = (f32[640,256]{1,0:T(8,128)S(1)}, f32[640,256]{1,0:T(8,128)S(1)}, u32[]{:S(2)}, u32[]{:S(2)}) collective-permute-start(f32[640,256]{1,0:T(8,128)S(1)} %subtract_select_fusion.3), channel_id=1, source_target_pairs={{0,64},{16,80},{32,96},{48,112},{64,0},{80,16},{96,32},{112,48},{1... | collective-permute-start | bytes 1966088 | tf_op jit(solution)/shard_map/ppermute | solution.py:16
  202.4 18.0 %collective-permute-start.15 = (f32[640,256]{1,0:T(8,128)S(1)}, f32[640,256]{1,0:T(8,128)S(1)}, u32[]{:S(2)}, u32[]{:S(2)}) collective-permute-start(f32[640,256]{1,0:T(8,128)S(1)} %subtract_select_fusion.2), channel_id=1, source_target_pairs={{8,0},{9,1},{10,2},{11,3},{12,4},{13,5},{14,6},{15,7},{24,16},{25,... | collective-permute-start | bytes 1966088 | tf_op jit(solution)/shard_map/ppermute | solution.py:29
  220.6 3.4 %copy-start = (f32[8192,256]{1,0:T(8,128)}, f32[8192,256]{1,0:T(8,128)S(1)}, u32[]{:S(2)}) copy-start(f32[8192,256]{1,0:T(8,128)S(1)} %select_dynamic-update-slice_fusion.2.refs_6_) | copy-start | bytes 25165828

commit v7 on v6

--- a/solution.py
+++ b/solution.py
@@ -8,12 +8,23 @@
 
 N = 65536
 W = 2048
-SIZES = (512, 2720, 640, 224)
+SIZES = (512, 2656, 608, 320)
 
 
 def from_partner(block, axis):
     count = lax.axis_size(axis)
     return lax.ppermute(block, axis, [(i, i ^ count // 2) for i in range(count)])
+
+
+def from_partner_by_core(block, first):
+    rows, cols = lax.axis_size("row"), lax.axis_size("col")
+    pairs = []
+    for r in range(rows):
+        for c in range(cols):
+            along_rows = c % 2 == first
+            partner = (r ^ rows // 2, c) if along_rows else (r, c ^ cols // 2)
+            pairs.append((r * cols + c, partner[0] * cols + partner[1]))
+    return lax.ppermute(block, ("row", "col"), pairs)
 
 
 def from_needed_partner(block, axis):
@@ -42,22 +53,20 @@
     return lax.slice_in_dim(x, start, start + size)
 
 
-def copy_first(x, starts, size):
+def copy_first(x, starts, size, first):
     pieces = 4
     step = size // pieces
 
-    def kernel(x_ref, *refs):
-        out_refs, sems = refs[:-1], refs[-1]
-        copies = []
-        for p in range(pieces):
-            for k, (start, out_ref) in enumerate(zip(starts, out_refs)):
-                copies.append(
-                    pltpu.make_async_copy(
-                        x_ref.at[pl.ds(start + p * step, step), :],
-                        out_ref.at[pl.ds(p * step, step), :],
-                        sems.at[k, p],
-                    )
-                )
+    def kernel(x_ref, out_ref, sems):
+        start = jnp.where(lax.axis_index("col") % 2 == first, starts[0], starts[1])
+        copies = [
+            pltpu.make_async_copy(
+                x_ref.at[pl.ds(pl.multiple_of(start + p * step, step), step), :],
+                out_ref.at[pl.ds(p * step, step), :],
+                sems.at[p],
+            )
+            for p in range(pieces)
+        ]
         for copy in copies:
             copy.start()
         for copy in copies:
@@ -66,9 +75,9 @@
     return pl.pallas_call(
         kernel,
         in_specs=[pl.BlockSpec(memory_space=pltpu.HBM)],
-        out_specs=[pl.BlockSpec(memory_space=pltpu.VMEM)] * len(starts),
-        out_shape=[pltpu.VMEM((size, x.shape[1]), x.dtype)] * len(starts),
-        scratch_shapes=[pltpu.SemaphoreType.DMA((len(starts), pieces))],
+        out_specs=pl.BlockSpec(memory_space=pltpu.VMEM),
+        out_shape=pltpu.VMEM((size, x.shape[1]), x.dtype),
+        scratch_shapes=[pltpu.SemaphoreType.DMA((pieces,))],
     )(x)
 
 
@@ -158,10 +167,15 @@
         parts.append((local_rows // 2 + start, size, "col", "row"))
         start += size
 
-    theirs = []
-    firsts = copy_first(slab_pair, [part[0] for part in parts[:2]], SIZES[0])
-    for j, (start, size, first, _) in enumerate(parts):
-        block = firsts[j] if j < 2 else copy_rows(slab_pair, start, size)
+    first_starts = [part[0] for part in parts[:2]]
+    got = []
+    for j in range(2):
+        block = copy_first(slab_pair, first_starts, SIZES[0], j)
+        got.append(from_partner_by_core(block, j))
+    core = lax.axis_index("col") % 2
+    theirs = [jnp.where(core == j, got[0], got[1]) for j in range(2)]
+    for j, (start, size, first, _) in enumerate(parts[2:], 2):
+        block = copy_rows(slab_pair, start, size)
         theirs.append(from_partner(block, first))
 
     at = lax.axis_index("col") * local_cols % W

time: 225 us -> 220 us (0.978)
  waiting for transfers between devices: 142 us -> 133 us
  other arithmetic: 16.7 us -> 21.5 us
  local copies, waits for them, and re-layouts: 12.1 us -> 8.76 us
    ppermute x0 -> x2, starting transfers between devices: none -> 7.17 us  [from_partner_by_core(): return lax.ppermute(block, ('row', 'col'), pairs)]
    ppermute x12 -> x10, waiting for transfers between devices: 135 us -> 128 us  [from_partner(): lax.ppermute(block, axis, [(i, i ^ count // 2) for i in range(count)])]
    ppermute x12 -> x10, starting transfers between devices: 29.7 us -> 23.5 us  [from_partner(): lax.ppermute(block, axis, [(i, i ^ count // 2) for i in range(count)])]
    dynamic_update_slice x6, other arithmetic: 3.52 us -> 8.77 us  [finish_rows(): return lax.dynamic_update_slice(out, kept, (start, 0))]
    unnamed x10 -> x2, local copies, waits for them, and re-layouts: 3.4 us -> 0.01 us
  transfers between devices with their start and end apart: 16 -> 16, of which waited for: 6 -> 6; matrix products, arithmetic and copies ran while one was open for 9% -> 14% of each run, Pallas kernels for 1% -> 1%
where the time goes in v7:
time: 220 us; the launch traced here: 219 us
  waiting for transfers between devices  133 us (60%)
  starting transfers between devices  35.8 us (16%)
  other arithmetic  21.5 us (10%)
  blocking collectives  16.9 us (8%)
  local copies, waits for them, and re-layouts  8.76 us (4%)
  Pallas kernels  3.14 us (1%)
    ppermute x10, waiting for transfers between devices, from_partner(): lax.ppermute(block, axis, [(i, i ^ count // 2) for i in range(count)])  128 us
    ppermute x10, starting transfers between devices, from_partner(): lax.ppermute(block, axis, [(i, i ^ count // 2) for i in range(count)])  23.5 us
    all_gather x1, blocking collectives, per_device(): pieces = lax.all_gather(piece, 'row', axis=0)  16.9 us
    select_n x8, other arithmetic, mix_rows(): return jnp.where(in_first_half(axis), partner + block, partner - block)  12.5 us
    dynamic_update_slice x6, other arithmetic, finish_rows(): return lax.dynamic_update_slice(out, kept, (start, 0))  8.77 us
    slice x3, local copies, waits for them, and re-layouts, copy_rows(): return lax.slice_in_dim(x, start, start + size)  8.52 us
    ppermute x2, starting transfers between devices, from_partner_by_core(): return lax.ppermute(block, ('row', 'col'), pairs)  7.17 us
    ppermute x4, starting transfers between devices, from_needed_partner(): return lax.ppermute(block, ('row', 'col'), pairs)  5.12 us
  transfers between devices with their start and end apart: 16, of which 6 were waited for; matrix products, arithmetic and copies ran while one was open for 14% of the time, Pallas kernels for 1%

profile of v7, /device:TPU:0, one launch (start us, length us, event | category | flops | bytes accessed | tf_op | source)
XLA Modules:
  0.0 219.2 jit_solution(5337517166600957636)
XLA Ops:
  1.1 4.1 %collective-permute-start.4 = (f32[512,256]{1,0:T(8,128)S(1)}, f32[512,256]{1,0:T(8,128)S(1)}, u32[]{:S(2)}, u32[]{:S(2)}) collective-permute-start(f32[512,256]{1,0:T(8,128)S(1)} %shard_map.29), channel_id=1, source_target_pairs={{0,64},{1,9},{2,66},{3,11},{4,68},{5,13},{6,70},{7,15},{8,72},{9,1... | collective-permute-start | bytes 1572872 | tf_op jit(solution)/shard_map/ppermute | solution.py:27
  6.3 3.1 %collective-permute-start.5 = (f32[512,256]{1,0:T(8,128)S(1)}, f32[512,256]{1,0:T(8,128)S(1)}, u32[]{:S(2)}, u32[]{:S(2)}) collective-permute-start(f32[512,256]{1,0:T(8,128)S(1)} %shard_map.30), channel_id=1, source_target_pairs={{0,8},{1,65},{2,10},{3,67},{4,12},{5,69},{6,14},{7,71},{8,0},{9,73... | collective-permute-start | bytes 1572872 | tf_op jit(solution)/shard_map/ppermute | solution.py:27
  9.5 5.3 %fusion.10 = (f32[2656,256]{1,0:T(8,128)}, f32[2656,256]{1,0:T(8,128)}) fusion(f32[8192,256]{1,0:T(8,128)} %x_ref.3), kind=kLoop, calls=%fused_computation.35 | loop fusion | bytes 10878976 | tf_op jit(solution)/shard_map/slice | solution.py:53
  15.3 1.8 fusion.11
  17.2 3.5 %collective-permute-start.2 = (f32[320,256]{1,0:T(8,128)}, f32[320,256]{1,0:T(8,128)S(1)}, u32[]{:S(2)}, u32[]{:S(2)}) collective-permute-start(f32[320,256]{1,0:T(8,128)} %get-tuple-element.53), channel_id=1, source_target_pairs={{0,64},{16,80},{32,96},{48,112},{64,0},{80,16},{96,32},{112,48},{1... | collective-permute-start | bytes 983048 | tf_op jit(solution)/shard_map/ppermute | solution.py:16
  20.7 16.9 %all-gather.1 = f32[8,1,256]{2,1,0:T(1,128)S(1)} all-gather(f32[1,1,256]{2,1,0:T(1,128)S(1)} %bitcast.9), channel_id=2, replica_groups=mesh['row'=8,'col'=16] {'row'}, dimensions={0}, use_global_device_ids=true | all-gather | bytes 9216 | tf_op jit(solution)/shard_map/all_gather | solution.py:183
  38.0 1.3 fusion.9
  39.4 44.7 %collective-permute-done.2 = f32[320,256]{1,0:T(8,128)S(1)} collective-permute-done((f32[320,256]{1,0:T(8,128)}, f32[320,256]{1,0:T(8,128)S(1)}, u32[]{:S(2)}, u32[]{:S(2)}) %collective-permute-start.2) | collective-permute-done | bytes 327712 | tf_op jit(solution)/shard_map/ppermute | solution.py:16
  84.0 3.0 %collective-permute-start = (f32[320,256]{1,0:T(8,128)S(1)}, f32[320,256]{1,0:T(8,128)S(1)}, u32[]{:S(2)}, u32[]{:S(2)}) collective-permute-start(f32[320,256]{1,0:T(8,128)S(1)} %get-tuple-element.54), channel_id=1, source_target_pairs={{0,8},{1,9},{2,10},{3,11},{4,12},{5,13},{6,14},{7,15},{8,0},{9,1},... | collective-permute-start | bytes 983048 | tf_op jit(solution)/shard_map/ppermute | solution.py:16
  88.1 6.2 %collective-permute-done = f32[320,256]{1,0:T(8,128)S(1)} collective-permute-done((f32[320,256]{1,0:T(8,128)S(1)}, f32[320,256]{1,0:T(8,128)S(1)}, u32[]{:S(2)}, u32[]{:S(2)}) %collective-permute-start) | collective-permute-done | bytes 327712 | tf_op jit(solution)/shard_map/ppermute | solution.py:16
  94.3 3.0 %collective-permute-start.12 = (f32[608,256]{1,0:T(8,128)S(1)}, f32[608,256]{1,0:T(8,128)S(1)}, u32[]{:S(2)}, u32[]{:S(2)}) collective-permute-start(f32[608,256]{1,0:T(8,128)S(1)} %get-tuple-element.50), channel_id=1, source_target_pairs={{0,8},{1,9},{2,10},{3,11},{4,12},{5,13},{6,14},{7,15},{8,0},{9,1},... | collective-permute-start | bytes 1867784 | tf_op jit(solution)/shard_map/ppermute | solution.py:16
  98.3 3.7 %collective-permute-start.14 = (f32[608,256]{1,0:T(8,128)S(1)}, f32[608,256]{1,0:T(8,128)S(1)}, u32[]{:S(2)}, u32[]{:S(2)}) collective-permute-start(f32[608,256]{1,0:T(8,128)S(1)} %get-tuple-element.49), channel_id=1, source_target_pairs={{0,64},{16,80},{32,96},{48,112},{64,0},{80,16},{96,32},{112,48},{1... | collective-permute-start | bytes 1867784 | tf_op jit(solution)/shard_map/ppermute | solution.py:16
  102.0 2.9 %subtract_select_fusion.1 = f32[2656,256]{1,0:T(8,128)S(1)} fusion(f32[2656,256]{1,0:T(8,128)} %collective-permute-done.8, f32[8192,256]{1,0:T(8,128)} %x_ref.3, pred[]{:T(512)S(6)} %lt.19), kind=kLoop, calls=%fused_computation.3 | loop fusion | flops 2039808 | bytes 8159233 | tf_op jit(solution)/shard_map/jit(_where)/select_n | solution.py:87
  105.1 2.9 %subtract_select_fusion = f32[2656,256]{1,0:T(8,128)S(1)} fusion(f32[2656,256]{1,0:T(8,128)} %collective-permute-done.10, f32[8192,256]{1,0:T(8,128)} %x_ref.3, pred[]{:T(512)S(6)} %lt.18), kind=kLoop, calls=%fused_computation.1 | loop fusion | flops 2039808 | bytes 8159233 | tf_op jit(solution)/shard_map/jit(_where)/select_n | solution.py:87
  108.0 3.6 %collective-permute-start.1 = (f32[320,256]{1,0:T(8,128)S(1)}, f32[320,256]{1,0:T(8,128)S(1)}, u32[]{:S(2)}, u32[]{:S(2)}) collective-permute-start(f32[320,256]{1,0:T(8,128)S(1)} %subtract_select_fusion.7), channel_id=1, source_target_pairs={{0,64},{16,80},{32,96},{48,112},{64,0},{80,16},{96,32},{112,48},{1... | collective-permute-start | bytes 983048 | tf_op jit(solution)/shard_map/ppermute | solution.py:16
  111.6 1.3 collective-permute-start.11
  116.9 1.3 collective-permute-start.7
  120.5 71.2 %collective-permute-done.6 = f32[512,256]{1,0:T(8,128)S(1)} collective-permute-done((f32[512,256]{1,0:T(8,128)S(1)}, f32[512,256]{1,0:T(8,128)S(1)}, u32[]{:S(2)}, u32[]{:S(2)}) %collective-permute-start.6) | collective-permute-done | bytes 524320 | tf_op jit(solution)/shard_map/ppermute | solution.py:16
  194.0 4.9 %collective-permute-start.13 = (f32[608,256]{1,0:T(8,128)S(1)}, f32[608,256]{1,0:T(8,128)S(1)}, u32[]{:S(2)}, u32[]{:S(2)}) collective-permute-start(f32[608,256]{1,0:T(8,128)S(1)} %subtract_select_fusion.3), channel_id=1, source_target_pairs={{0,64},{16,80},{32,96},{48,112},{64,0},{80,16},{96,32},{112,48},{1... | collective-permute-start | bytes 1867784 | tf_op jit(solution)/shard_map/ppermute | solution.py:16
  199.9 1.3 collective-permute-start.15
  201.2 2.4 %select_dynamic-update-slice_fusion.1 = f32[8192,256]{1,0:T(8,128)} fusion(f32[8192,256]{1,0:T(8,128)} %select_dynamic-update-slice_fusion.4, f32[2656,256]{1,0:T(8,128)S(1)} %collective-permute-done.9, f32[2656,256]{1,0:T(8,128)S(1)} %subtract_select_fusion.1, f32[256]{0:T(256)S(1)} %bitcast.5, f32[2656]{0:T(1024)S(1)} %get-tuple-element.60, s32[]{:T(128)S(6)} %sub.121, ...), kind=kLoop, calls=%fused_computation.2 | loop fusion | flops 5439488 | bytes 8170885 | tf_op jit(solution)/shard_map/dynamic_update_slice | solution.py:157
  203.5 2.4 %select_dynamic-update-slice_fusion = f32[8192,256]{1,0:T(8,128)} fusion(f32[8192,256]{1,0:T(8,128)} %select_dynamic-update-slice_fusion.1, f32[2656,256]{1,0:T(8,128)S(1)} %collective-permute-done.11, f32[2656,256]{1,0:T(8,128)S(1)} %subtract_select_fusion, f32[2656]{0:T(1024)S(1)} %get-tuple-element.59, s32[]{:T(128)S(6)} %sub.124, f32[256]{0:T(256)S(1)} %bitcast.6, ...), kind=kLoop, calls=%fused_computation | loop fusion | flops 5439488 | bytes 8170885 | tf_op jit(solution)/shard_map/dynamic_update_slice | solution.py:157
  205.9 5.5 %collective-permute-done.13 = f32[608,256]{1,0:T(8,128)S(1)} collective-permute-done((f32[608,256]{1,0:T(8,128)S(1)}, f32[608,256]{1,0:T(8,128)S(1)}, u32[]{:S(2)}, u32[]{:S(2)}) %collective-permute-start.13) | collective-permute-done | bytes 622624 | tf_op jit(solution)/shard_map/ppermute | solution.py:16
  212.5 4.8 %collective-permute-done.15 = f32[608,256]{1,0:T(8,128)S(1)} collective-permute-done((f32[608,256]{1,0:T(8,128)S(1)}, f32[608,256]{1,0:T(8,128)S(1)}, u32[]{:S(2)}, u32[]{:S(2)}) %collective-permute-start.15) | collective-permute-done | bytes 622624 | tf_op jit(solution)/shard_map/ppermute | solution.py:40
  (42 shorter events, 17.9 us)
Async XLA Ops:
  1.1 106.9 %collective-permute-start.4 = (f32[512,256]{1,0:T(8,128)S(1)}, f32[512,256]{1,0:T(8,128)S(1)}, u32[]{:S(2)}, u32[]{:S(2)}) collective-permute-start(f32[512,256]{1,0:T(8,128)S(1)} %shard_map.29), channel_id=1, source_target_pairs={{0,64},{1,9},{2,66},{3,11},{4,68},{5,13},{6,70},{7,15},{8,72},{9,1... | collective-permute-start | bytes 1572872 | tf_op jit(solution)/shard_map/ppermute | solution.py:27
  6.3 14.3 %copy-start = (f32[8192]{0:T(1024)S(1)}, f32[8192]{0:T(1024)}, u32[]{:S(2)}) copy-start(f32[8192]{0:T(1024)} %param.3) | copy-start | bytes 98308
  6.3 105.3 %collective-permute-start.5 = (f32[512,256]{1,0:T(8,128)S(1)}, f32[512,256]{1,0:T(8,128)S(1)}, u32[]{:S(2)}, u32[]{:S(2)}) collective-permute-start(f32[512,256]{1,0:T(8,128)S(1)} %shard_map.30), channel_id=1, source_target_pairs={{0,8},{1,65},{2,10},{3,67},{4,12},{5,69},{6,14},{7,71},{8,0},{9,73... | collective-permute-start | bytes 1572872 | tf_op jit(solution)/shard_map/ppermute | solution.py:27
  14.8 83.6 %collective-permute-start.8 = (f32[2656,256]{1,0:T(8,128)}, f32[2656,256]{1,0:T(8,128)}, u32[]{:S(2)}, u32[]{:S(2)}) collective-permute-start(f32[2656,256]{1,0:T(8,128)} %get-tuple-element.52), channel_id=1, source_target_pairs={{0,8},{1,9},{2,10},{3,11},{4,12},{5,13},{6,14},{7,15},{8,0},{9,1},... | collective-permute-start | bytes 8159240 | tf_op jit(solution)/shard_map/ppermute | solution.py:16
  15.3 89.7 %collective-permute-start.10 = (f32[2656,256]{1,0:T(8,128)}, f32[2656,256]{1,0:T(8,128)}, u32[]{:S(2)}, u32[]{:S(2)}) collective-permute-start(f32[2656,256]{1,0:T(8,128)} %get-tuple-element.51), channel_id=1, source_target_pairs={{0,64},{16,80},{32,96},{48,112},{64,0},{80,16},{96,32},{112,48},{1... | collective-permute-start | bytes 8159240 | tf_op jit(solution)/shard_map/ppermute | solution.py:16
  17.2 66.9 %collective-permute-start.2 = (f32[320,256]{1,0:T(8,128)}, f32[320,256]{1,0:T(8,128)S(1)}, u32[]{:S(2)}, u32[]{:S(2)}) collective-permute-start(f32[320,256]{1,0:T(8,128)} %get-tuple-element.53), channel_id=1, source_target_pairs={{0,64},{16,80},{32,96},{48,112},{64,0},{80,16},{96,32},{112,48},{1... | collective-permute-start | bytes 983048 | tf_op jit(solution)/shard_map/ppermute | solution.py:16
  84.0 10.2 %collective-permute-start = (f32[320,256]{1,0:T(8,128)S(1)}, f32[320,256]{1,0:T(8,128)S(1)}, u32[]{:S(2)}, u32[]{:S(2)}) collective-permute-start(f32[320,256]{1,0:T(8,128)S(1)} %get-tuple-element.54), channel_id=1, source_target_pairs={{0,8},{1,9},{2,10},{3,11},{4,12},{5,13},{6,14},{7,15},{8,0},{9,1},... | collective-permute-start | bytes 983048 | tf_op jit(solution)/shard_map/ppermute | solution.py:16
  94.3 21.0 %collective-permute-start.12 = (f32[608,256]{1,0:T(8,128)S(1)}, f32[608,256]{1,0:T(8,128)S(1)}, u32[]{:S(2)}, u32[]{:S(2)}) collective-permute-start(f32[608,256]{1,0:T(8,128)S(1)} %get-tuple-element.50), channel_id=1, source_target_pairs={{0,8},{1,9},{2,10},{3,11},{4,12},{5,13},{6,14},{7,15},{8,0},{9,1},... | collective-permute-start | bytes 1867784 | tf_op jit(solution)/shard_map/ppermute | solution.py:16
  98.3 18.5 %collective-permute-start.14 = (f32[608,256]{1,0:T(8,128)S(1)}, f32[608,256]{1,0:T(8,128)S(1)}, u32[]{:S(2)}, u32[]{:S(2)}) collective-permute-start(f32[608,256]{1,0:T(8,128)S(1)} %get-tuple-element.49), channel_id=1, source_target_pairs={{0,64},{16,80},{32,96},{48,112},{64,0},{80,16},{96,32},{112,48},{1... | collective-permute-start | bytes 1867784 | tf_op jit(solution)/shard_map/ppermute | solution.py:16
  105.0 94.9 %collective-permute-start.9 = (f32[2656,256]{1,0:T(8,128)S(1)}, f32[2656,256]{1,0:T(8,128)S(1)}, u32[]{:S(2)}, u32[]{:S(2)}) collective-permute-start(f32[2656,256]{1,0:T(8,128)S(1)} %subtract_select_fusion.1), channel_id=1, source_target_pairs={{0,64},{16,80},{32,96},{48,112},{64,0},{80,16},{96,32},{112,48},{1... | collective-permute-start | bytes 8159240 | tf_op jit(solution)/shard_map/ppermute | solution.py:16
  108.0 110.3 %collective-permute-start.1 = (f32[320,256]{1,0:T(8,128)S(1)}, f32[320,256]{1,0:T(8,128)S(1)}, u32[]{:S(2)}, u32[]{:S(2)}) collective-permute-start(f32[320,256]{1,0:T(8,128)S(1)} %subtract_select_fusion.7), channel_id=1, source_target_pairs={{0,64},{16,80},{32,96},{48,112},{64,0},{80,16},{96,32},{112,48},{1... | collective-permute-start | bytes 983048 | tf_op jit(solution)/shard_map/ppermute | solution.py:16
  111.6 91.9 %collective-permute-start.11 = (f32[2656,256]{1,0:T(8,128)S(1)}, f32[2656,256]{1,0:T(8,128)S(1)}, u32[]{:S(2)}, u32[]{:S(2)}) collective-permute-start(f32[2656,256]{1,0:T(8,128)S(1)} %subtract_select_fusion), channel_id=1, source_target_pairs={{8,0},{9,1},{10,2},{11,3},{12,4},{13,5},{14,6},{15,7},{24,16},{25,... | collective-permute-start | bytes 8159240 | tf_op jit(solution)/shard_map/ppermute | solution.py:40
  115.3 76.5 %collective-permute-start.6 = (f32[512,256]{1,0:T(8,128)S(1)}, f32[512,256]{1,0:T(8,128)S(1)}, u32[]{:S(2)}, u32[]{:S(2)}) collective-permute-start(f32[512,256]{1,0:T(8,128)S(1)} %subtract_select_fusion.5), channel_id=1, source_target_pairs={{0,64},{16,80},{32,96},{48,112},{64,0},{80,16},{96,32},{112,48},{1... | collective-permute-start | bytes 1572872 | tf_op jit(solution)/shard_map/ppermute | solution.py:16
  116.9 77.1 %collective-permute-start.7 = (f32[512,256]{1,0:T(8,128)S(1)}, f32[512,256]{1,0:T(8,128)S(1)}, u32[]{:S(2)}, u32[]{:S(2)}) collective-permute-start(f32[512,256]{1,0:T(8,128)S(1)} %subtract_select_fusion.4), channel_id=1, source_target_pairs={{8,0},{9,1},{10,2},{11,3},{12,4},{13,5},{14,6},{15,7},{24,16},{25,... | collective-permute-start | bytes 1572872 | tf_op jit(solution)/shard_map/ppermute | solution.py:40
  191.8 26.6 %collective-permute-start.3 = (f32[320,256]{1,0:T(8,128)S(1)}, f32[320,256]{1,0:T(8,128)S(1)}, u32[]{:S(2)}, u32[]{:S(2)}) collective-permute-start(f32[320,256]{1,0:T(8,128)S(1)} %subtract_select_fusion.6), channel_id=1, source_target_pairs={{8,0},{9,1},{10,2},{11,3},{12,4},{13,5},{14,6},{15,7},{24,16},{25,... | collective-permute-start | bytes 983048 | tf_op jit(solution)/shard_map/ppermute | solution.py:40
  194.0 17.4 %collective-permute-start.13 = (f32[608,256]{1,0:T(8,128)S(1)}, f32[608,256]{1,0:T(8,128)S(1)}, u32[]{:S(2)}, u32[]{:S(2)}) collective-permute-start(f32[608,256]{1,0:T(8,128)S(1)} %subtract_select_fusion.3), channel_id=1, source_target_pairs={{0,64},{16,80},{32,96},{48,112},{64,0},{80,16},{96,32},{112,48},{1... | collective-permute-start | bytes 1867784 | tf_op jit(solution)/shard_map/ppermute | solution.py:16
  199.9 17.4 %collective-permute-start.15 = (f32[608,256]{1,0:T(8,128)S(1)}, f32[608,256]{1,0:T(8,128)S(1)}, u32[]{:S(2)}, u32[]{:S(2)}) collective-permute-start(f32[608,256]{1,0:T(8,128)S(1)} %subtract_select_fusion.2), channel_id=1, source_target_pairs={{8,0},{9,1},{10,2},{11,3},{12,4},{13,5},{14,6},{15,7},{24,16},{25,... | collective-permute-start | bytes 1867784 | tf_op jit(solution)/shard_map/ppermute | solution.py:40

commit v8 on v7

--- a/solution.py
+++ b/solution.py
@@ -24,19 +24,6 @@
             along_rows = c % 2 == first
             partner = (r ^ rows // 2, c) if along_rows else (r, c ^ cols // 2)
             pairs.append((r * cols + c, partner[0] * cols + partner[1]))
-    return lax.ppermute(block, ("row", "col"), pairs)
-
-
-def from_needed_partner(block, axis):
-    if axis == "row":
-        return from_partner(block, axis)
-    rows, cols = lax.axis_size("row"), lax.axis_size("col")
-    pairs = [
-        (r * cols + c, r * cols + (c ^ cols // 2))
-        for r in range(rows)
-        for c in range(cols)
-        if r >= rows // 2 or c >= cols // 2
-    ]
     return lax.ppermute(block, ("row", "col"), pairs)
 
 
@@ -187,7 +174,7 @@
     mixes, acrosses = [], []
     for j, (start, size, first, second) in enumerate(parts):
         mixes.append(mix_rows(slab_pair, theirs[j], start, first))
-        acrosses.append(from_needed_partner(mixes[j], second))
+        acrosses.append(from_partner(mixes[j], second))
 
     out = unwritten(slab_pair.shape, slab_pair.dtype)
     last = []

time: 220 us -> 217 us (0.986)
  waiting for transfers between devices: 133 us -> 130 us
    ppermute x4 -> x0, starting transfers between devices: 5.12 us -> none  [from_needed_partner(): return lax.ppermute(block, ('row', 'col'), pairs)]
    ppermute x10 -> x14, starting transfers between devices: 23.5 us -> 28.5 us  [from_partner(): lax.ppermute(block, axis, [(i, i ^ count // 2) for i in range(count)])]
    ppermute x4 -> x0, waiting for transfers between devices: 4.8 us -> none  [from_needed_partner(): return lax.ppermute(block, ('row', 'col'), pairs)]
    ppermute x10 -> x14, waiting for transfers between devices: 128 us -> 130 us  [from_partner(): lax.ppermute(block, axis, [(i, i ^ count // 2) for i in range(count)])]
where the time goes in v8:
time: 217 us
  waiting for transfers between devices  130 us (60%)
  starting transfers between devices  35.7 us (16%)
  other arithmetic  21.5 us (10%)
  blocking collectives  16.9 us (8%)
  local copies, waits for them, and re-layouts  8.76 us (4%)
  Pallas kernels  3.14 us (1%)
    ppermute x14, waiting for transfers between devices, from_partner(): lax.ppermute(block, axis, [(i, i ^ count // 2) for i in range(count)])  130 us
    ppermute x14, starting transfers between devices, from_partner(): lax.ppermute(block, axis, [(i, i ^ count // 2) for i in range(count)])  28.5 us
    all_gather x1, blocking collectives, per_device(): pieces = lax.all_gather(piece, 'row', axis=0)  16.9 us
    select_n x8, other arithmetic, mix_rows(): return jnp.where(in_first_half(axis), partner + block, partner - block)  12.5 us
    dynamic_update_slice x6, other arithmetic, finish_rows(): return lax.dynamic_update_slice(out, kept, (start, 0))  8.72 us
    slice x3, local copies, waits for them, and re-layouts, copy_rows(): return lax.slice_in_dim(x, start, start + size)  8.52 us
    ppermute x2, starting transfers between devices, from_partner_by_core(): return lax.ppermute(block, ('row', 'col'), pairs)  7.17 us
  transfers between devices with their start and end apart: 16, of which 6 were waited for; matrix products, arithmetic and copies ran while one was open for 14% of the time, Pallas kernels for 1%

profile of v8, /device:TPU:0, one launch (start us, length us, event | category | flops | bytes accessed | tf_op | source)
XLA Modules:
  0.0 216.6 jit_solution(11357449266995958667)
XLA Ops:
  1.1 4.1 %collective-permute-start.4 = (f32[512,256]{1,0:T(8,128)S(1)}, f32[512,256]{1,0:T(8,128)S(1)}, u32[]{:S(2)}, u32[]{:S(2)}) collective-permute-start(f32[512,256]{1,0:T(8,128)S(1)} %shard_map.29), channel_id=1, source_target_pairs={{0,64},{1,9},{2,66},{3,11},{4,68},{5,13},{6,70},{7,15},{8,72},{9,1... | collective-permute-start | bytes 1572872 | tf_op jit(solution)/shard_map/ppermute | solution.py:27
  6.3 3.1 %collective-permute-start.5 = (f32[512,256]{1,0:T(8,128)S(1)}, f32[512,256]{1,0:T(8,128)S(1)}, u32[]{:S(2)}, u32[]{:S(2)}) collective-permute-start(f32[512,256]{1,0:T(8,128)S(1)} %shard_map.30), channel_id=1, source_target_pairs={{0,8},{1,65},{2,10},{3,67},{4,12},{5,69},{6,14},{7,71},{8,0},{9,73... | collective-permute-start | bytes 1572872 | tf_op jit(solution)/shard_map/ppermute | solution.py:27
  9.5 5.3 %fusion.10 = (f32[2656,256]{1,0:T(8,128)}, f32[2656,256]{1,0:T(8,128)}) fusion(f32[8192,256]{1,0:T(8,128)} %x_ref.3), kind=kLoop, calls=%fused_computation.35 | loop fusion | bytes 10878976 | tf_op jit(solution)/shard_map/slice | solution.py:40
  15.3 1.8 fusion.11
  17.2 3.5 %collective-permute-start.2 = (f32[320,256]{1,0:T(8,128)}, f32[320,256]{1,0:T(8,128)S(1)}, u32[]{:S(2)}, u32[]{:S(2)}) collective-permute-start(f32[320,256]{1,0:T(8,128)} %get-tuple-element.53), channel_id=1, source_target_pairs={{0,64},{16,80},{32,96},{48,112},{64,0},{80,16},{96,32},{112,48},{1... | collective-permute-start | bytes 983048 | tf_op jit(solution)/shard_map/ppermute | solution.py:16
  20.7 16.9 %all-gather.1 = f32[8,1,256]{2,1,0:T(1,128)S(1)} all-gather(f32[1,1,256]{2,1,0:T(1,128)S(1)} %bitcast.9), channel_id=2, replica_groups=mesh['row'=8,'col'=16] {'row'}, dimensions={0}, use_global_device_ids=true | all-gather | bytes 9216 | tf_op jit(solution)/shard_map/all_gather | solution.py:170
  38.0 1.3 fusion.9
  39.4 44.7 %collective-permute-done.2 = f32[320,256]{1,0:T(8,128)S(1)} collective-permute-done((f32[320,256]{1,0:T(8,128)}, f32[320,256]{1,0:T(8,128)S(1)}, u32[]{:S(2)}, u32[]{:S(2)}) %collective-permute-start.2) | collective-permute-done | bytes 327712 | tf_op jit(solution)/shard_map/ppermute | solution.py:16
  84.0 3.0 %collective-permute-start = (f32[320,256]{1,0:T(8,128)S(1)}, f32[320,256]{1,0:T(8,128)S(1)}, u32[]{:S(2)}, u32[]{:S(2)}) collective-permute-start(f32[320,256]{1,0:T(8,128)S(1)} %get-tuple-element.54), channel_id=1, source_target_pairs={{0,8},{1,9},{2,10},{3,11},{4,12},{5,13},{6,14},{7,15},{8,0},{9,1},... | collective-permute-start | bytes 983048 | tf_op jit(solution)/shard_map/ppermute | solution.py:16
  88.1 6.2 %collective-permute-done = f32[320,256]{1,0:T(8,128)S(1)} collective-permute-done((f32[320,256]{1,0:T(8,128)S(1)}, f32[320,256]{1,0:T(8,128)S(1)}, u32[]{:S(2)}, u32[]{:S(2)}) %collective-permute-start) | collective-permute-done | bytes 327712 | tf_op jit(solution)/shard_map/ppermute | solution.py:16
  94.3 3.0 %collective-permute-start.12 = (f32[608,256]{1,0:T(8,128)S(1)}, f32[608,256]{1,0:T(8,128)S(1)}, u32[]{:S(2)}, u32[]{:S(2)}) collective-permute-start(f32[608,256]{1,0:T(8,128)S(1)} %get-tuple-element.50), channel_id=1, source_target_pairs={{0,8},{1,9},{2,10},{3,11},{4,12},{5,13},{6,14},{7,15},{8,0},{9,1},... | collective-permute-start | bytes 1867784 | tf_op jit(solution)/shard_map/ppermute | solution.py:16
  98.3 3.7 %collective-permute-start.14 = (f32[608,256]{1,0:T(8,128)S(1)}, f32[608,256]{1,0:T(8,128)S(1)}, u32[]{:S(2)}, u32[]{:S(2)}) collective-permute-start(f32[608,256]{1,0:T(8,128)S(1)} %get-tuple-element.49), channel_id=1, source_target_pairs={{0,64},{16,80},{32,96},{48,112},{64,0},{80,16},{96,32},{112,48},{1... | collective-permute-start | bytes 1867784 | tf_op jit(solution)/shard_map/ppermute | solution.py:16
  102.0 2.9 %subtract_select_fusion.1 = f32[2656,256]{1,0:T(8,128)S(1)} fusion(f32[2656,256]{1,0:T(8,128)} %collective-permute-done.8, f32[8192,256]{1,0:T(8,128)} %x_ref.3, pred[]{:T(512)S(6)} %lt.19), kind=kLoop, calls=%fused_computation.3 | loop fusion | flops 2039808 | bytes 8159233 | tf_op jit(solution)/shard_map/jit(_where)/select_n | solution.py:74
  105.1 2.9 %subtract_select_fusion = f32[2656,256]{1,0:T(8,128)S(1)} fusion(f32[2656,256]{1,0:T(8,128)} %collective-permute-done.10, f32[8192,256]{1,0:T(8,128)} %x_ref.3, pred[]{:T(512)S(6)} %lt.18), kind=kLoop, calls=%fused_computation.1 | loop fusion | flops 2039808 | bytes 8159233 | tf_op jit(solution)/shard_map/jit(_where)/select_n | solution.py:74
  108.0 3.6 %collective-permute-start.1 = (f32[320,256]{1,0:T(8,128)S(1)}, f32[320,256]{1,0:T(8,128)S(1)}, u32[]{:S(2)}, u32[]{:S(2)}) collective-permute-start(f32[320,256]{1,0:T(8,128)S(1)} %subtract_select_fusion.7), channel_id=1, source_target_pairs={{0,64},{16,80},{32,96},{48,112},{64,0},{80,16},{96,32},{112,48},{1... | collective-permute-start | bytes 983048 | tf_op jit(solution)/shard_map/ppermute | solution.py:16
  114.5 1.4 collective-permute-start.6
  116.9 2.4 %collective-permute-start.7 = (f32[512,256]{1,0:T(8,128)S(1)}, f32[512,256]{1,0:T(8,128)S(1)}, u32[]{:S(2)}, u32[]{:S(2)}) collective-permute-start(f32[512,256]{1,0:T(8,128)S(1)} %subtract_select_fusion.4), channel_id=1, source_target_pairs={{0,8},{1,9},{2,10},{3,11},{4,12},{5,13},{6,14},{7,15},{8,0},{9,1},... | collective-permute-start | bytes 1572872 | tf_op jit(solution)/shard_map/ppermute | solution.py:16
  121.6 70.2 %collective-permute-done.6 = f32[512,256]{1,0:T(8,128)S(1)} collective-permute-done((f32[512,256]{1,0:T(8,128)S(1)}, f32[512,256]{1,0:T(8,128)S(1)}, u32[]{:S(2)}, u32[]{:S(2)}) %collective-permute-start.6) | collective-permute-done | bytes 524320 | tf_op jit(solution)/shard_map/ppermute | solution.py:16
  193.7 3.2 %collective-permute-start.13 = (f32[608,256]{1,0:T(8,128)S(1)}, f32[608,256]{1,0:T(8,128)S(1)}, u32[]{:S(2)}, u32[]{:S(2)}) collective-permute-start(f32[608,256]{1,0:T(8,128)S(1)} %subtract_select_fusion.3), channel_id=1, source_target_pairs={{0,64},{16,80},{32,96},{48,112},{64,0},{80,16},{96,32},{112,48},{1... | collective-permute-start | bytes 1867784 | tf_op jit(solution)/shard_map/ppermute | solution.py:16
  198.0 2.5 %collective-permute-start.15 = (f32[608,256]{1,0:T(8,128)S(1)}, f32[608,256]{1,0:T(8,128)S(1)}, u32[]{:S(2)}, u32[]{:S(2)}) collective-permute-start(f32[608,256]{1,0:T(8,128)S(1)} %subtract_select_fusion.2), channel_id=1, source_target_pairs={{0,8},{1,9},{2,10},{3,11},{4,12},{5,13},{6,14},{7,15},{8,0},{9,1},... | collective-permute-start | bytes 1867784 | tf_op jit(solution)/shard_map/ppermute | solution.py:16
  200.5 2.3 %select_dynamic-update-slice_fusion.1 = f32[8192,256]{1,0:T(8,128)} fusion(f32[8192,256]{1,0:T(8,128)} %select_dynamic-update-slice_fusion.4, f32[2656,256]{1,0:T(8,128)S(1)} %collective-permute-done.9, f32[2656,256]{1,0:T(8,128)S(1)} %subtract_select_fusion.1, f32[256]{0:T(256)S(1)} %bitcast.5, f32[2656]{0:T(1024)S(1)} %get-tuple-element.60, s32[]{:T(128)S(6)} %sub.121, ...), kind=kLoop, calls=%fused_computation.2 | loop fusion | flops 5439488 | bytes 8170885 | tf_op jit(solution)/shard_map/dynamic_update_slice | solution.py:144
  202.8 2.4 %select_dynamic-update-slice_fusion = f32[8192,256]{1,0:T(8,128)} fusion(f32[8192,256]{1,0:T(8,128)} %select_dynamic-update-slice_fusion.1, f32[2656,256]{1,0:T(8,128)S(1)} %collective-permute-done.11, f32[2656,256]{1,0:T(8,128)S(1)} %subtract_select_fusion, f32[2656]{0:T(1024)S(1)} %get-tuple-element.59, s32[]{:T(128)S(6)} %sub.124, f32[256]{0:T(256)S(1)} %bitcast.6, ...), kind=kLoop, calls=%fused_computation | loop fusion | flops 5439488 | bytes 8170885 | tf_op jit(solution)/shard_map/dynamic_update_slice | solution.py:144
  205.2 4.6 %collective-permute-done.13 = f32[608,256]{1,0:T(8,128)S(1)} collective-permute-done((f32[608,256]{1,0:T(8,128)S(1)}, f32[608,256]{1,0:T(8,128)S(1)}, u32[]{:S(2)}, u32[]{:S(2)}) %collective-permute-start.13) | collective-permute-done | bytes 622624 | tf_op jit(solution)/shard_map/ppermute | solution.py:16
  210.9 3.8 %collective-permute-done.15 = f32[608,256]{1,0:T(8,128)S(1)} collective-permute-done((f32[608,256]{1,0:T(8,128)S(1)}, f32[608,256]{1,0:T(8,128)S(1)}, u32[]{:S(2)}, u32[]{:S(2)}) %collective-permute-start.15) | collective-permute-done | bytes 622624 | tf_op jit(solution)/shard_map/ppermute | solution.py:16
  (42 shorter events, 17.5 us)
Async XLA Ops:
  1.1 106.9 %collective-permute-start.4 = (f32[512,256]{1,0:T(8,128)S(1)}, f32[512,256]{1,0:T(8,128)S(1)}, u32[]{:S(2)}, u32[]{:S(2)}) collective-permute-start(f32[512,256]{1,0:T(8,128)S(1)} %shard_map.29), channel_id=1, source_target_pairs={{0,64},{1,9},{2,66},{3,11},{4,68},{5,13},{6,70},{7,15},{8,72},{9,1... | collective-permute-start | bytes 1572872 | tf_op jit(solution)/shard_map/ppermute | solution.py:27
  6.3 14.3 %copy-start = (f32[8192]{0:T(1024)S(1)}, f32[8192]{0:T(1024)}, u32[]{:S(2)}) copy-start(f32[8192]{0:T(1024)} %param.3) | copy-start | bytes 98308
  6.3 105.3 %collective-permute-start.5 = (f32[512,256]{1,0:T(8,128)S(1)}, f32[512,256]{1,0:T(8,128)S(1)}, u32[]{:S(2)}, u32[]{:S(2)}) collective-permute-start(f32[512,256]{1,0:T(8,128)S(1)} %shard_map.30), channel_id=1, source_target_pairs={{0,8},{1,65},{2,10},{3,67},{4,12},{5,69},{6,14},{7,71},{8,0},{9,73... | collective-permute-start | bytes 1572872 | tf_op jit(solution)/shard_map/ppermute | solution.py:27
  14.8 83.6 %collective-permute-start.8 = (f32[2656,256]{1,0:T(8,128)}, f32[2656,256]{1,0:T(8,128)}, u32[]{:S(2)}, u32[]{:S(2)}) collective-permute-start(f32[2656,256]{1,0:T(8,128)} %get-tuple-element.52), channel_id=1, source_target_pairs={{0,8},{1,9},{2,10},{3,11},{4,12},{5,13},{6,14},{7,15},{8,0},{9,1},... | collective-permute-start | bytes 8159240 | tf_op jit(solution)/shard_map/ppermute | solution.py:16
  15.3 89.7 %collective-permute-start.10 = (f32[2656,256]{1,0:T(8,128)}, f32[2656,256]{1,0:T(8,128)}, u32[]{:S(2)}, u32[]{:S(2)}) collective-permute-start(f32[2656,256]{1,0:T(8,128)} %get-tuple-element.51), channel_id=1, source_target_pairs={{0,64},{16,80},{32,96},{48,112},{64,0},{80,16},{96,32},{112,48},{1... | collective-permute-start | bytes 8159240 | tf_op jit(solution)/shard_map/ppermute | solution.py:16
  17.2 66.9 %collective-permute-start.2 = (f32[320,256]{1,0:T(8,128)}, f32[320,256]{1,0:T(8,128)S(1)}, u32[]{:S(2)}, u32[]{:S(2)}) collective-permute-start(f32[320,256]{1,0:T(8,128)} %get-tuple-element.53), channel_id=1, source_target_pairs={{0,64},{16,80},{32,96},{48,112},{64,0},{80,16},{96,32},{112,48},{1... | collective-permute-start | bytes 983048 | tf_op jit(solution)/shard_map/ppermute | solution.py:16
  84.0 10.2 %collective-permute-start = (f32[320,256]{1,0:T(8,128)S(1)}, f32[320,256]{1,0:T(8,128)S(1)}, u32[]{:S(2)}, u32[]{:S(2)}) collective-permute-start(f32[320,256]{1,0:T(8,128)S(1)} %get-tuple-element.54), channel_id=1, source_target_pairs={{0,8},{1,9},{2,10},{3,11},{4,12},{5,13},{6,14},{7,15},{8,0},{9,1},... | collective-permute-start | bytes 983048 | tf_op jit(solution)/shard_map/ppermute | solution.py:16
  94.3 20.2 %collective-permute-start.12 = (f32[608,256]{1,0:T(8,128)S(1)}, f32[608,256]{1,0:T(8,128)S(1)}, u32[]{:S(2)}, u32[]{:S(2)}) collective-permute-start(f32[608,256]{1,0:T(8,128)S(1)} %get-tuple-element.50), channel_id=1, source_target_pairs={{0,8},{1,9},{2,10},{3,11},{4,12},{5,13},{6,14},{7,15},{8,0},{9,1},... | collective-permute-start | bytes 1867784 | tf_op jit(solution)/shard_map/ppermute | solution.py:16
  98.3 18.5 %collective-permute-start.14 = (f32[608,256]{1,0:T(8,128)S(1)}, f32[608,256]{1,0:T(8,128)S(1)}, u32[]{:S(2)}, u32[]{:S(2)}) collective-permute-start(f32[608,256]{1,0:T(8,128)S(1)} %get-tuple-element.49), channel_id=1, source_target_pairs={{0,64},{16,80},{32,96},{48,112},{64,0},{80,16},{96,32},{112,48},{1... | collective-permute-start | bytes 1867784 | tf_op jit(solution)/shard_map/ppermute | solution.py:16
  105.0 93.0 %collective-permute-start.9 = (f32[2656,256]{1,0:T(8,128)S(1)}, f32[2656,256]{1,0:T(8,128)S(1)}, u32[]{:S(2)}, u32[]{:S(2)}) collective-permute-start(f32[2656,256]{1,0:T(8,128)S(1)} %subtract_select_fusion.1), channel_id=1, source_target_pairs={{0,64},{16,80},{32,96},{48,112},{64,0},{80,16},{96,32},{112,48},{1... | collective-permute-start | bytes 8159240 | tf_op jit(solution)/shard_map/ppermute | solution.py:16
  108.0 107.6 %collective-permute-start.1 = (f32[320,256]{1,0:T(8,128)S(1)}, f32[320,256]{1,0:T(8,128)S(1)}, u32[]{:S(2)}, u32[]{:S(2)}) collective-permute-start(f32[320,256]{1,0:T(8,128)S(1)} %subtract_select_fusion.7), channel_id=1, source_target_pairs={{0,64},{16,80},{32,96},{48,112},{64,0},{80,16},{96,32},{112,48},{1... | collective-permute-start | bytes 983048 | tf_op jit(solution)/shard_map/ppermute | solution.py:16
  111.6 91.2 %collective-permute-start.11 = (f32[2656,256]{1,0:T(8,128)S(1)}, f32[2656,256]{1,0:T(8,128)S(1)}, u32[]{:S(2)}, u32[]{:S(2)}) collective-permute-start(f32[2656,256]{1,0:T(8,128)S(1)} %subtract_select_fusion), channel_id=1, source_target_pairs={{0,8},{1,9},{2,10},{3,11},{4,12},{5,13},{6,14},{7,15},{8,0},{9,1},... | collective-permute-start | bytes 8159240 | tf_op jit(solution)/shard_map/ppermute | solution.py:16
  114.5 77.3 %collective-permute-start.6 = (f32[512,256]{1,0:T(8,128)S(1)}, f32[512,256]{1,0:T(8,128)S(1)}, u32[]{:S(2)}, u32[]{:S(2)}) collective-permute-start(f32[512,256]{1,0:T(8,128)S(1)} %subtract_select_fusion.5), channel_id=1, source_target_pairs={{0,64},{16,80},{32,96},{48,112},{64,0},{80,16},{96,32},{112,48},{1... | collective-permute-start | bytes 1572872 | tf_op jit(solution)/shard_map/ppermute | solution.py:16
  116.9 76.8 %collective-permute-start.7 = (f32[512,256]{1,0:T(8,128)S(1)}, f32[512,256]{1,0:T(8,128)S(1)}, u32[]{:S(2)}, u32[]{:S(2)}) collective-permute-start(f32[512,256]{1,0:T(8,128)S(1)} %subtract_select_fusion.4), channel_id=1, source_target_pairs={{0,8},{1,9},{2,10},{3,11},{4,12},{5,13},{6,14},{7,15},{8,0},{9,1},... | collective-permute-start | bytes 1572872 | tf_op jit(solution)/shard_map/ppermute | solution.py:16
  191.8 23.9 %collective-permute-start.3 = (f32[320,256]{1,0:T(8,128)S(1)}, f32[320,256]{1,0:T(8,128)S(1)}, u32[]{:S(2)}, u32[]{:S(2)}) collective-permute-start(f32[320,256]{1,0:T(8,128)S(1)} %subtract_select_fusion.6), channel_id=1, source_target_pairs={{0,8},{1,9},{2,10},{3,11},{4,12},{5,13},{6,14},{7,15},{8,0},{9,1},... | collective-permute-start | bytes 983048 | tf_op jit(solution)/shard_map/ppermute | solution.py:16
  193.7 16.1 %collective-permute-start.13 = (f32[608,256]{1,0:T(8,128)S(1)}, f32[608,256]{1,0:T(8,128)S(1)}, u32[]{:S(2)}, u32[]{:S(2)}) collective-permute-start(f32[608,256]{1,0:T(8,128)S(1)} %subtract_select_fusion.3), channel_id=1, source_target_pairs={{0,64},{16,80},{32,96},{48,112},{64,0},{80,16},{96,32},{112,48},{1... | collective-permute-start | bytes 1867784 | tf_op jit(solution)/shard_map/ppermute | solution.py:16
  198.0 16.7 %collective-permute-start.15 = (f32[608,256]{1,0:T(8,128)S(1)}, f32[608,256]{1,0:T(8,128)S(1)}, u32[]{:S(2)}, u32[]{:S(2)}) collective-permute-start(f32[608,256]{1,0:T(8,128)S(1)} %subtract_select_fusion.2), channel_id=1, source_target_pairs={{0,8},{1,9},{2,10},{3,11},{4,12},{5,13},{6,14},{7,15},{8,0},{9,1},... | collective-permute-start | bytes 1867784 | tf_op jit(solution)/shard_map/ppermute | solution.py:16

commit v9 on v8

--- a/solution.py
+++ b/solution.py
@@ -8,7 +8,8 @@
 
 N = 65536
 W = 2048
-SIZES = (512, 2656, 608, 320)
+SIZES = (512, 2848, 480, 256)
+PIECES = 4
 
 
 def from_partner(block, axis):
@@ -99,18 +100,18 @@
 
 def finish_last(out, chunks):
     size, cols = chunks[0][0].shape
-    half = size // 2
+    piece = size // PIECES
 
     def kernel(*refs):
         out_ref, done_ref, sems = refs[-3:]
         copies = []
         for k, (_, _, _, start) in enumerate(chunks):
             mixed_ref, across_ref, factor_ref = refs[3 * k : 3 * k + 3]
-            for p in range(2):
-                rows = pl.ds(p * half, half)
+            for p in range(PIECES):
+                rows = pl.ds(p * piece, piece)
                 done_ref[k, rows, :] = (across_ref[rows, :] + mixed_ref[rows, :]) * factor_ref[rows, :]
                 copy = pltpu.make_async_copy(
-                    done_ref.at[k, rows, :], out_ref.at[pl.ds(start + p * half, half), :], sems.at[k, p]
+                    done_ref.at[k, rows, :], out_ref.at[pl.ds(start + p * piece, piece), :], sems.at[k, p]
                 )
                 copy.start()
                 copies.append(copy)
@@ -127,7 +128,7 @@
         out_shape=jax.ShapeDtypeStruct(out.shape, out.dtype),
         scratch_shapes=[
             pltpu.VMEM((len(chunks), size, cols), jnp.float32),
-            pltpu.SemaphoreType.DMA((len(chunks), 2)),
+            pltpu.SemaphoreType.DMA((len(chunks), PIECES)),
         ],
         input_output_aliases={len(held): 0},
     )(*held, out)

time: 217 us -> 222 us (1.023)
  waiting for transfers between devices: 130 us -> 141 us
  starting transfers between devices: 35.7 us -> 30.2 us
    ppermute x14, waiting for transfers between devices: 130 us -> 141 us  [from_partner(): lax.ppermute(block, axis, [(i, i ^ count // 2) for i in range(count)])]
    ppermute x14, starting transfers between devices: 28.5 us -> 25.6 us  [from_partner(): lax.ppermute(block, axis, [(i, i ^ count // 2) for i in range(count)])]
    ppermute x2, starting transfers between devices: 7.17 us -> 4.54 us  [from_partner_by_core(): return lax.ppermute(block, ('row', 'col'), pairs)]
  transfers between devices with their start and end apart: 16 -> 16, of which waited for: 6 -> 7; matrix products, arithmetic and copies ran while one was open for 14% -> 11% of each run, Pallas kernels for 1% -> 1%
where the time goes in v9:
time: 222 us
  waiting for transfers between devices  141 us (64%)
  starting transfers between devices  30.2 us (14%)
  other arithmetic  21.6 us (10%)
  blocking collectives  16.9 us (8%)
  local copies, waits for them, and re-layouts  8.88 us (4%)
  Pallas kernels  3.11 us (1%)
    ppermute x14, waiting for transfers between devices, from_partner(): lax.ppermute(block, axis, [(i, i ^ count // 2) for i in range(count)])  141 us
    ppermute x14, starting transfers between devices, from_partner(): lax.ppermute(block, axis, [(i, i ^ count // 2) for i in range(count)])  25.6 us
    all_gather x1, blocking collectives, per_device(): pieces = lax.all_gather(piece, 'row', axis=0)  16.9 us
    select_n x8, other arithmetic, mix_rows(): return jnp.where(in_first_half(axis), partner + block, partner - block)  12.6 us
    dynamic_update_slice x6, other arithmetic, finish_rows(): return lax.dynamic_update_slice(out, kept, (start, 0))  8.75 us
    slice x3, local copies, waits for them, and re-layouts, copy_rows(): return lax.slice_in_dim(x, start, start + size)  8.71 us
    ppermute x2, starting transfers between devices, from_partner_by_core(): return lax.ppermute(block, ('row', 'col'), pairs)  4.54 us
  transfers between devices with their start and end apart: 16, of which 7 were waited for; matrix products, arithmetic and copies ran while one was open for 11% of the time, Pallas kernels for 1%

profile of v9, /device:TPU:0, one launch (start us, length us, event | category | flops | bytes accessed | tf_op | source)
XLA Modules:
  0.0 221.9 jit_solution(2814278112461977507)
XLA Ops:
  0.0 5.6 %fusion.10 = (f32[2848,256]{1,0:T(8,128)}, f32[2848,256]{1,0:T(8,128)}) fusion(f32[8192,256]{1,0:T(8,128)} %x_ref.3), kind=kLoop, calls=%fused_computation.35 | loop fusion | bytes 11665408 | tf_op jit(solution)/shard_map/slice | solution.py:41
  5.6 3.1 %collective-permute-start.8 = (f32[2848,256]{1,0:T(8,128)}, f32[2848,256]{1,0:T(8,128)}, u32[]{:S(2)}, u32[]{:S(2)}) collective-permute-start(f32[2848,256]{1,0:T(8,128)} %get-tuple-element.52), channel_id=1, source_target_pairs={{0,8},{1,9},{2,10},{3,11},{4,12},{5,13},{6,14},{7,15},{8,0},{9,1},... | collective-permute-start | bytes 8749064 | tf_op jit(solution)/shard_map/ppermute | solution.py:17
  8.7 1.1 shard_map.29
  9.9 4.0 %collective-permute-start.4 = (f32[512,256]{1,0:T(8,128)S(1)}, f32[512,256]{1,0:T(8,128)S(1)}, u32[]{:S(2)}, u32[]{:S(2)}) collective-permute-start(f32[512,256]{1,0:T(8,128)S(1)} %shard_map.29), channel_id=1, source_target_pairs={{0,64},{1,9},{2,66},{3,11},{4,68},{5,13},{6,70},{7,15},{8,72},{9,1... | collective-permute-start | bytes 1572872 | tf_op jit(solution)/shard_map/ppermute | solution.py:28
  15.6 1.9 fusion.11
  17.5 3.5 %collective-permute-start.2 = (f32[256,256]{1,0:T(8,128)}, f32[256,256]{1,0:T(8,128)S(1)}, u32[]{:S(2)}, u32[]{:S(2)}) collective-permute-start(f32[256,256]{1,0:T(8,128)} %get-tuple-element.53), channel_id=1, source_target_pairs={{0,64},{16,80},{32,96},{48,112},{64,0},{80,16},{96,32},{112,48},{1... | collective-permute-start | bytes 786440 | tf_op jit(solution)/shard_map/ppermute | solution.py:17
  21.0 16.9 %all-gather.1 = f32[8,1,256]{2,1,0:T(1,128)S(1)} all-gather(f32[1,1,256]{2,1,0:T(1,128)S(1)} %bitcast.9), channel_id=2, replica_groups=mesh['row'=8,'col'=16] {'row'}, dimensions={0}, use_global_device_ids=true | all-gather | bytes 9216 | tf_op jit(solution)/shard_map/all_gather | solution.py:171
  38.2 1.2 fusion.9
  39.5 55.1 %collective-permute-done.2 = f32[256,256]{1,0:T(8,128)S(1)} collective-permute-done((f32[256,256]{1,0:T(8,128)}, f32[256,256]{1,0:T(8,128)S(1)}, u32[]{:S(2)}, u32[]{:S(2)}) %collective-permute-start.2) | collective-permute-done | bytes 262176 | tf_op jit(solution)/shard_map/ppermute | solution.py:17
  95.6 9.0 %collective-permute-done = f32[256,256]{1,0:T(8,128)S(1)} collective-permute-done((f32[256,256]{1,0:T(8,128)}, f32[256,256]{1,0:T(8,128)S(1)}, u32[]{:S(2)}, u32[]{:S(2)}) %collective-permute-start) | collective-permute-done | bytes 262176 | tf_op jit(solution)/shard_map/ppermute | solution.py:17
  106.1 3.6 %collective-permute-start.14 = (f32[480,256]{1,0:T(8,128)S(1)}, f32[480,256]{1,0:T(8,128)S(1)}, u32[]{:S(2)}, u32[]{:S(2)}) collective-permute-start(f32[480,256]{1,0:T(8,128)S(1)} %get-tuple-element.49), channel_id=1, source_target_pairs={{0,64},{16,80},{32,96},{48,112},{64,0},{80,16},{96,32},{112,48},{1... | collective-permute-start | bytes 1474568 | tf_op jit(solution)/shard_map/ppermute | solution.py:17
  109.7 3.1 %subtract_select_fusion.1 = f32[2848,256]{1,0:T(8,128)S(1)} fusion(f32[2848,256]{1,0:T(8,128)} %collective-permute-done.8, f32[8192,256]{1,0:T(8,128)} %x_ref.3, pred[]{:T(512)S(6)} %lt.19), kind=kLoop, calls=%fused_computation.3 | loop fusion | flops 2187264 | bytes 8749057 | tf_op jit(solution)/shard_map/jit(_where)/select_n | solution.py:75
  112.9 3.1 %subtract_select_fusion = f32[2848,256]{1,0:T(8,128)S(1)} fusion(f32[2848,256]{1,0:T(8,128)} %collective-permute-done.10, f32[8192,256]{1,0:T(8,128)} %x_ref.3, pred[]{:T(512)S(6)} %lt.18), kind=kLoop, calls=%fused_computation.1 | loop fusion | flops 2187264 | bytes 8749057 | tf_op jit(solution)/shard_map/jit(_where)/select_n | solution.py:75
  116.0 2.5 %collective-permute-done.12 = f32[480,256]{1,0:T(8,128)S(1)} collective-permute-done((f32[480,256]{1,0:T(8,128)S(1)}, f32[480,256]{1,0:T(8,128)S(1)}, u32[]{:S(2)}, u32[]{:S(2)}) %collective-permute-start.12) | collective-permute-done | bytes 491552 | tf_op jit(solution)/shard_map/ppermute | solution.py:17
  119.5 2.3 %collective-permute-done.14 = f32[480,256]{1,0:T(8,128)S(1)} collective-permute-done((f32[480,256]{1,0:T(8,128)S(1)}, f32[480,256]{1,0:T(8,128)S(1)}, u32[]{:S(2)}, u32[]{:S(2)}) %collective-permute-start.14) | collective-permute-done | bytes 491552 | tf_op jit(solution)/shard_map/ppermute | solution.py:17
  121.8 3.5 %collective-permute-start.1 = (f32[256,256]{1,0:T(8,128)S(1)}, f32[256,256]{1,0:T(8,128)S(1)}, u32[]{:S(2)}, u32[]{:S(2)}) collective-permute-start(f32[256,256]{1,0:T(8,128)S(1)} %subtract_select_fusion.7), channel_id=1, source_target_pairs={{0,64},{16,80},{32,96},{48,112},{64,0},{80,16},{96,32},{112,48},{1... | collective-permute-start | bytes 786440 | tf_op jit(solution)/shard_map/ppermute | solution.py:17
  128.8 3.3 %collective-permute-start.7 = (f32[512,256]{1,0:T(8,128)S(1)}, f32[512,256]{1,0:T(8,128)S(1)}, u32[]{:S(2)}, u32[]{:S(2)}) collective-permute-start(f32[512,256]{1,0:T(8,128)S(1)} %subtract_select_fusion.2), channel_id=1, source_target_pairs={{0,8},{1,9},{2,10},{3,11},{4,12},{5,13},{6,14},{7,15},{8,0},{9,1},... | collective-permute-start | bytes 1572872 | tf_op jit(solution)/shard_map/ppermute | solution.py:17
  133.3 66.5 %collective-permute-done.6 = f32[512,256]{1,0:T(8,128)S(1)} collective-permute-done((f32[512,256]{1,0:T(8,128)S(1)}, f32[512,256]{1,0:T(8,128)S(1)}, u32[]{:S(2)}, u32[]{:S(2)}) %collective-permute-start.6) | collective-permute-done | bytes 524320 | tf_op jit(solution)/shard_map/ppermute | solution.py:17
  199.7 3.0 %collective-permute-start.3 = (f32[256,256]{1,0:T(8,128)S(1)}, f32[256,256]{1,0:T(8,128)S(1)}, u32[]{:S(2)}, u32[]{:S(2)}) collective-permute-start(f32[256,256]{1,0:T(8,128)S(1)} %subtract_select_fusion.6), channel_id=1, source_target_pairs={{0,8},{1,9},{2,10},{3,11},{4,12},{5,13},{6,14},{7,15},{8,0},{9,1},... | collective-permute-start | bytes 786440 | tf_op jit(solution)/shard_map/ppermute | solution.py:17
  203.6 3.2 %collective-permute-start.13 = (f32[480,256]{1,0:T(8,128)S(1)}, f32[480,256]{1,0:T(8,128)S(1)}, u32[]{:S(2)}, u32[]{:S(2)}) collective-permute-start(f32[480,256]{1,0:T(8,128)S(1)} %subtract_select_fusion.5), channel_id=1, source_target_pairs={{0,64},{16,80},{32,96},{48,112},{64,0},{80,16},{96,32},{112,48},{1... | collective-permute-start | bytes 1474568 | tf_op jit(solution)/shard_map/ppermute | solution.py:17
  208.4 2.4 %select_dynamic-update-slice_fusion.1 = f32[8192,256]{1,0:T(8,128)} fusion(f32[8192,256]{1,0:T(8,128)} %select_dynamic-update-slice_fusion.2, f32[2848,256]{1,0:T(8,128)S(1)} %collective-permute-done.9, f32[2848,256]{1,0:T(8,128)S(1)} %subtract_select_fusion.1, f32[256]{0:T(256)S(1)} %bitcast.5, f32[2848]{0:T(1024)S(1)} %get-tuple-element.60, s32[]{:T(128)S(6)} %sub.121, ...), kind=kLoop, calls=%fused_computation.2 | loop fusion | flops 5832704 | bytes 8761477 | tf_op jit(solution)/shard_map/dynamic_update_slice | solution.py:145
  210.9 2.5 %select_dynamic-update-slice_fusion = f32[8192,256]{1,0:T(8,128)} fusion(f32[8192,256]{1,0:T(8,128)} %select_dynamic-update-slice_fusion.1, f32[2848,256]{1,0:T(8,128)S(1)} %collective-permute-done.11, f32[2848,256]{1,0:T(8,128)S(1)} %subtract_select_fusion, f32[2848]{0:T(1024)S(1)} %get-tuple-element.59, s32[]{:T(128)S(6)} %sub.124, f32[256]{0:T(256)S(1)} %bitcast.6, ...), kind=kLoop, calls=%fused_computation | loop fusion | flops 5832704 | bytes 8761477 | tf_op jit(solution)/shard_map/dynamic_update_slice | solution.py:145
  213.4 3.1 %collective-permute-done.13 = f32[480,256]{1,0:T(8,128)S(1)} collective-permute-done((f32[480,256]{1,0:T(8,128)S(1)}, f32[480,256]{1,0:T(8,128)S(1)}, u32[]{:S(2)}, u32[]{:S(2)}) %collective-permute-start.13) | collective-permute-done | bytes 491552 | tf_op jit(solution)/shard_map/ppermute | solution.py:17
  217.4 2.7 %collective-permute-done.15 = f32[480,256]{1,0:T(8,128)S(1)} collective-permute-done((f32[480,256]{1,0:T(8,128)S(1)}, f32[480,256]{1,0:T(8,128)S(1)}, u32[]{:S(2)}, u32[]{:S(2)}) %collective-permute-start.15) | collective-permute-done | bytes 491552 | tf_op jit(solution)/shard_map/ppermute | solution.py:17
  (42 shorter events, 15.5 us)
Async XLA Ops:
  5.6 100.5 %collective-permute-start.8 = (f32[2848,256]{1,0:T(8,128)}, f32[2848,256]{1,0:T(8,128)}, u32[]{:S(2)}, u32[]{:S(2)}) collective-permute-start(f32[2848,256]{1,0:T(8,128)} %get-tuple-element.52), channel_id=1, source_target_pairs={{0,8},{1,9},{2,10},{3,11},{4,12},{5,13},{6,14},{7,15},{8,0},{9,1},... | collective-permute-start | bytes 8749064 | tf_op jit(solution)/shard_map/ppermute | solution.py:17
  9.9 11.1 %copy-start = (f32[8192]{0:T(1024)S(1)}, f32[8192]{0:T(1024)}, u32[]{:S(2)}) copy-start(f32[8192]{0:T(1024)} %param.3) | copy-start | bytes 98308
  9.9 116.5 %collective-permute-start.4 = (f32[512,256]{1,0:T(8,128)S(1)}, f32[512,256]{1,0:T(8,128)S(1)}, u32[]{:S(2)}, u32[]{:S(2)}) collective-permute-start(f32[512,256]{1,0:T(8,128)S(1)} %shard_map.29), channel_id=1, source_target_pairs={{0,64},{1,9},{2,66},{3,11},{4,68},{5,13},{6,70},{7,15},{8,72},{9,1... | collective-permute-start | bytes 1572872 | tf_op jit(solution)/shard_map/ppermute | solution.py:28
  15.0 111.5 %collective-permute-start.5 = (f32[512,256]{1,0:T(8,128)S(1)}, f32[512,256]{1,0:T(8,128)S(1)}, u32[]{:S(2)}, u32[]{:S(2)}) collective-permute-start(f32[512,256]{1,0:T(8,128)S(1)} %shard_map.30), channel_id=1, source_target_pairs={{0,8},{1,65},{2,10},{3,67},{4,12},{5,69},{6,14},{7,71},{8,0},{9,73... | collective-permute-start | bytes 1572872 | tf_op jit(solution)/shard_map/ppermute | solution.py:28
  15.6 97.3 %collective-permute-start.10 = (f32[2848,256]{1,0:T(8,128)}, f32[2848,256]{1,0:T(8,128)}, u32[]{:S(2)}, u32[]{:S(2)}) collective-permute-start(f32[2848,256]{1,0:T(8,128)} %get-tuple-element.51), channel_id=1, source_target_pairs={{0,64},{16,80},{32,96},{48,112},{64,0},{80,16},{96,32},{112,48},{1... | collective-permute-start | bytes 8749064 | tf_op jit(solution)/shard_map/ppermute | solution.py:17
  17.5 77.1 %collective-permute-start.2 = (f32[256,256]{1,0:T(8,128)}, f32[256,256]{1,0:T(8,128)S(1)}, u32[]{:S(2)}, u32[]{:S(2)}) collective-permute-start(f32[256,256]{1,0:T(8,128)} %get-tuple-element.53), channel_id=1, source_target_pairs={{0,64},{16,80},{32,96},{48,112},{64,0},{80,16},{96,32},{112,48},{1... | collective-permute-start | bytes 786440 | tf_op jit(solution)/shard_map/ppermute | solution.py:17
  94.5 10.1 %collective-permute-start = (f32[256,256]{1,0:T(8,128)}, f32[256,256]{1,0:T(8,128)S(1)}, u32[]{:S(2)}, u32[]{:S(2)}) collective-permute-start(f32[256,256]{1,0:T(8,128)} %get-tuple-element.54), channel_id=1, source_target_pairs={{0,8},{1,9},{2,10},{3,11},{4,12},{5,13},{6,14},{7,15},{8,0},{9,1},... | collective-permute-start | bytes 786440 | tf_op jit(solution)/shard_map/ppermute | solution.py:17
  104.6 13.9 %collective-permute-start.12 = (f32[480,256]{1,0:T(8,128)S(1)}, f32[480,256]{1,0:T(8,128)S(1)}, u32[]{:S(2)}, u32[]{:S(2)}) collective-permute-start(f32[480,256]{1,0:T(8,128)S(1)} %get-tuple-element.50), channel_id=1, source_target_pairs={{0,8},{1,9},{2,10},{3,11},{4,12},{5,13},{6,14},{7,15},{8,0},{9,1},... | collective-permute-start | bytes 1474568 | tf_op jit(solution)/shard_map/ppermute | solution.py:17
  106.1 15.7 %collective-permute-start.14 = (f32[480,256]{1,0:T(8,128)S(1)}, f32[480,256]{1,0:T(8,128)S(1)}, u32[]{:S(2)}, u32[]{:S(2)}) collective-permute-start(f32[480,256]{1,0:T(8,128)S(1)} %get-tuple-element.49), channel_id=1, source_target_pairs={{0,64},{16,80},{32,96},{48,112},{64,0},{80,16},{96,32},{112,48},{1... | collective-permute-start | bytes 1474568 | tf_op jit(solution)/shard_map/ppermute | solution.py:17
  112.8 95.0 %collective-permute-start.9 = (f32[2848,256]{1,0:T(8,128)S(1)}, f32[2848,256]{1,0:T(8,128)S(1)}, u32[]{:S(2)}, u32[]{:S(2)}) collective-permute-start(f32[2848,256]{1,0:T(8,128)S(1)} %subtract_select_fusion.1), channel_id=1, source_target_pairs={{0,64},{16,80},{32,96},{48,112},{64,0},{80,16},{96,32},{112,48},{1... | collective-permute-start | bytes 8749064 | tf_op jit(solution)/shard_map/ppermute | solution.py:17
  118.5 92.4 %collective-permute-start.11 = (f32[2848,256]{1,0:T(8,128)S(1)}, f32[2848,256]{1,0:T(8,128)S(1)}, u32[]{:S(2)}, u32[]{:S(2)}) collective-permute-start(f32[2848,256]{1,0:T(8,128)S(1)} %subtract_select_fusion), channel_id=1, source_target_pairs={{0,8},{1,9},{2,10},{3,11},{4,12},{5,13},{6,14},{7,15},{8,0},{9,1},... | collective-permute-start | bytes 8749064 | tf_op jit(solution)/shard_map/ppermute | solution.py:17
  121.8 99.2 %collective-permute-start.1 = (f32[256,256]{1,0:T(8,128)S(1)}, f32[256,256]{1,0:T(8,128)S(1)}, u32[]{:S(2)}, u32[]{:S(2)}) collective-permute-start(f32[256,256]{1,0:T(8,128)S(1)} %subtract_select_fusion.7), channel_id=1, source_target_pairs={{0,64},{16,80},{32,96},{48,112},{64,0},{80,16},{96,32},{112,48},{1... | collective-permute-start | bytes 786440 | tf_op jit(solution)/shard_map/ppermute | solution.py:17
  127.6 72.1 %collective-permute-start.6 = (f32[512,256]{1,0:T(8,128)S(1)}, f32[512,256]{1,0:T(8,128)S(1)}, u32[]{:S(2)}, u32[]{:S(2)}) collective-permute-start(f32[512,256]{1,0:T(8,128)S(1)} %subtract_select_fusion.3), channel_id=1, source_target_pairs={{0,64},{16,80},{32,96},{48,112},{64,0},{80,16},{96,32},{112,48},{1... | collective-permute-start | bytes 1572872 | tf_op jit(solution)/shard_map/ppermute | solution.py:17
  128.8 74.8 %collective-permute-start.7 = (f32[512,256]{1,0:T(8,128)S(1)}, f32[512,256]{1,0:T(8,128)S(1)}, u32[]{:S(2)}, u32[]{:S(2)}) collective-permute-start(f32[512,256]{1,0:T(8,128)S(1)} %subtract_select_fusion.2), channel_id=1, source_target_pairs={{0,8},{1,9},{2,10},{3,11},{4,12},{5,13},{6,14},{7,15},{8,0},{9,1},... | collective-permute-start | bytes 1572872 | tf_op jit(solution)/shard_map/ppermute | solution.py:17
  199.7 21.3 %collective-permute-start.3 = (f32[256,256]{1,0:T(8,128)S(1)}, f32[256,256]{1,0:T(8,128)S(1)}, u32[]{:S(2)}, u32[]{:S(2)}) collective-permute-start(f32[256,256]{1,0:T(8,128)S(1)} %subtract_select_fusion.6), channel_id=1, source_target_pairs={{0,8},{1,9},{2,10},{3,11},{4,12},{5,13},{6,14},{7,15},{8,0},{9,1},... | collective-permute-start | bytes 786440 | tf_op jit(solution)/shard_map/ppermute | solution.py:17
  203.6 12.8 %collective-permute-start.13 = (f32[480,256]{1,0:T(8,128)S(1)}, f32[480,256]{1,0:T(8,128)S(1)}, u32[]{:S(2)}, u32[]{:S(2)}) collective-permute-start(f32[480,256]{1,0:T(8,128)S(1)} %subtract_select_fusion.5), channel_id=1, source_target_pairs={{0,64},{16,80},{32,96},{48,112},{64,0},{80,16},{96,32},{112,48},{1... | collective-permute-start | bytes 1474568 | tf_op jit(solution)/shard_map/ppermute | solution.py:17
  207.9 12.2 %collective-permute-start.15 = (f32[480,256]{1,0:T(8,128)S(1)}, f32[480,256]{1,0:T(8,128)S(1)}, u32[]{:S(2)}, u32[]{:S(2)}) collective-permute-start(f32[480,256]{1,0:T(8,128)S(1)} %subtract_select_fusion.4), channel_id=1, source_target_pairs={{0,8},{1,9},{2,10},{3,11},{4,12},{5,13},{6,14},{7,15},{8,0},{9,1},... | collective-permute-start | bytes 1474568 | tf_op jit(solution)/shard_map/ppermute | solution.py:17
